TPU v7x, 32 devices: a whole 2x2x4 slice. The times are simulated.
32 devices in a mesh: dp: 8 (over z, y), mp: 4 (over x, core).
Axes of the slice: x: 2, y: 2, z: 4, core: 2. Of those that a mesh axis runs over, the one named last changes fastest.
Arguments:
- prefix_hidden: bfloat16 [32, 1024, 2048], P(('dp', 'mp')), may hold values from -6 to 6
- prefix_len: int32 [32], P('dp'), may hold values from 256 to 1024
- actions: float32 [32, 50, 32], P('dp'), may hold values from -6 to 6
- noise: float32 [32, 50, 32], P('dp'), may hold values from -6 to 6
- time_index: int32 [32], P('dp'), may hold values from 0 to 999
- prefix_gain: float32 [2048], replicated, may hold values from 0.25 to 1.75
- key_weight: bfloat16 [2048, 256], P('dp'), may hold values from -0.125 to 0.125
- value_weight: bfloat16 [2048, 256], P('dp'), may hold values from -0.125 to 0.125
- action_in: bfloat16 [32, 1024], replicated, may hold values from -1 to 1
- attn_gain: float32 [1024], replicated, may hold values from 0.25 to 1.75
- query_w: bfloat16 [1024, 2048], P('dp', 'mp'), may hold values from -0.1875 to 0.1875
- akey_w: bfloat16 [1024, 256], P('dp'), may hold values from -0.1875 to 0.1875
- avalue_w: bfloat16 [1024, 256], P('dp'), may hold values from -0.1875 to 0.1875
- out_w: bfloat16 [2048, 1024], P('mp', 'dp'), may hold values from -0.125 to 0.125
- mlp_gain: float32 [1024], replicated, may hold values from 0.25 to 1.75
- gate_w: bfloat16 [1024, 4096], P('dp', 'mp'), may hold values from -0.1875 to 0.1875
- up_w: bfloat16 [1024, 4096], P('dp', 'mp'), may hold values from -0.1875 to 0.1875
- down_w: bfloat16 [4096, 1024], P('mp', 'dp'), may hold values from -0.09375 to 0.09375
- final_gain: float32 [1024], replicated, may hold values from 0.25 to 1.75
- head_w: bfloat16 [1024, 32], replicated, may hold values from -0.1875 to 0.1875
Outputs:
- velocity: float32 [32, 50, 32], P(('dp', 'mp'))
- ep_loss: float32 [32], P(('dp', 'mp'))
Inputs may be any that keep to these rules, and one draw needn't show every extreme that they name: `prefix_len`: prefix positions at or above an episode's length are padding that no output reads.
All inputs are finite; a program needn't handle non-finite values.
Results may differ from a plain program's by a relative error of at most 0.009.
Values may be sent and summed in bfloat16 or wider, within the bound.
No kernel may reach another device: no remote copies, remote signals or barrier semaphores. Data moves between devices by JAX's collectives and lax.ppermute only.
A program may use at most 64 MiB of HBM per device.

v0:
```python
import math

import jax
import jax.numpy as jnp
from jax import lax
from jax.sharding import PartitionSpec as P

TSTEPS = 1000


def rms(values, gain):
    return values * lax.rsqrt(jnp.mean(values * values, axis=-1, keepdims=True) + 1e-06) * gain


def time_embed(times, width):
    half = width // 2
    steps = jnp.arange(half, dtype=jnp.float32)
    period = 0.004 * jnp.power(jnp.float32(1000.0), steps / (half - 1))
    angle = times[:, None] * (2.0 * math.pi) / period[None, :]
    return jnp.concatenate([jnp.sin(angle), jnp.cos(angle)], axis=-1)


def attend(query, pkeys, pvals, akeys, avals, lengths):
    live = jnp.arange(pkeys.shape[1], dtype=jnp.int32)[None, :] < lengths[:, None]
    scores = jnp.einsum("erd,epd->erp", query, pkeys, preferred_element_type=jnp.float32)
    probs = jnp.where(live[:, None, :], jnp.exp(scores), 0.0)
    action_scores = jnp.einsum("erd,ecd->erc", query, akeys, preferred_element_type=jnp.float32)
    action_probs = jnp.exp(action_scores)
    denom = jnp.sum(probs, axis=-1) + jnp.sum(action_probs, axis=-1)
    weighted = jnp.einsum(
        "erp,epd->erd", probs.astype(jnp.bfloat16), pvals, preferred_element_type=jnp.float32
    )
    weighted = weighted + jnp.einsum(
        "erc,ecd->erd", action_probs.astype(jnp.bfloat16), avals, preferred_element_type=jnp.float32
    )
    return (weighted / denom[:, :, None]).astype(jnp.bfloat16)


def on_device(
    prefix_hidden,
    prefix_len,
    actions,
    noise,
    time_index,
    prefix_gain,
    key_weight,
    value_weight,
    action_in,
    attn_gain,
    query_w,
    akey_w,
    avalue_w,
    out_w,
    mlp_gain,
    gate_w,
    up_w,
    down_w,
    final_gain,
    head_w,
):
    own_eps, positions, width = prefix_hidden.shape
    group_eps, span, adim = actions.shape
    expert = action_in.shape[1]
    head_size = key_weight.shape[1]
    local_heads = query_w.shape[1] // head_size
    rows_total = group_eps * span
    own_rows = own_eps * span
    member = lax.axis_index("mp")
    first_row = member * own_rows
    first_ep = member * own_eps
    times = (time_index.astype(jnp.float32) + 0.5) / TSTEPS
    x_t = times[:, None, None] * noise + (1.0 - times)[:, None, None] * actions
    target = noise - actions
    x_in = x_t.reshape(rows_total, adim).astype(jnp.bfloat16)
    temb = time_embed(times, expert)
    h0 = (
        jnp.dot(x_in, action_in, preferred_element_type=jnp.float32).reshape(
            group_eps, span, expert
        )
        + temb[:, None, :]
    )
    h0 = h0.reshape(rows_total, expert)
    key_full, value_full = (
        lax.all_gather(key_weight, "dp", axis=0, tiled=True),
        lax.all_gather(value_weight, "dp", axis=0, tiled=True),
    )
    prefix_normed = rms(
        prefix_hidden.reshape(own_eps * positions, width).astype(jnp.float32), prefix_gain
    ).astype(jnp.bfloat16)
    pkeys = (
        jnp.dot(prefix_normed, key_full, preferred_element_type=jnp.float32)
        .astype(jnp.bfloat16)
        .reshape(own_eps, positions, head_size)
    )
    pvals = (
        jnp.dot(prefix_normed, value_full, preferred_element_type=jnp.float32)
        .astype(jnp.bfloat16)
        .reshape(own_eps, positions, head_size)
    )
    normed = rms(h0, attn_gain).astype(jnp.bfloat16)
    query_full, akey_full, avalue_full = (
        lax.all_gather(query_w, "dp", axis=0, tiled=True),
        lax.all_gather(akey_w, "dp", axis=0, tiled=True),
        lax.all_gather(avalue_w, "dp", axis=0, tiled=True),
    )
    query = (
        jnp.dot(normed, query_full, preferred_element_type=jnp.float32) * head_size ** (-0.5)
    ).astype(jnp.bfloat16)
    akeys = (
        jnp.dot(normed, akey_full, preferred_element_type=jnp.float32)
        .astype(jnp.bfloat16)
        .reshape(group_eps, span, head_size)
    )
    avals = (
        jnp.dot(normed, avalue_full, preferred_element_type=jnp.float32)
        .astype(jnp.bfloat16)
        .reshape(group_eps, span, head_size)
    )
    keys_all, vals_all = (
        lax.all_gather(pkeys, "mp", axis=0, tiled=True),
        lax.all_gather(pvals, "mp", axis=0, tiled=True),
    )
    attn = attend(
        query.reshape(group_eps, span * local_heads, head_size),
        keys_all,
        vals_all,
        akeys,
        avals,
        prefix_len,
    )
    attn = attn.reshape(rows_total, local_heads * head_size)
    out_full = lax.all_gather(out_w, "dp", axis=1, tiled=True)
    gate_full, up_full = (
        lax.all_gather(gate_w, "dp", axis=0, tiled=True),
        lax.all_gather(up_w, "dp", axis=0, tiled=True),
    )
    down_full = lax.all_gather(down_w, "dp", axis=1, tiled=True)
    h0_own = lax.dynamic_slice_in_dim(h0, first_row, own_rows, 0)
    h1 = h0_own + lax.psum_scatter(
        jnp.dot(attn, out_full, preferred_element_type=jnp.float32).astype(jnp.bfloat16),
        "mp",
        scatter_dimension=0,
        tiled=True,
    ).astype(jnp.float32)
    mixed_own = rms(h1, mlp_gain).astype(jnp.bfloat16)
    mixed = lax.all_gather(mixed_own, "mp", axis=0, tiled=True)
    gate = jnp.dot(mixed, gate_full, preferred_element_type=jnp.float32)
    upper = jnp.dot(mixed, up_full, preferred_element_type=jnp.float32)
    hidden = (jax.nn.gelu(gate, approximate=True) * upper).astype(jnp.bfloat16)
    h2 = h1 + lax.psum_scatter(
        jnp.dot(hidden, down_full, preferred_element_type=jnp.float32).astype(jnp.bfloat16),
        "mp",
        scatter_dimension=0,
        tiled=True,
    ).astype(jnp.float32)
    final = rms(h2, final_gain).astype(jnp.bfloat16)
    velocity = jnp.dot(final, head_w, preferred_element_type=jnp.float32).reshape(
        own_eps, span, adim
    )
    own_target = lax.dynamic_slice_in_dim(target, first_ep, own_eps, 0)
    diff = velocity - own_target
    ep_loss = jnp.mean(diff * diff, axis=(1, 2))
    return (velocity, ep_loss)


def solution(mesh):
    in_specs = (
        P(("dp", "mp"), None, None),
        P("dp"),
        P("dp", None, None),
        P("dp", None, None),
        P("dp"),
        P(),
        P("dp", None),
        P("dp", None),
        P(),
        P(),
        P("dp", "mp"),
        P("dp", None),
        P("dp", None),
        P("mp", "dp"),
        P(),
        P("dp", "mp"),
        P("dp", "mp"),
        P("mp", "dp"),
        P(),
        P(),
    )
    out_specs = (P(("dp", "mp"), None, None), P(("dp", "mp")))
    return jax.shard_map(
        on_device, mesh=mesh, in_specs=in_specs, out_specs=out_specs, check_vma=False
    )
```

profile of v0, /device:TPU:6, one launch (start us, length us, event | category | flops | bytes accessed | tf_op | source)
XLA Modules:
  0.0 404.9 jit_solution(4263375516487390356)
XLA Ops:
  7.2 0.7 all-gather.15.cloned.1.call-update
  8.0 0.7 all-gather.17.cloned.1.call-update
  8.7 0.7 all-gather.13.cloned.1.call-update
  9.5 3.1 fusion.2
  12.5 38.1 %all-gather.15.cloned.1.call-done = bf16[2048,256]{1,0:T(8,128)(2,1)} async-done(((bf16[256,256]{1,0:T(8,128)(2,1)}), bf16[2048,256]{1,0:T(8,128)(2,1)}) %all-gather.15.cloned.1.call-update) | async-done | bytes 1048592 | tf_op jit(solution)/shard_map/all_gather | solution.py:84
  50.7 4.6 %convolution_convert_fusion.1 = bf16[1024,256]{1,0:T(8,128)(2,1)} fusion(bf16[2048,256]{1,0:T(8,128)(2,1)} %all-gather.15.cloned.1.call-done, bf16[1,1024,2048]{2,1,0:T(8,128)(2,1)} %param.20, f32[2048]{0:T(1024)S(1)} %copy-done.12, f32[1024]{0:T(1024)S(1)} %add_rsqrt_fusion), kind=kOutput, calls=%fused_computation.9 | convolution fusion | flops 1082392576 | bytes 5779456 | tf_op jit(solution)/shard_map/dot_general | solution.py:91
  55.4 36.4 %all-gather.17.cloned.1.call-done = bf16[2048,256]{1,0:T(8,128)(2,1)} async-done(((bf16[256,256]{1,0:T(8,128)(2,1)}), bf16[2048,256]{1,0:T(8,128)(2,1)}) %all-gather.17.cloned.1.call-update) | async-done | bytes 1048592 | tf_op jit(solution)/shard_map/all_gather | solution.py:85
  91.8 4.6 %convolution_convert_fusion = bf16[1024,256]{1,0:T(8,128)(2,1)} fusion(bf16[2048,256]{1,0:T(8,128)(2,1)} %all-gather.17.cloned.1.call-done, bf16[1,1024,2048]{2,1,0:T(8,128)(2,1)} %param.20, f32[2048]{0:T(1024)S(1)} %copy-done.12, f32[1024]{0:T(1024)S(1)} %add_rsqrt_fusion), kind=kOutput, calls=%fused_computation.8 | convolution fusion | flops 1082392576 | bytes 5779456 | tf_op jit(solution)/shard_map/dot_general | solution.py:96
  96.5 0.5 all-gather.19.cloned.1.call-update
  97.1 0.7 all-gather.21.cloned.1.call-update
  97.8 0.7 all-gather.23.cloned.1.call-update
  98.6 0.7 all-gather.25.cloned.1.call-update
  99.3 0.1 fusion.38
  99.5 0.5 multiply_reduce_fusion
  100.0 0.1 reshape.115
  100.2 30.9 %all_gather.41 = bf16[1024,256]{1,0:T(8,128)(2,1)S(1)} all-gather(bf16[128,256]{1,0:T(8,128)(2,1)S(1)} %copy-done.3), channel_id=1, replica_groups=mesh['dp'=8,'mp'=4] {'dp'}, dimensions={0}, use_global_device_ids=true | all-gather | bytes 589824 | tf_op jit(solution)/shard_map/all_gather | solution.py:103
  131.1 0.1 multiply_convert_fusion
  131.2 0.3 convolution_convert_fusion.5
  131.6 31.5 %all_gather.42 = bf16[1024,256]{1,0:T(8,128)(2,1)S(1)} all-gather(bf16[128,256]{1,0:T(8,128)(2,1)S(1)} %copy-done.4), channel_id=1, replica_groups=mesh['dp'=8,'mp'=4] {'dp'}, dimensions={0}, use_global_device_ids=true | all-gather | bytes 589824 | tf_op jit(solution)/shard_map/all_gather | solution.py:104
  163.1 0.3 convolution_convert_fusion.4
  163.5 1.6 fusion.10
  165.2 0.2 fusion.46
  165.5 2.5 fusion.45
  168.0 14.4 %all-gather.29.cloned.1.call-done = bf16[4096,256]{1,0:T(8,128)(2,1)} async-done(((bf16[1024,256]{1,0:T(8,128)(2,1)}), bf16[4096,256]{1,0:T(8,128)(2,1)}) %all-gather.29.cloned.1.call-update) | async-done | bytes 2097168 | tf_op jit(solution)/shard_map/all_gather | solution.py:121
  182.4 2.0 fusion.11
  184.5 0.3 fusion.9
  184.8 39.4 %all-gather.19.cloned.1.call-done = bf16[512,1024]{1,0:T(8,128)(2,1)} async-done(((bf16[512,128]{1,0:T(8,128)(2,1)}), bf16[512,1024]{1,0:T(8,128)(2,1)}) %all-gather.19.cloned.1.call-update) | async-done | bytes 1048592 | tf_op jit(solution)/shard_map/all_gather | solution.py:132
  224.2 1.6 convolution_convert_fusion.3
  225.8 10.1 %fusion = bf16[56,1024]{1,0:T(8,128)(2,1)S(1)} fusion(bf16[200,1024]{1,0:T(8,128)(2,1)S(1)} %convolution_convert_fusion.3), kind=kCustom, calls=%all-reduce-scatter | all-reduce-scatter fusion | flops 229377 | bytes 524800
  236.0 1.9 collective-permute-start
  237.9 0.6 dynamic-slice.6
  239.1 2.2 collective-permute-done
  241.4 0.2 concatenate.4
  241.6 0.2 multiply_reduce_fusion.2
  241.8 0.1 fusion.25
  241.9 6.3 %all-gather.2 = bf16[4,50,1024]{2,1,0:T(8,128)(2,1)S(1)} all-gather(bf16[1,50,1024]{2,1,0:T(8,128)(2,1)S(1)} %fusion.25), channel_id=1, replica_groups=mesh['dp'=8,'mp'=4] {'mp'}, dimensions={0}, use_global_device_ids=true | all-gather | bytes 512000 | tf_op jit(solution)/shard_map/all_gather | solution.py:146
  248.2 0.1 reshape.127
  248.3 25.8 %all-gather.21.cloned.1.call-done = bf16[1024,1024]{1,0:T(8,128)(2,1)} async-done(((bf16[128,1024]{1,0:T(8,128)(2,1)}), bf16[1024,1024]{1,0:T(8,128)(2,1)}) %all-gather.21.cloned.1.call-update) | async-done | bytes 2097168 | tf_op jit(solution)/shard_map/all_gather | solution.py:134
  274.1 2.2 fusion.47
  276.3 47.6 %all-gather.23.cloned.1.call-done = bf16[1024,1024]{1,0:T(8,128)(2,1)} async-done(((bf16[128,1024]{1,0:T(8,128)(2,1)}), bf16[1024,1024]{1,0:T(8,128)(2,1)}) %all-gather.23.cloned.1.call-update) | async-done | bytes 2097168 | tf_op jit(solution)/shard_map/all_gather | solution.py:135
  323.8 51.9 %all-gather.25.cloned.1.call-done = bf16[1024,1024]{1,0:T(8,128)(2,1)} async-done(((bf16[1024,128]{1,0:T(8,128)(2,1)}), bf16[1024,1024]{1,0:T(8,128)(2,1)}) %all-gather.25.cloned.1.call-update) | async-done | bytes 2097168 | tf_op jit(solution)/shard_map/all_gather | solution.py:137
  375.7 3.3 convolution_convert_fusion.2
  379.0 10.2 %fusion.1 = bf16[56,1024]{1,0:T(8,128)(2,1)S(1)} fusion(bf16[200,1024]{1,0:T(8,128)(2,1)S(1)} %convolution_convert_fusion.2), kind=kCustom, calls=%all-reduce-scatter.1 | all-reduce-scatter fusion | flops 229377 | bytes 524800
  389.3 1.9 collective-permute-start.1
  391.2 3.5 collective-permute-done.1
  394.7 0.2 concatenate.5
  394.9 0.2 multiply_reduce_fusion.1
  395.1 1.5 fusion.35
  (55 shorter events, 1.0 us)
Async XLA Ops:
  7.2 92.3 %copy-start = (bf16[32,1024]{1,0:T(8,128)(2,1)S(1)}, bf16[32,1024]{1,0:T(8,128)(2,1)}, u32[]{:S(2)}) copy-start(bf16[32,1024]{1,0:T(8,128)(2,1)} %param.28) | copy-start | bytes 196612
  7.2 43.5 %all-gather.15.cloned.1.call-start = ((), (), s32[]{:S(2)}) async-start(), calls=%async_computation.1 | async-start | bytes 1179648 | tf_op jit(solution)/shard_map/all_gather | solution.py:84
  7.9 83.9 %all-gather.17.cloned.1.call-start = ((), (), s32[]{:S(2)}) async-start(), calls=%async_computation.2 | async-start | bytes 1179648 | tf_op jit(solution)/shard_map/all_gather | solution.py:85
  8.7 154.9 %all-gather.13.cloned.1.call-start = ((), (), s32[]{:S(2)}) async-start(), calls=%async_computation | async-start | bytes 1179648 | tf_op jit(solution)/shard_map/all_gather | solution.py:102
  9.4 41.3 %copy-start.12 = (f32[2048]{0:T(1024)S(1)}, f32[2048]{0:T(1024)}, u32[]{:S(2)}) copy-start(f32[2048]{0:T(1024)} %param.25) | copy-start | bytes 24580
  9.4 156.1 %all-gather.27.cloned.1.call-start = ((), (), s32[]{:S(2)}) async-start(), calls=%async_computation.7 | async-start | bytes 2621440 | tf_op jit(solution)/shard_map/all_gather | solution.py:120
  55.4 43.9 %copy-start.11 = (s32[4]{0:T(128)S(1)}, s32[4]{0:T(128)}, u32[]{:S(2)}) copy-start(s32[4]{0:T(128)} %param.24) | copy-start | bytes 52
  55.4 44.1 %copy-start.1 = (f32[4,50,32]{1,2,0:T(8,128)S(1)}, f32[4,50,32]{1,2,0:T(8,128)}, u32[]{:S(2)}) copy-start(f32[4,50,32]{1,2,0:T(8,128)} %param.22) | copy-start | bytes 76804
  55.4 44.1 %copy-start.2 = (f32[4,50,32]{1,2,0:T(8,128)S(1)}, f32[4,50,32]{1,2,0:T(8,128)}, u32[]{:S(2)}) copy-start(f32[4,50,32]{1,2,0:T(8,128)} %param.23) | copy-start | bytes 76804
  55.4 127.0 %all-gather.29.cloned.1.call-start = ((), (), s32[]{:S(2)}) async-start(), calls=%async_computation.8 | async-start | bytes 2621440 | tf_op jit(solution)/shard_map/all_gather | solution.py:121
  96.4 3.8 copy-start.3
  96.5 127.8 %all-gather.19.cloned.1.call-start = ((), (), s32[]{:S(2)}) async-start(), calls=%async_computation.3 | async-start | bytes 1179648 | tf_op jit(solution)/shard_map/all_gather | solution.py:132
  97.0 34.1 %copy-start.6 = (f32[1024]{0:T(1024)S(1)}, f32[1024]{0:T(1024)}, u32[]{:S(2)}) copy-start(f32[1024]{0:T(1024)} %param.29) | copy-start | bytes 12292
  97.0 177.0 %all-gather.21.cloned.1.call-start = ((), (), s32[]{:S(2)}) async-start(), calls=%async_computation.4 | async-start | bytes 2359296 | tf_op jit(solution)/shard_map/all_gather | solution.py:134
  97.8 226.0 %all-gather.23.cloned.1.call-start = ((), (), s32[]{:S(2)}) async-start(), calls=%async_computation.5 | async-start | bytes 2359296 | tf_op jit(solution)/shard_map/all_gather | solution.py:135
  98.5 277.1 %all-gather.25.cloned.1.call-start = ((), (), s32[]{:S(2)}) async-start(), calls=%async_computation.6 | async-start | bytes 2359296 | tf_op jit(solution)/shard_map/all_gather | solution.py:137
  100.0 31.6 %copy-start.4 = (bf16[128,256]{1,0:T(8,128)(2,1)S(1)}, bf16[128,256]{1,0:T(8,128)(2,1)}, u32[]{:S(2)}) copy-start(bf16[128,256]{1,0:T(8,128)(2,1)} %param.32) | copy-start | bytes 196612
  131.1 32.4 %copy-start.9 = (s32[4]{0:T(128)S(1)}, s32[4]{0:T(128)}, u32[]{:S(2)}) copy-start(s32[4]{0:T(128)} %param.21) | copy-start | bytes 52
  184.5 53.4 %copy-start.10 = (u32[32]{0:T(128)S(1)}, u32[32]{0:T(128)}, u32[]{:S(2)}) copy-start(u32[32]{0:T(128)} %constant.63) | copy-start | bytes 388
  184.7 57.0 %copy-start.7 = (f32[1024]{0:T(1024)S(1)}, f32[1024]{0:T(1024)}, u32[]{:S(2)}) copy-start(f32[1024]{0:T(1024)} %param.34) | copy-start | bytes 12292
  236.0 5.4 %collective-permute-start = (bf16[18,1024]{1,0:T(8,128)(2,1)S(1)}, bf16[18,1024]{1,0:T(8,128)(2,1)S(1)}, u32[]{:S(2)}, u32[]{:S(2)}) collective-permute-start(bf16[18,1024]{1,0:T(8,128)(2,1)S(1)} %slice), channel_id=1, source_target_pairs={{0,1},{1,2},{2,3},{4,5},{5,6},{6,7},{8,9},{9,10},{10,11},{12,13},{... | collective-permute-start | bytes 110600
  276.2 118.9 %copy-start.5 = (bf16[1024,32]{0,1:T(8,128)(2,1)S(1)}, bf16[1024,32]{0,1:T(8,128)(2,1)}, u32[]{:S(2)}) copy-start(bf16[1024,32]{0,1:T(8,128)(2,1)} %param.39) | copy-start | bytes 196612
  276.3 118.9 %copy-start.8 = (f32[1024]{0:T(1024)S(1)}, f32[1024]{0:T(1024)}, u32[]{:S(2)}) copy-start(f32[1024]{0:T(1024)} %param.38) | copy-start | bytes 12292
  389.3 5.4 %collective-permute-start.1 = (bf16[18,1024]{1,0:T(8,128)(2,1)S(1)}, bf16[18,1024]{1,0:T(8,128)(2,1)S(1)}, u32[]{:S(2)}, u32[]{:S(2)}) collective-permute-start(bf16[18,1024]{1,0:T(8,128)(2,1)S(1)} %slice.1), channel_id=1, source_target_pairs={{0,1},{1,2},{2,3},{4,5},{5,6},{6,7},{8,9},{9,10},{10,11},{12,13},{... | collective-permute-start | bytes 110600
Sparse Core Ops, SparseCore 0:
  10.1 40.5 all-gather.14
  52.8 38.9 all-gather.16
  94.0 41.6 all-gather.12
  137.0 21.2 all-gather.26
  159.8 22.5 all-gather.28
  184.3 39.8 all-gather.18
  226.3 47.6 all-gather.20
  276.2 47.6 all-gather.22
  325.9 49.7 all-gather.24
where the time goes:
time: 405 us
  waiting for transfers between devices  264 us (65%)
  blocking collectives  89.1 us (22%)
  matrix products  25.5 us (6%)
  between operations  16.7 us (4%)
  starting transfers between devices  4.19 us (1%)
    all_gather x1, waiting for transfers between devices, on_device(): down_full = lax.all_gather(down_w, 'dp', axis=1, tiled=True)  51.9 us
    all_gather x1, waiting for transfers between devices, on_device(): lax.all_gather(up_w, 'dp', axis=0, tiled=True)  47.6 us
    all_gather x1, waiting for transfers between devices, on_device(): out_full = lax.all_gather(out_w, 'dp', axis=1, tiled=True)  39.4 us
    all_gather x1, waiting for transfers between devices, on_device(): lax.all_gather(key_weight, 'dp', axis=0, tiled=True)  38.1 us
    all_gather x1, waiting for transfers between devices, on_device(): lax.all_gather(value_weight, 'dp', axis=0, tiled=True)  36.4 us
    all_gather x1, blocking collectives, on_device(): lax.all_gather(avalue_w, 'dp', axis=0, tiled=True)  31.5 us
    all_gather x1, blocking collectives, on_device(): lax.all_gather(akey_w, 'dp', axis=0, tiled=True)  30.9 us
    all_gather x1, waiting for transfers between devices, on_device(): lax.all_gather(gate_w, 'dp', axis=0, tiled=True)  25.8 us
  transfers between devices with their start and end apart: 11, of which 9 were waited for; matrix products, arithmetic and copies ran while one was open for 9% of the time, Pallas kernels for 0%

commit v1 on v0

--- a/solution.py
+++ b/solution.py
@@ -3,9 +3,19 @@
 import jax
 import jax.numpy as jnp
 from jax import lax
+from jax.experimental import pallas as pl
+from jax.experimental.pallas import tpu as pltpu
+from jax.sharding import Mesh
 from jax.sharding import PartitionSpec as P
 
+
 TSTEPS = 1000
+BF = jnp.bfloat16
+F32 = jnp.float32
+LANES = 128
+PAD = 64
+DP, MP = ("o", "i"), ("x", "c")
+RELS = ((0, 0), (1, 0), (0, 1), (1, 1))
 
 
 def rms(values, gain):
@@ -36,7 +46,7 @@
     return (weighted / denom[:, :, None]).astype(jnp.bfloat16)
 
 
-def on_device(
+def gather_all(
     prefix_hidden,
     prefix_len,
     actions,
@@ -65,7 +75,7 @@
     local_heads = query_w.shape[1] // head_size
     rows_total = group_eps * span
     own_rows = own_eps * span
-    member = lax.axis_index("mp")
+    member = lax.axis_index(MP)
     first_row = member * own_rows
     first_ep = member * own_eps
     times = (time_index.astype(jnp.float32) + 0.5) / TSTEPS
@@ -81,8 +91,8 @@
     )
     h0 = h0.reshape(rows_total, expert)
     key_full, value_full = (
-        lax.all_gather(key_weight, "dp", axis=0, tiled=True),
-        lax.all_gather(value_weight, "dp", axis=0, tiled=True),
+        lax.all_gather(key_weight, DP, axis=0, tiled=True),
+        lax.all_gather(value_weight, DP, axis=0, tiled=True),
     )
     prefix_normed = rms(
         prefix_hidden.reshape(own_eps * positions, width).astype(jnp.float32), prefix_gain
@@ -99,9 +109,9 @@
     )
     normed = rms(h0, attn_gain).astype(jnp.bfloat16)
     query_full, akey_full, avalue_full = (
-        lax.all_gather(query_w, "dp", axis=0, tiled=True),
-        lax.all_gather(akey_w, "dp", axis=0, tiled=True),
-        lax.all_gather(avalue_w, "dp", axis=0, tiled=True),
+        lax.all_gather(query_w, DP, axis=0, tiled=True),
+        lax.all_gather(akey_w, DP, axis=0, tiled=True),
+        lax.all_gather(avalue_w, DP, axis=0, tiled=True),
     )
     query = (
         jnp.dot(normed, query_full, preferred_element_type=jnp.float32) * head_size ** (-0.5)
@@ -117,8 +127,8 @@
         .reshape(group_eps, span, head_size)
     )
     keys_all, vals_all = (
-        lax.all_gather(pkeys, "mp", axis=0, tiled=True),
-        lax.all_gather(pvals, "mp", axis=0, tiled=True),
+        lax.all_gather(pkeys, MP, axis=0, tiled=True),
+        lax.all_gather(pvals, MP, axis=0, tiled=True),
     )
     attn = attend(
         query.reshape(group_eps, span * local_heads, head_size),
@@ -129,27 +139,27 @@
         prefix_len,
     )
     attn = attn.reshape(rows_total, local_heads * head_size)
-    out_full = lax.all_gather(out_w, "dp", axis=1, tiled=True)
+    out_full = lax.all_gather(out_w, DP, axis=1, tiled=True)
     gate_full, up_full = (
-        lax.all_gather(gate_w, "dp", axis=0, tiled=True),
-        lax.all_gather(up_w, "dp", axis=0, tiled=True),
-    )
-    down_full = lax.all_gather(down_w, "dp", axis=1, tiled=True)
+        lax.all_gather(gate_w, DP, axis=0, tiled=True),
+        lax.all_gather(up_w, DP, axis=0, tiled=True),
+    )
+    down_full = lax.all_gather(down_w, DP, axis=1, tiled=True)
     h0_own = lax.dynamic_slice_in_dim(h0, first_row, own_rows, 0)
     h1 = h0_own + lax.psum_scatter(
         jnp.dot(attn, out_full, preferred_element_type=jnp.float32).astype(jnp.bfloat16),
-        "mp",
+        MP,
         scatter_dimension=0,
         tiled=True,
     ).astype(jnp.float32)
     mixed_own = rms(h1, mlp_gain).astype(jnp.bfloat16)
-    mixed = lax.all_gather(mixed_own, "mp", axis=0, tiled=True)
+    mixed = lax.all_gather(mixed_own, MP, axis=0, tiled=True)
     gate = jnp.dot(mixed, gate_full, preferred_element_type=jnp.float32)
     upper = jnp.dot(mixed, up_full, preferred_element_type=jnp.float32)
     hidden = (jax.nn.gelu(gate, approximate=True) * upper).astype(jnp.bfloat16)
     h2 = h1 + lax.psum_scatter(
         jnp.dot(hidden, down_full, preferred_element_type=jnp.float32).astype(jnp.bfloat16),
-        "mp",
+        MP,
         scatter_dimension=0,
         tiled=True,
     ).astype(jnp.float32)
@@ -161,6 +171,500 @@
     diff = velocity - own_target
     ep_loss = jnp.mean(diff * diff, axis=(1, 2))
     return (velocity, ep_loss)
+
+
+def dot(a, b):
+    return jnp.dot(a, b, preferred_element_type=F32)
+
+
+def after(values, *earlier):
+    return lax.optimization_barrier((values,) + earlier)[0]
+
+
+def at(*block):
+    return pl.BlockSpec(block, lambda *s: (0,) * len(block))
+
+
+def like(*shape, dtype=BF):
+    return jax.ShapeDtypeStruct(shape, dtype)
+
+
+def split_rows(total, rows, outs):
+    outs[0][...] = total[:rows].astype(outs[0].dtype)
+    for k in range(1, len(outs)):
+        outs[k][...] = total[PAD * k : PAD * k + rows].astype(outs[k].dtype)
+
+
+def pack_weights(query_w, akey_w, avalue_w, key_w, value_w, down_w, out_w, gate_w, up_w):
+    rows, hq = query_w.shape
+    ha, hk = akey_w.shape[1], key_w.shape[1]
+    quarter, half = ha // 2, key_w.shape[0] // 2
+    nd, units = down_w.shape[0], gate_w.shape[1]
+
+    def kernel(q, ak, av, kw, vw, dw, ow, gw, uw, first, od, gu):
+        xx, cc = lax.axis_index("x"), lax.axis_index("c")
+        cols = pl.ds(pl.multiple_of(cc * quarter, quarter), quarter)
+        part = pl.ds(pl.multiple_of(cc * half, half), half)
+        first[:, :hq] = q[...]
+
+        @pl.when(xx == 0)
+        def _():
+            first[:, hq : hq + quarter] = ak[:, cols]
+            first[:, hq + quarter :] = kw[part, :]
+
+        @pl.when(xx != 0)
+        def _():
+            first[:, hq : hq + quarter] = av[:, cols]
+            first[:, hq + quarter :] = vw[part, :]
+
+        od[:nd] = dw[...]
+        od[nd:] = ow[...]
+        gu[:, :units] = gw[...]
+        gu[:, units:] = uw[...]
+
+    return pl.pallas_call(
+        kernel,
+        out_shape=(
+            like(rows, hq + quarter + hk),
+            like(nd + out_w.shape[0], down_w.shape[1]),
+            like(rows, 2 * units),
+        ),
+        name="pack_weights",
+    )(query_w, akey_w, avalue_w, key_w, value_w, down_w, out_w, gate_w, up_w)
+
+
+def expert_in(x_g, temb, action_in, attn_gain, mlp_gain, final_gain, head_w, span, per):
+    rows = x_g.shape[0]
+    groups, width = temb.shape
+    adim = head_w.shape[0]
+    count = width // per
+
+    def kernel(x, te, act, ga, gm, gf, hw, an, h0, gains, head_p, h_all):
+        oo, cc = lax.axis_index("o"), lax.axis_index("c")
+        for b in range(count):
+            r, c = b % (count // 2), b // (count // 2)
+            block = (oo ^ r) * 2 + (cc ^ c)
+            src = pl.ds(pl.multiple_of(block * per, per), per)
+            dst = slice(b * per, (b + 1) * per)
+            h = dot(x[...], act[:, src])
+            for k in range(groups):
+                h_all[PAD * k : PAD * (k + 1), dst] = h[PAD * k : PAD * (k + 1)] + te[k : k + 1, src]
+            gains[0:1, dst] = gm[:, src]
+            gains[1:2, dst] = gf[:, src]
+            gains[2:3, dst] = ga[:, src]
+            head_p[:, dst] = hw[:, src]
+        h = h_all[...]
+        h0[...] = h[:span]
+        an[...] = (
+            h * lax.rsqrt(jnp.mean(h * h, axis=-1, keepdims=True) + 1e-06) * gains[2:3, :]
+        ).astype(BF)
+
+    return pl.pallas_call(
+        kernel,
+        out_shape=(
+            like(rows, width),
+            like(span, width, dtype=F32),
+            like(8, width, dtype=F32),
+            like(adim, width),
+        ),
+        scratch_shapes=[pltpu.VMEM((rows, width), F32)],
+        name="expert_in",
+    )(
+        x_g,
+        temb,
+        action_in,
+        attn_gain.reshape(1, width),
+        mlp_gain.reshape(1, width),
+        final_gain.reshape(1, width),
+        head_w,
+    )
+
+
+def unpack_first(got, cols):
+    rows, total = got[0].shape
+    count = len(got)
+
+    def kernel(*refs):
+        qa, kv = refs[count:]
+        for r in range(count):
+            qa[r * rows : (r + 1) * rows] = refs[r][:, :cols]
+            kv[r * rows : (r + 1) * rows] = refs[r][:, cols:]
+
+    return pl.pallas_call(
+        kernel,
+        out_shape=(like(count * rows, cols), like(count * rows, total - cols)),
+        name="unpack_first",
+    )(*got)
+
+
+def queries(an, own, other, heads_cols, scale, span):
+    mid, cols = own.shape
+
+    def kernel(a, w0, w1, *refs):
+        outs, total = refs[:-1], refs[-1]
+        v = dot(a[:, :mid], w0[...]) + dot(a[:, mid:], w1[...])
+        total[:, :heads_cols] = v[:, :heads_cols] * scale
+        total[:, heads_cols:] = v[:, heads_cols:]
+        split_rows(total[...], span, outs)
+
+    return pl.pallas_call(
+        kernel,
+        out_shape=[like(span, cols) for _ in RELS],
+        scratch_shapes=[pltpu.VMEM((an.shape[0], cols), F32)],
+        name="queries",
+    )(an, own, other)
+
+
+def attention(prefix, gain, kv_own, kv_oth, qa, length, heads_cols):
+    positions, width = prefix.shape
+    tall, hd = kv_own[0].shape
+    span, qa_cols = qa[0].shape
+    per_part = heads_cols // hd
+    heads = len(RELS) * per_part
+    step = 512
+    steps = positions // step
+    count = 16
+    per = width // count
+    no = count // 4
+
+    def kernel(len_ref, x, g, *refs):
+        own, oth, qs = refs[0:4], refs[4:8], refs[8:12]
+        outs = refs[12:16]
+        q_all, pn, acc, den = refs[16:20]
+        s = pl.program_id(0)
+        oo, ii, xx, cc = (lax.axis_index(n) for n in ("o", "i", "x", "c"))
+
+        @pl.when(s == 0)
+        def _():
+            q_all[...] = jnp.zeros_like(q_all)
+            for k in range(len(RELS)):
+                for h in range(per_part):
+                    q_all[PAD * (k * per_part + h) : PAD * (k * per_part + h) + span] = qs[k][
+                        :, h * hd : (h + 1) * hd
+                    ]
+            acc[...] = jnp.zeros_like(acc)
+            den[...] = jnp.zeros_like(den)
+
+        v = x[...].astype(F32)
+        scale = lax.rsqrt(jnp.mean(v * v, axis=-1, keepdims=True) + 1e-06)
+        for b in range(count):
+            r, i, c = b % no, (b // no) % 2, b // (2 * no)
+            block = ((oo ^ r) * 2 + (cc ^ c)) * 2 + (ii ^ i)
+            src = pl.ds(pl.multiple_of(block * per, per), per)
+            pn[:, b * per : (b + 1) * per] = (x[:, src].astype(F32) * scale * g[:, src]).astype(BF)
+        same = diff = 0.0
+        for c, refs_c in enumerate((own, oth)):
+            for i in range(2):
+                m = pn[:, (c * 2 + i) * tall : (c * 2 + i + 1) * tall]
+                same = same + dot(m, refs_c[i][...])
+                diff = diff + dot(m, refs_c[2 + i][...])
+        first = xx == 0
+        same, diff = same.astype(BF), diff.astype(BF)
+        keys = jnp.where(first, same, diff)
+        vals = jnp.where(first, diff, same)
+        nt = (((1,), (1,)), ((), ()))
+        sc = lax.dot_general(q_all[...], keys, nt, preferred_element_type=F32)
+        spot = s * step + lax.broadcasted_iota(jnp.int32, sc.shape, 1)
+        p = jnp.where(spot < len_ref[0], jnp.exp(sc), 0.0)
+        den[...] += jnp.sum(p, axis=-1, keepdims=True)
+        acc[...] += dot(p.astype(BF), vals)
+
+        @pl.when(s == steps - 1)
+        def _():
+            parts = [q[:, heads_cols:] for q in qs]
+            flat = ii == 0
+            lo = [jnp.where(flat, parts[2 * k], parts[2 * k + 1]) for k in range(2)]
+            hi = [jnp.where(flat, parts[2 * k + 1], parts[2 * k]) for k in range(2)]
+            sa = jnp.concatenate([lo[0], hi[0]], axis=1)
+            da = jnp.concatenate([lo[1], hi[1]], axis=1)
+            ak, av = jnp.where(first, sa, da), jnp.where(first, da, sa)
+            pa = jnp.exp(lax.dot_general(q_all[...], ak, nt, preferred_element_type=F32))
+            total = den[...] + jnp.sum(pa, axis=-1, keepdims=True)
+            res = ((acc[...] + dot(pa.astype(BF), av)) / total).astype(BF)
+            for k in range(len(RELS)):
+                for h in range(per_part):
+                    n = PAD * (k * per_part + h)
+                    outs[k][:, h * hd : (h + 1) * hd] = res[n : n + span]
+
+    return pl.pallas_call(
+        kernel,
+        grid=(steps,),
+        out_shape=[like(span, heads_cols) for _ in RELS],
+        in_specs=[
+            pl.BlockSpec(memory_space=pltpu.SMEM),
+            pl.BlockSpec((step, width), lambda s: (s, 0)),
+            at(1, width),
+        ]
+        + [at(tall, hd)] * 8
+        + [at(span, qa_cols)] * 4,
+        out_specs=[at(span, heads_cols)] * 4,
+        scratch_shapes=[
+            pltpu.VMEM((PAD * heads, hd), BF),
+            pltpu.VMEM((step, width), BF),
+            pltpu.VMEM((PAD * heads, hd), F32),
+            pltpu.VMEM((PAD * heads, 1), F32),
+        ],
+        name="prefix_attention",
+    )(length, prefix, gain.reshape(1, width), *kv_own, *kv_oth, *qa)
+
+
+def row_outs(rows, width, parts):
+    return [like(rows, width, dtype=F32)] + [like(rows, width) for _ in range(parts - 1)]
+
+
+def out_project(attn, pieces, units):
+    rows = attn[0].shape[0]
+    parts, count = len(attn), len(pieces)
+    tall, cols = pieces[0].shape
+    place = tall // units - 1
+
+    def kernel(*refs):
+        a_refs, w_refs = refs[:parts], refs[parts : parts + count]
+        outs, a_all, total = refs[parts + count : -2], refs[-2], refs[-1]
+        for k in range(parts):
+            a_all[PAD * k : PAD * k + rows] = a_refs[k][...]
+        for b in range(0, count, 2):
+            pair = jnp.concatenate([w_refs[b][...], w_refs[b + 1][...]], axis=1)
+            total[:, b * cols : (b + 2) * cols] = dot(a_all[...], pair)
+        split_rows(total, rows, outs)
+
+    return pl.pallas_call(
+        kernel,
+        grid=(1,),
+        out_shape=row_outs(rows, count * cols, parts),
+        in_specs=[at(rows, units)] * parts
+        + [pl.BlockSpec((units, cols), lambda s: (place, 0))] * count,
+        out_specs=[at(rows, count * cols)] * parts,
+        scratch_shapes=[
+            pltpu.VMEM((PAD * parts, units), BF),
+            pltpu.VMEM((PAD * parts, count * cols), F32),
+        ],
+        name="out_project",
+    )(*attn, *pieces)
+
+
+def feed_forward(mn, gu, od, units):
+    rows = mn[0].shape[0]
+    parts, count = len(mn), len(gu)
+    per, cols = gu[0].shape[0], od[0].shape[1]
+    step = 256
+    steps = units // step
+
+    def kernel(*refs):
+        m_refs, refs = refs[:parts], refs[parts:]
+        g_refs, u_refs, d_refs = refs[:count], refs[count : 2 * count], refs[2 * count : 3 * count]
+        outs, m_all, total = refs[3 * count : -2], refs[-2], refs[-1]
+        s = pl.program_id(0)
+
+        @pl.when(s == 0)
+        def _():
+            for k in range(parts):
+                m_all[PAD * k : PAD * k + rows] = m_refs[k][...]
+            total[...] = jnp.zeros_like(total)
+
+        gate = dot(m_all[...], jnp.concatenate([g[...] for g in g_refs], axis=0))
+        up = dot(m_all[...], jnp.concatenate([u[...] for u in u_refs], axis=0))
+        hid = (jax.nn.gelu(gate, approximate=True) * up).astype(BF)
+        for b in range(0, count, 2):
+            pair = jnp.concatenate([d_refs[b][...], d_refs[b + 1][...]], axis=1)
+            total[:, b * cols : (b + 2) * cols] += dot(hid, pair)
+
+        @pl.when(s == steps - 1)
+        def _():
+            split_rows(total, rows, outs)
+
+    return pl.pallas_call(
+        kernel,
+        grid=(steps,),
+        out_shape=row_outs(rows, count * cols, parts),
+        in_specs=[at(rows, count * per)] * parts
+        + [pl.BlockSpec((per, step), lambda s: (0, s))] * count
+        + [pl.BlockSpec((per, step), lambda s: (0, s + steps))] * count
+        + [pl.BlockSpec((step, cols), lambda s: (s, 0))] * count,
+        out_specs=[at(rows, count * cols)] * parts,
+        scratch_shapes=[
+            pltpu.VMEM((PAD * parts, count * per), BF),
+            pltpu.VMEM((PAD * parts, count * cols), F32),
+        ],
+        name="feed_forward",
+    )(*mn, *gu, *gu, *od)
+
+
+def make(no, ni, nx, nc):
+    def flip(value, axis):
+        return lax.ppermute(value, axis, [(0, 1), (1, 0)])
+
+    def cross(value, di, dx):
+        pairs = [
+            (i * nx + x, (i ^ di) * nx + (x ^ dx)) for i in range(ni) for x in range(nx)
+        ]
+        return lax.ppermute(value, ("i", "x"), pairs)
+
+    def spread(value):
+        return [value] + [cross(value, di, dx) for di, dx in RELS[1:]]
+
+    def exchange(parts):
+        return [parts[0]] + [cross(p, di, dx) for p, (di, dx) in zip(parts[1:], RELS[1:])]
+
+    def turned(value, r):
+        return lax.ppermute(
+            value,
+            ("o", "i", "c"),
+            [
+                ((o * ni + i) * nc + c, ((o ^ r) * ni + c) * nc + i)
+                for o in range(no)
+                for i in range(ni)
+                for c in range(nc)
+            ],
+        )
+
+    def hop(value, pairs):
+        return lax.ppermute(value, "o", pairs)
+
+    def partner(r):
+        return [(o, o ^ r) for o in range(no)]
+
+    MIDDLE, OUTWARD = [(1, 2), (2, 1)], [(1, 0), (2, 3)]
+
+    def fast(
+        prefix_hidden,
+        prefix_len,
+        actions,
+        noise,
+        time_index,
+        prefix_gain,
+        key_weight,
+        value_weight,
+        action_in,
+        attn_gain,
+        query_w,
+        akey_w,
+        avalue_w,
+        out_w,
+        mlp_gain,
+        gate_w,
+        up_w,
+        down_w,
+        final_gain,
+        head_w,
+):
+        own_eps, positions, width = prefix_hidden.shape
+        _, span, adim = actions.shape
+        expert = action_in.shape[1]
+        hd = key_weight.shape[1]
+        heads_cols = query_w.shape[1]
+        units = gate_w.shape[1]
+        oo, xx, cc = (lax.axis_index(a) for a in ("o", "x", "c"))
+        member = xx * nc + cc
+
+        def order(first, second, at_one):
+            return jnp.where(at_one == 0, first, second), jnp.where(at_one == 0, second, first)
+
+        first, od, gu = pack_weights(
+            query_w, akey_w, avalue_w, key_weight, value_weight, down_w, out_w, gate_w, up_w
+        )
+        got = [turned(first, r) for r in range(no)]
+        od_0, gu_0 = turned(od, 0), turned(gu, 0)
+
+        times = (time_index.astype(F32) + 0.5) / TSTEPS
+        x_t = times[:, None, None] * noise + (1.0 - times)[:, None, None] * actions
+        x_in = x_t.astype(BF)
+
+        def mine_of(values):
+            v = values.reshape((nx, nc) + values.shape[1:])
+            return lax.dynamic_index_in_dim(v, cc, 1, keepdims=False)
+
+        packed = jnp.concatenate(
+            [
+                mine_of(x_in).astype(F32),
+                jnp.broadcast_to(mine_of(times)[:, None, None], (nx, 1, adim)),
+            ],
+            axis=1,
+        )
+        packed_oth = flip(packed, "i")
+        a0, a1 = order(packed[0], packed[1], xx)
+        b0, b1 = order(packed_oth[0], packed_oth[1], xx)
+        packed = jnp.stack([a0, b0, a1, b1])
+        temb = time_embed(packed[:, span, 0], expert)
+        x_g = jnp.pad(packed[:, :span], ((0, 0), (0, PAD - span), (0, 0))).astype(BF)
+        an, h0, gains, head_p = expert_in(
+            x_g.reshape(len(RELS) * PAD, adim),
+            temb,
+            action_in,
+            attn_gain,
+            mlp_gain,
+            final_gain,
+            head_w.T,
+            span,
+            expert // (no * nc),
+        )
+
+        got = [after(t, an) for t in got]
+        qa_own, kv = unpack_first(got, first.shape[1] - hd)
+        kv_all = spread(kv)
+        od_got = [od_0] + [hop(after(od_0, qa_own), partner(r)) for r in range(1, no)]
+        qa_oth = flip(qa_own, "c")
+        q_parts = queries(an, qa_own, qa_oth, heads_cols, hd ** (-0.5), span)
+        qa = exchange(q_parts)
+        gu_t = after(gu_0, q_parts[0])
+        gu_a, gu_b = hop(gu_t, partner(1)), hop(gu_t, MIDDLE)
+        kv_all = [after(t, q_parts[0]) for t in kv_all]
+        kv_oth = [flip(t, "c") for t in kv_all]
+        length = lax.dynamic_slice_in_dim(prefix_len, member, 1, 0)
+        attn = attention(
+            prefix_hidden.reshape(positions, width),
+            prefix_gain,
+            kv_all,
+            kv_oth,
+            qa,
+            length,
+            heads_cols,
+        )
+
+        attn_in = exchange(attn)
+        gu_c, gu_d = hop(after(gu_b, attn[0]), OUTWARD), hop(after(gu_a, attn[0]), MIDDLE)
+        od_all = od_got + [flip(after(t, attn[0]), "c") for t in od_got]
+        out_parts = out_project(attn_in, od_all, heads_cols)
+        out_in = exchange(out_parts)
+        gu_e = hop(after(gu_d, out_parts[0]), OUTWARD)
+        h1 = h0 + sum(t.astype(F32) for t in out_in)
+
+        mn = spread(rms(h1, gains[0]).astype(BF))
+        inner = (oo == 1) | (oo == 2)
+        gu_t, gu_a, gu_b, gu_c, gu_d, gu_e = (
+            after(t, h1) for t in (gu_t, gu_a, gu_b, gu_c, gu_d, after(gu_e, *mn))
+        )
+        gu_got = [gu_t, gu_a, jnp.where(inner, gu_d, gu_c), jnp.where(inner, gu_b, gu_e)]
+        gu_all = gu_got + [flip(t, "c") for t in gu_got]
+        ff_parts = feed_forward(mn, gu_all, od_all, units)
+        h2 = h1 + sum(t.astype(F32) for t in exchange(ff_parts))
+
+        final = rms(h2, gains[1]).astype(BF)
+        velocity = lax.dot_general(
+            final, head_p, (((1,), (1,)), ((), ())), preferred_element_type=F32
+        )
+        target = noise - actions
+        own_target = lax.dynamic_slice_in_dim(target, member, own_eps, 0)
+        velocity = velocity.reshape(own_eps, span, adim)
+        diff = velocity - own_target
+        return velocity, jnp.mean(diff * diff, axis=(1, 2))
+
+    def on_device(*values):
+        eps, positions, _ = values[0].shape
+        expert = values[8].shape[1]
+        fits = (
+            (no, ni, nx, nc) == (4, 2, 2, 2)
+            and eps == 1
+            and values[2].shape[1] <= PAD
+            and positions % 256 == 0
+            and (expert // (no * nc)) % LANES == 0
+            and values[6].shape[0] == 2 * values[10].shape[0] == 2 * values[13].shape[1]
+        )
+        if not fits:
+            return gather_all(*values)
+        return fast(*values)
+
+    return on_device
 
 
 def solution(mesh):
@@ -187,6 +691,22 @@
         P(),
     )
     out_specs = (P(("dp", "mp"), None, None), P(("dp", "mp")))
+    ndp, nmp = mesh.shape["dp"], mesh.shape["mp"]
+    sizes = (ndp // 2, 2, nmp // 2, 2)
+    fine = Mesh(mesh.devices.reshape(sizes), DP + MP)
+    names = {"dp": DP, "mp": MP}
+
+    def finer(spec):
+        flat = []
+        for entry in spec:
+            entry = (entry,) if isinstance(entry, str) else entry
+            flat.append(None if entry is None else tuple(n for e in entry for n in names[e]))
+        return P(*flat)
+
     return jax.shard_map(
-        on_device, mesh=mesh, in_specs=in_specs, out_specs=out_specs, check_vma=False
-    )
+        make(*sizes),
+        mesh=fine,
+        in_specs=tuple(finer(s) for s in in_specs),
+        out_specs=tuple(finer(s) for s in out_specs),
+        check_vma=False,
+    )

time: 405 us -> 172 us (0.42)
  the two profiles are of different devices: /device:TPU:6 before, /device:TPU:0 now
where the time goes in v1:
time: 172 us; the launch traced here: 171 us
  waiting for transfers between devices  72.1 us (42%)
  starting transfers between devices  52.8 us (31%)
  Pallas kernels  28 us (16%)
  local copies, waits for them, and re-layouts  8.11 us (5%)
  other arithmetic  5.32 us (3%)
  between operations  2.88 us (2%)
  matrix products  2.19 us (1%)
    ppermute x8, waiting for transfers between devices, hop(): return lax.ppermute(value, 'o', pairs)  33.2 us
    ppermute x18, waiting for transfers between devices, cross(): return lax.ppermute(value, ('i', 'x'), pairs)  28.9 us
    ppermute x18, starting transfers between devices, cross(): return lax.ppermute(value, ('i', 'x'), pairs)  24 us
    ppermute x8, starting transfers between devices, hop(): return lax.ppermute(value, 'o', pairs)  12.4 us
    ppermute x6, starting transfers between devices, turned(): lax.ppermute(value, ('o', 'i', 'c'), [((o * ni + i) * nc + c, ((o ^ r) *...  10.6 us
    pallas_call x1, Pallas kernels, attention(): pl.pallas_call(kernel, grid=(steps,), out_shape=[like(span, heads_cols) f...  9.49 us
    ppermute x14, waiting for transfers between devices, flip(): return lax.ppermute(value, axis, [(0, 1), (1, 0)])  6.38 us
    pallas_call x1, Pallas kernels, feed_forward(): pl.pallas_call(kernel, grid=(steps,), out_shape=row_outs(rows, count * co...  6.35 us
  transfers between devices with their start and end apart: 46, of which 17 were waited for; matrix products, arithmetic and copies ran while one was open for 5% of the time, Pallas kernels for 10%

profile of v1, /device:TPU:0, one launch (start us, length us, event | category | flops | bytes accessed | tf_op | source)
XLA Modules:
  0.0 171.4 jit_solution(18235433246936109711)
XLA Ops:
  0.6 2.4 %pack_weights.1 = (bf16[128,896]{1,0:T(8,128)(2,1)}, bf16[1536,128]{1,0:T(8,128)(2,1)}, bf16[128,2048]{1,0:T(8,128)(2,1)}) custom-call(bf16[128,512]{1,0:T(8,128)(2,1)} %q.1, bf16[128,256]{1,0:T(8,128)(2,1)} %ak.1, bf16[128,256]{1,0:T(8,128)(2,1)} %av.1, bf16[256,256]{1,0:T(8,128)(2,1)} %kw.1, bf16[256,256]{1,0:T(8,128)(2,1)} %vw.1, bf16[1024,128]{1,0:T(8,128)(2,1)} %dw.1, ...), custom_call_target="tpu_custom_call" | custom-call | tf_op jit(solution)/shard_map/pack_weights/pallas_call | solution.py:225
  3.0 5.1 %collective-permute-start.4 = (bf16[128,896]{1,0:T(8,128)(2,1)}, bf16[128,896]{1,0:T(8,128)(2,1)S(1)}, u32[]{:S(2)}, u32[]{:S(2)}) collective-permute-start(bf16[128,896]{1,0:T(8,128)(2,1)} %get-tuple-element.52), channel_id=1, source_target_pairs={{0,24},{1,28},{4,25},{5,29},{8,16},{9,20},{12,17},{13,21},{16,8},{... | collective-permute-start | bytes 688136 | tf_op jit(solution)/shard_map/ppermute | solution.py:510
  8.7 1.6 collective-permute-start.1
  12.3 3.9 %collective-permute-start = (f32[2,51,32]{1,2,0:T(8,128)S(1)}, f32[2,51,32]{1,2,0:T(8,128)S(1)}, u32[]{:S(2)}, u32[]{:S(2)}) collective-permute-start(f32[2,51,32]{1,2,0:T(8,128)S(1)} %pad_maximum_fusion.1), channel_id=1, source_target_pairs={{0,4},{4,0},{1,5},{5,1},{2,6},{6,2},{3,7},{7,3},{8,12},{12,8},{9,1... | collective-permute-start | bytes 39176 | tf_op jit(solution)/shard_map/ppermute | solution.py:495
  16.3 4.8 %collective-permute-done = f32[2,51,32]{1,2,0:T(8,128)S(1)} collective-permute-done((f32[2,51,32]{1,2,0:T(8,128)S(1)}, f32[2,51,32]{1,2,0:T(8,128)S(1)}, u32[]{:S(2)}, u32[]{:S(2)}) %collective-permute-start) | collective-permute-done | bytes 13088 | tf_op jit(solution)/shard_map/ppermute | solution.py:495
  22.8 2.2 %expert_in.1 = (bf16[256,1024]{1,0:T(8,128)(2,1)}, f32[50,1024]{1,0:T(8,128)}, f32[8,1024]{1,0:T(8,128)}, bf16[32,1024]{1,0:T(8,128)(2,1)}) custom-call(bf16[256,32]{1,0:T(8,128)(2,1)} %bitcast.19, f32[4,1024]{1,0:T(4,128)} %pad_maximum_fusion.2.te, bf16[32,1024]{1,0:T(8,128)(2,1)} %act.1, f32[1,1024]{1,0:T(1,128)} %bitcast.26, f32[1,1024]{1,0:T(1,128)} %bitcast.27, ...), custom_call_target="tpu_custom_call" | custom-call | tf_op jit(solution)/shard_map/expert_in/pallas_call | solution.py:262
  25.0 3.5 %collective-permute-done.3.refs_2_ = bf16[128,896]{1,0:T(8,128)(2,1)S(1)} collective-permute-done((bf16[128,896]{1,0:T(8,128)(2,1)}, bf16[128,896]{1,0:T(8,128)(2,1)S(1)}, u32[]{:S(2)}, u32[]{:S(2)}) %collective-permute-start.3) | collective-permute-done | bytes 229408 | tf_op jit(solution)/shard_map/ppermute | solution.py:510
  30.0 2.3 %unpack_first.1 = (bf16[512,640]{1,0:T(8,128)(2,1)}, bf16[512,256]{1,0:T(8,128)(2,1)}) custom-call(bf16[128,896]{1,0:T(8,128)(2,1)} %copy-done.23, bf16[128,896]{1,0:T(8,128)(2,1)} %copy-done.22, bf16[128,896]{1,0:T(8,128)(2,1)} %copy-done.21, bf16[128,896]{1,0:T(8,128)(2,1)} %copy-done.20), custom_call_target="tpu_custom_call" | custom-call | tf_op jit(solution)/shard_map/unpack_first/pallas_call | solution.py:293
  32.4 1.7 collective-permute-start.33
  34.1 1.6 collective-permute-start.19
  35.7 4.1 %collective-permute-start.6 = (bf16[512,256]{1,0:T(8,128)(2,1)}, bf16[512,256]{1,0:T(8,128)(2,1)S(1)}, u32[]{:S(2)}, u32[]{:S(2)}) collective-permute-start(bf16[512,256]{1,0:T(8,128)(2,1)} %get-tuple-element.61.refs_0_), channel_id=1, source_target_pairs={{0,4},{2,6},{4,0},{6,2},{1,5},{3,7},{5,1},{7,3},{8,12},{10,14},{12... | collective-permute-start | bytes 786440 | tf_op jit(solution)/shard_map/ppermute | solution.py:501
  39.8 1.5 collective-permute-start.7
  42.2 2.7 %queries.1 = (bf16[50,640]{1,0:T(8,128)(2,1)}, bf16[50,640]{1,0:T(8,128)(2,1)}, bf16[50,640]{1,0:T(8,128)(2,1)}, bf16[50,640]{1,0:T(8,128)(2,1)}) custom-call(bf16[256,1024]{1,0:T(8,128)(2,1)} %get-tuple-element.53.a, bf16[512,640]{1,0:T(8,128)(2,1)} %get-tuple-element.59.w0, bf16[512,640]{1,0:T(8,128)(2,1)} %copy-done.12), custom_call_target="tpu_custom_call" | custom-call | tf_op jit(solution)/shard_map/queries/pallas_call | solution.py:310
  44.8 14.3 %collective-permute-done.6.refs_1_ = bf16[512,256]{1,0:T(8,128)(2,1)S(1)} collective-permute-done((bf16[512,256]{1,0:T(8,128)(2,1)}, bf16[512,256]{1,0:T(8,128)(2,1)S(1)}, u32[]{:S(2)}, u32[]{:S(2)}) %collective-permute-start.6) | collective-permute-done | bytes 262176 | tf_op jit(solution)/shard_map/ppermute | solution.py:501
  60.7 1.5 collective-permute-start.14
  62.2 2.4 %collective-permute-done.13.refs_9_ = bf16[50,640]{1,0:T(8,128)(2,1)S(1)} collective-permute-done((bf16[50,640]{1,0:T(8,128)(2,1)}, bf16[50,640]{1,0:T(8,128)(2,1)S(1)}, u32[]{:S(2)}, u32[]{:S(2)}) %collective-permute-start.13) | collective-permute-done | bytes 64032 | tf_op jit(solution)/shard_map/ppermute | solution.py:501
  64.6 1.6 collective-permute-start.15
  66.2 2.5 %collective-permute-start.22 = (bf16[1536,128]{1,0:T(8,128)(2,1)S(1)}, bf16[1536,128]{1,0:T(8,128)(2,1)S(1)}, u32[]{:S(2)}, u32[]{:S(2)}) collective-permute-start(bf16[1536,128]{1,0:T(8,128)(2,1)S(1)} %collective-permute-done.19.refs_4_.refs_20_), channel_id=1, source_target_pairs={{0,24},{8,16},{16,8},{24,0},{1,25},{9,17},{17,9},{25,1},{2,26},{10... | collective-permute-start | bytes 1179656 | tf_op jit(solution)/shard_map/ppermute | solution.py:522
  68.6 1.4 collective-permute-done.15.refs_11_
  70.0 2.8 %collective-permute-start.21 = (bf16[1536,128]{1,0:T(8,128)(2,1)S(1)}, bf16[1536,128]{1,0:T(8,128)(2,1)S(1)}, u32[]{:S(2)}, u32[]{:S(2)}) collective-permute-start(bf16[1536,128]{1,0:T(8,128)(2,1)S(1)} %collective-permute-done.19.refs_4_.refs_20_), channel_id=1, source_target_pairs={{0,16},{8,24},{16,0},{24,8},{1,17},{9,25},{17,1},{25,9},{2,18},{10... | collective-permute-start | bytes 1179656 | tf_op jit(solution)/shard_map/ppermute | solution.py:522
  73.5 1.4 collective-permute-start.20
  75.6 1.2 dynamic_slice.16.len_ref
  77.3 9.5 %prefix_attention.1 = (bf16[50,512]{1,0:T(8,128)(2,1)}, bf16[50,512]{1,0:T(8,128)(2,1)}, bf16[50,512]{1,0:T(8,128)(2,1)}, bf16[50,512]{1,0:T(8,128)(2,1)}) custom-call(s32[1]{0:T(128)} %dynamic_slice.16.len_ref, bf16[1024,2048]{1,0:T(8,128)(2,1)} %bitcast.18, f32[1,2048]{1,0:T(1,128)} %bitcast.25, bf16[512,256]{1,0:T(8,128)(2,1)} %get-tuple-element.61.refs_0_, ...), custom_call_target="tpu_custom_call" | custom-call | tf_op jit(solution)/shard_map/prefix_attention/pallas_call | solution.py:389
  87.2 1.5 collective-permute-start.17
  88.7 14.3 %collective-permute-done.21.refs_6_.refs_22_ = bf16[1536,128]{1,0:T(8,128)(2,1)S(1)} collective-permute-done((bf16[1536,128]{1,0:T(8,128)(2,1)S(1)}, bf16[1536,128]{1,0:T(8,128)(2,1)S(1)}, u32[]{:S(2)}, u32[]{:S(2)}) %collective-permute-start.21) | collective-permute-done | bytes 393248 | tf_op jit(solution)/shard_map/ppermute | solution.py:522
  103.0 1.9 %collective-permute-start.18 = (bf16[50,512]{1,0:T(8,128)(2,1)}, bf16[50,512]{1,0:T(8,128)(2,1)S(1)}, u32[]{:S(2)}, u32[]{:S(2)}) collective-permute-start(bf16[50,512]{1,0:T(8,128)(2,1)} %get-tuple-element.71), channel_id=1, source_target_pairs={{0,6},{2,4},{4,2},{6,0},{1,7},{3,5},{5,3},{7,1},{8,14},{10,12},{12... | collective-permute-start | bytes 153608 | tf_op jit(solution)/shard_map/ppermute | solution.py:501
  106.4 1.9 %collective-permute-done.18.refs_3_ = bf16[50,512]{1,0:T(8,128)(2,1)S(1)} collective-permute-done((bf16[50,512]{1,0:T(8,128)(2,1)}, bf16[50,512]{1,0:T(8,128)(2,1)S(1)}, u32[]{:S(2)}, u32[]{:S(2)}) %collective-permute-start.18) | collective-permute-done | bytes 51232 | tf_op jit(solution)/shard_map/ppermute | solution.py:501
  108.3 1.5 collective-permute-start.36
  109.8 1.5 collective-permute-start.35
  111.4 2.6 %out_project.1 = (f32[50,1024]{1,0:T(8,128)}, bf16[50,1024]{1,0:T(8,128)(2,1)}, bf16[50,1024]{1,0:T(8,128)(2,1)}, bf16[50,1024]{1,0:T(8,128)(2,1)}) custom-call(bf16[50,512]{1,0:T(8,128)(2,1)} %get-tuple-element.68.refs_0_, bf16[50,512]{1,0:T(8,128)(2,1)} %copy-done.31, bf16[50,512]{1,0:T(8,128)(2,1)} %copy-done.32, bf16[50,512]{1,0:T(8,128)(2,1)} %copy-done.33, ...), custom_call_target="tpu_custom_call" | custom-call | tf_op jit(solution)/shard_map/out_project/pallas_call | solution.py:431
  114.0 2.0 %collective-permute-start.27 = (bf16[50,1024]{1,0:T(8,128)(2,1)}, bf16[50,1024]{1,0:T(8,128)(2,1)S(1)}, u32[]{:S(2)}, u32[]{:S(2)}) collective-permute-start(bf16[50,1024]{1,0:T(8,128)(2,1)} %get-tuple-element.79), channel_id=1, source_target_pairs={{0,4},{2,6},{4,0},{6,2},{1,5},{3,7},{5,1},{7,3},{8,12},{10,14},{12... | collective-permute-start | bytes 307208 | tf_op jit(solution)/shard_map/ppermute | solution.py:501
  117.4 1.4 fusion.12
  118.9 1.3 collective-permute-start.37
  120.2 2.0 %collective-permute-done.28 = bf16[50,1024]{1,0:T(8,128)(2,1)S(1)} collective-permute-done((bf16[50,1024]{1,0:T(8,128)(2,1)}, bf16[50,1024]{1,0:T(8,128)(2,1)S(1)}, u32[]{:S(2)}, u32[]{:S(2)}) %collective-permute-start.28) | collective-permute-done | bytes 102432 | tf_op jit(solution)/shard_map/ppermute | solution.py:501
  122.1 1.5 collective-permute-done.29
  123.6 1.2 multiply_reduce_fusion.1
  124.9 1.3 collective-permute-start.38
  126.3 1.7 %collective-permute-start.32 = (bf16[50,1024]{1,0:T(8,128)(2,1)S(1)}, bf16[50,1024]{1,0:T(8,128)(2,1)S(1)}, u32[]{:S(2)}, u32[]{:S(2)}) collective-permute-start(bf16[50,1024]{1,0:T(8,128)(2,1)S(1)} %multiply_convert_fusion.1.refs_0_), channel_id=1, source_target_pairs={{0,6},{2,4},{4,2},{6,0},{1,7},{3,5},{5,3},{7,1},{8,14},{10,12},{12... | collective-permute-start | bytes 307208 | tf_op jit(solution)/shard_map/ppermute | solution.py:501
  128.0 1.5 collective-permute-start.31
  129.8 7.5 %collective-permute-done.37 = bf16[128,2048]{1,0:T(8,128)(2,1)S(1)} collective-permute-done((bf16[128,2048]{1,0:T(8,128)(2,1)}, bf16[128,2048]{1,0:T(8,128)(2,1)S(1)}, u32[]{:S(2)}, u32[]{:S(2)}) %collective-permute-start.37) | collective-permute-done | bytes 524320 | tf_op jit(solution)/shard_map/ppermute | solution.py:522
  138.1 10.5 %collective-permute-done.38 = bf16[128,2048]{1,0:T(8,128)(2,1)S(1)} collective-permute-done((bf16[128,2048]{1,0:T(8,128)(2,1)}, bf16[128,2048]{1,0:T(8,128)(2,1)S(1)}, u32[]{:S(2)}, u32[]{:S(2)}) %collective-permute-start.38) | collective-permute-done | bytes 524320 | tf_op jit(solution)/shard_map/ppermute | solution.py:522
  150.8 6.3 %feed_forward.1 = (f32[50,1024]{1,0:T(8,128)}, bf16[50,1024]{1,0:T(8,128)(2,1)}, bf16[50,1024]{1,0:T(8,128)(2,1)}, bf16[50,1024]{1,0:T(8,128)(2,1)}) custom-call(bf16[50,1024]{1,0:T(8,128)(2,1)} %copy-done.13, bf16[50,1024]{1,0:T(8,128)(2,1)} %copy-done.26, bf16[50,1024]{1,0:T(8,128)(2,1)} %copy-done.25, bf16[50,1024]{1,0:T(8,128)(2,1)} %copy-done.24, ...), custom_call_target="tpu_custom_call" | custom-call | tf_op jit(solution)/shard_map/feed_forward/pallas_call | solution.py:476
  157.2 1.3 collective-permute-start.43
  159.1 1.7 collective-permute-start.45
  160.7 1.9 %collective-permute-done.43 = bf16[50,1024]{1,0:T(8,128)(2,1)S(1)} collective-permute-done((bf16[50,1024]{1,0:T(8,128)(2,1)}, bf16[50,1024]{1,0:T(8,128)(2,1)S(1)}, u32[]{:S(2)}, u32[]{:S(2)}) %collective-permute-start.43) | collective-permute-done | bytes 102432 | tf_op jit(solution)/shard_map/ppermute | solution.py:501
  162.6 2.1 %collective-permute-done.44 = bf16[50,1024]{1,0:T(8,128)(2,1)S(1)} collective-permute-done((bf16[50,1024]{1,0:T(8,128)(2,1)}, bf16[50,1024]{1,0:T(8,128)(2,1)S(1)}, u32[]{:S(2)}, u32[]{:S(2)}) %collective-permute-start.44) | collective-permute-done | bytes 102432 | tf_op jit(solution)/shard_map/ppermute | solution.py:501
  164.7 1.5 collective-permute-done.45
  167.4 2.2 %fusion.6 = (f32[]{:T(128)}, f32[1,50,32]{1,2,0:T(8,128)}) fusion(f32[4,50,32]{1,2,0:T(8,128)} %param.22, s32[]{:T(128)S(6)} %select_n.52, f32[4,50,32]{1,2,0:T(8,128)} %param.23, bf16[32,1024]{1,0:T(8,128)(2,1)S(1)} %copy-done.30, f32[50,1024]{1,0:T(8,128)S(1)} %get-tuple-element.101, f32[1024]{0:T(1024)} %bitcast.23, f32[50]{0:T(128)S(1)} %add_rsqrt_fusion), kind=kOutput, calls=%fused_computation.24 | convolution fusion | flops 3436799 | bytes 293840 | tf_op jit(solution)/shard_map/dot_general | solution.py:643
  (145 shorter events, 18.5 us)
Async XLA Ops:
  3.0 22.0 %collective-permute-start.4 = (bf16[128,896]{1,0:T(8,128)(2,1)}, bf16[128,896]{1,0:T(8,128)(2,1)S(1)}, u32[]{:S(2)}, u32[]{:S(2)}) collective-permute-start(bf16[128,896]{1,0:T(8,128)(2,1)} %get-tuple-element.52), channel_id=1, source_target_pairs={{0,24},{1,28},{4,25},{5,29},{8,16},{9,20},{12,17},{13,21},{16,8},{... | collective-permute-start | bytes 688136 | tf_op jit(solution)/shard_map/ppermute | solution.py:510
  8.1 20.5 %collective-permute-start.3 = (bf16[128,896]{1,0:T(8,128)(2,1)}, bf16[128,896]{1,0:T(8,128)(2,1)S(1)}, u32[]{:S(2)}, u32[]{:S(2)}) collective-permute-start(bf16[128,896]{1,0:T(8,128)(2,1)} %get-tuple-element.52), channel_id=1, source_target_pairs={{0,16},{1,20},{4,17},{5,21},{8,24},{9,28},{12,25},{13,29},{16,0},{... | collective-permute-start | bytes 688136 | tf_op jit(solution)/shard_map/ppermute | solution.py:510
  8.1 20.5 %collective-permute-start.2 = (bf16[128,896]{1,0:T(8,128)(2,1)}, bf16[128,896]{1,0:T(8,128)(2,1)S(1)}, u32[]{:S(2)}, u32[]{:S(2)}) collective-permute-start(bf16[128,896]{1,0:T(8,128)(2,1)} %get-tuple-element.52), channel_id=1, source_target_pairs={{0,8},{1,12},{4,9},{5,13},{8,0},{9,4},{12,1},{13,5},{16,24},{17,28... | collective-permute-start | bytes 688136 | tf_op jit(solution)/shard_map/ppermute | solution.py:510
  8.7 19.9 %collective-permute-start.1 = (bf16[128,896]{1,0:T(8,128)(2,1)}, bf16[128,896]{1,0:T(8,128)(2,1)S(1)}, u32[]{:S(2)}, u32[]{:S(2)}) collective-permute-start(bf16[128,896]{1,0:T(8,128)(2,1)} %get-tuple-element.52), channel_id=1, source_target_pairs={{0,0},{1,4},{4,1},{5,5},{8,8},{9,12},{12,9},{13,13},{16,16},{17,20... | collective-permute-start | bytes 688136 | tf_op jit(solution)/shard_map/ppermute | solution.py:510
  12.3 8.8 %collective-permute-start = (f32[2,51,32]{1,2,0:T(8,128)S(1)}, f32[2,51,32]{1,2,0:T(8,128)S(1)}, u32[]{:S(2)}, u32[]{:S(2)}) collective-permute-start(f32[2,51,32]{1,2,0:T(8,128)S(1)} %pad_maximum_fusion.1), channel_id=1, source_target_pairs={{0,4},{4,0},{1,5},{5,1},{2,6},{6,2},{3,7},{7,3},{8,12},{12,8},{9,1... | collective-permute-start | bytes 39176 | tf_op jit(solution)/shard_map/ppermute | solution.py:495
  32.3 9.0 %collective-permute-start.5 = (bf16[512,640]{1,0:T(8,128)(2,1)}, bf16[512,640]{1,0:T(8,128)(2,1)S(1)}, u32[]{:S(2)}, u32[]{:S(2)}) collective-permute-start(bf16[512,640]{1,0:T(8,128)(2,1)} %get-tuple-element.59.w0), channel_id=1, source_target_pairs={{0,1},{1,0},{2,3},{3,2},{4,5},{5,4},{6,7},{7,6},{8,9},{9,8},{10,11... | collective-permute-start | bytes 1966088 | tf_op jit(solution)/shard_map/ppermute | solution.py:495
  32.4 28.3 %collective-permute-start.33 = (bf16[128,2048]{1,0:T(8,128)(2,1)}, bf16[128,2048]{1,0:T(8,128)(2,1)S(1)}, u32[]{:S(2)}, u32[]{:S(2)}) collective-permute-start(bf16[128,2048]{1,0:T(8,128)(2,1)} %get-tuple-element.83), channel_id=1, source_target_pairs={{0,0},{1,4},{4,1},{5,5},{8,8},{9,12},{12,9},{13,13},{16,16},{17,20... | collective-permute-start | bytes 1572872 | tf_op jit(solution)/shard_map/ppermute | solution.py:510
  34.1 25.6 %collective-permute-start.19 = (bf16[1536,128]{1,0:T(8,128)(2,1)}, bf16[1536,128]{1,0:T(8,128)(2,1)S(1)}, u32[]{:S(2)}, u32[]{:S(2)}) collective-permute-start(bf16[1536,128]{1,0:T(8,128)(2,1)} %get-tuple-element.72), channel_id=1, source_target_pairs={{0,0},{1,4},{4,1},{5,5},{8,8},{9,12},{12,9},{13,13},{16,16},{17,20... | collective-permute-start | bytes 1179656 | tf_op jit(solution)/shard_map/ppermute | solution.py:510
  35.7 23.5 %collective-permute-start.6 = (bf16[512,256]{1,0:T(8,128)(2,1)}, bf16[512,256]{1,0:T(8,128)(2,1)S(1)}, u32[]{:S(2)}, u32[]{:S(2)}) collective-permute-start(bf16[512,256]{1,0:T(8,128)(2,1)} %get-tuple-element.61.refs_0_), channel_id=1, source_target_pairs={{0,4},{2,6},{4,0},{6,2},{1,5},{3,7},{5,1},{7,3},{8,12},{10,14},{12... | collective-permute-start | bytes 786440 | tf_op jit(solution)/shard_map/ppermute | solution.py:501
  39.8 19.4 %collective-permute-start.7 = (bf16[512,256]{1,0:T(8,128)(2,1)}, bf16[512,256]{1,0:T(8,128)(2,1)S(1)}, u32[]{:S(2)}, u32[]{:S(2)}) collective-permute-start(bf16[512,256]{1,0:T(8,128)(2,1)} %get-tuple-element.61.refs_0_), channel_id=1, source_target_pairs={{0,2},{2,0},{4,6},{6,4},{1,3},{3,1},{5,7},{7,5},{8,10},{10,8},{12,... | collective-permute-start | bytes 786440 | tf_op jit(solution)/shard_map/ppermute | solution.py:501
  41.3 18.5 %collective-permute-start.8 = (bf16[512,256]{1,0:T(8,128)(2,1)}, bf16[512,256]{1,0:T(8,128)(2,1)S(1)}, u32[]{:S(2)}, u32[]{:S(2)}) collective-permute-start(bf16[512,256]{1,0:T(8,128)(2,1)} %get-tuple-element.61.refs_0_), channel_id=1, source_target_pairs={{0,6},{2,4},{4,2},{6,0},{1,7},{3,5},{5,3},{7,1},{8,14},{10,12},{12... | collective-permute-start | bytes 786440 | tf_op jit(solution)/shard_map/ppermute | solution.py:501
  59.2 13.6 %collective-permute-start.9 = (bf16[512,256]{1,0:T(8,128)(2,1)}, bf16[512,256]{1,0:T(8,128)(2,1)S(1)}, u32[]{:S(2)}, u32[]{:S(2)}) collective-permute-start(bf16[512,256]{1,0:T(8,128)(2,1)} %get-tuple-element.61.refs_0_), channel_id=1, source_target_pairs={{0,1},{1,0},{2,3},{3,2},{4,5},{5,4},{6,7},{7,6},{8,9},{9,8},{10,11... | collective-permute-start | bytes 786440 | tf_op jit(solution)/shard_map/ppermute | solution.py:495
  59.2 14.3 %collective-permute-start.10 = (bf16[512,256]{1,0:T(8,128)(2,1)S(1)}, bf16[512,256]{1,0:T(8,128)(2,1)S(1)}, u32[]{:S(2)}, u32[]{:S(2)}) collective-permute-start(bf16[512,256]{1,0:T(8,128)(2,1)S(1)} %collective-permute-done.6.refs_1_), channel_id=1, source_target_pairs={{0,1},{1,0},{2,3},{3,2},{4,5},{5,4},{6,7},{7,6},{8,9},{9,8},{10,11... | collective-permute-start | bytes 786440 | tf_op jit(solution)/shard_map/ppermute | solution.py:495
  59.7 51.6 %copy-start.7 = (bf16[1536,128]{1,0:T(8,128)(2,1)}, bf16[1536,128]{1,0:T(8,128)(2,1)S(1)}, u32[]{:S(2)}) copy-start(bf16[1536,128]{1,0:T(8,128)(2,1)S(1)} %collective-permute-done.19.refs_4_.refs_20_) | copy-start | bytes 1179652
  59.7 15.2 %collective-permute-start.11 = (bf16[512,256]{1,0:T(8,128)(2,1)S(1)}, bf16[512,256]{1,0:T(8,128)(2,1)S(1)}, u32[]{:S(2)}, u32[]{:S(2)}) collective-permute-start(bf16[512,256]{1,0:T(8,128)(2,1)S(1)} %collective-permute-done.7.refs_2_), channel_id=1, source_target_pairs={{0,1},{1,0},{2,3},{3,2},{4,5},{5,4},{6,7},{7,6},{8,9},{9,8},{10,11... | collective-permute-start | bytes 786440 | tf_op jit(solution)/shard_map/ppermute | solution.py:495
  59.8 4.8 %collective-permute-start.13 = (bf16[50,640]{1,0:T(8,128)(2,1)}, bf16[50,640]{1,0:T(8,128)(2,1)S(1)}, u32[]{:S(2)}, u32[]{:S(2)}) collective-permute-start(bf16[50,640]{1,0:T(8,128)(2,1)} %get-tuple-element.65), channel_id=1, source_target_pairs={{0,4},{2,6},{4,0},{6,2},{1,5},{3,7},{5,1},{7,3},{8,12},{10,14},{12... | collective-permute-start | bytes 192008 | tf_op jit(solution)/shard_map/ppermute | solution.py:501
  60.7 76.7 %copy-start.2 = (bf16[128,2048]{1,0:T(8,128)(2,1)}, bf16[128,2048]{1,0:T(8,128)(2,1)S(1)}, u32[]{:S(2)}) copy-start(bf16[128,2048]{1,0:T(8,128)(2,1)S(1)} %collective-permute-done.33.refs_4_.refs_12_) | copy-start | bytes 1572868
  60.7 5.5 %collective-permute-start.14 = (bf16[50,640]{1,0:T(8,128)(2,1)}, bf16[50,640]{1,0:T(8,128)(2,1)S(1)}, u32[]{:S(2)}, u32[]{:S(2)}) collective-permute-start(bf16[50,640]{1,0:T(8,128)(2,1)} %get-tuple-element.66), channel_id=1, source_target_pairs={{0,2},{2,0},{4,6},{6,4},{1,3},{3,1},{5,7},{7,5},{8,10},{10,8},{12,... | collective-permute-start | bytes 192008 | tf_op jit(solution)/shard_map/ppermute | solution.py:501
  64.6 5.4 %collective-permute-start.15 = (bf16[50,640]{1,0:T(8,128)(2,1)}, bf16[50,640]{1,0:T(8,128)(2,1)S(1)}, u32[]{:S(2)}, u32[]{:S(2)}) collective-permute-start(bf16[50,640]{1,0:T(8,128)(2,1)} %get-tuple-element.67), channel_id=1, source_target_pairs={{0,6},{2,4},{4,2},{6,0},{1,7},{3,5},{5,3},{7,1},{8,14},{10,12},{12... | collective-permute-start | bytes 192008 | tf_op jit(solution)/shard_map/ppermute | solution.py:501
  66.2 21.0 %collective-permute-start.22 = (bf16[1536,128]{1,0:T(8,128)(2,1)S(1)}, bf16[1536,128]{1,0:T(8,128)(2,1)S(1)}, u32[]{:S(2)}, u32[]{:S(2)}) collective-permute-start(bf16[1536,128]{1,0:T(8,128)(2,1)S(1)} %collective-permute-done.19.refs_4_.refs_20_), channel_id=1, source_target_pairs={{0,24},{8,16},{16,8},{24,0},{1,25},{9,17},{17,9},{25,1},{2,26},{10... | collective-permute-start | bytes 1179656 | tf_op jit(solution)/shard_map/ppermute | solution.py:522
  70.0 33.0 %collective-permute-start.21 = (bf16[1536,128]{1,0:T(8,128)(2,1)S(1)}, bf16[1536,128]{1,0:T(8,128)(2,1)S(1)}, u32[]{:S(2)}, u32[]{:S(2)}) collective-permute-start(bf16[1536,128]{1,0:T(8,128)(2,1)S(1)} %collective-permute-done.19.refs_4_.refs_20_), channel_id=1, source_target_pairs={{0,16},{8,24},{16,0},{24,8},{1,17},{9,25},{17,1},{25,9},{2,18},{10... | collective-permute-start | bytes 1179656 | tf_op jit(solution)/shard_map/ppermute | solution.py:522
  72.8 35.5 %collective-permute-start.34 = (bf16[128,2048]{1,0:T(8,128)(2,1)S(1)}, bf16[128,2048]{1,0:T(8,128)(2,1)S(1)}, u32[]{:S(2)}, u32[]{:S(2)}) collective-permute-start(bf16[128,2048]{1,0:T(8,128)(2,1)S(1)} %collective-permute-done.33.refs_4_.refs_12_), channel_id=1, source_target_pairs={{0,8},{8,0},{16,24},{24,16},{1,9},{9,1},{17,25},{25,17},{2,10},{10... | collective-permute-start | bytes 1572872 | tf_op jit(solution)/shard_map/ppermute | solution.py:522
  73.5 32.3 %collective-permute-start.20 = (bf16[1536,128]{1,0:T(8,128)(2,1)S(1)}, bf16[1536,128]{1,0:T(8,128)(2,1)S(1)}, u32[]{:S(2)}, u32[]{:S(2)}) collective-permute-start(bf16[1536,128]{1,0:T(8,128)(2,1)S(1)} %collective-permute-done.19.refs_4_.refs_20_), channel_id=1, source_target_pairs={{0,8},{8,0},{16,24},{24,16},{1,9},{9,1},{17,25},{25,17},{2,10},{10... | collective-permute-start | bytes 1179656 | tf_op jit(solution)/shard_map/ppermute | solution.py:522
  75.6 1.7 collective-permute-start.12
  86.8 19.0 %collective-permute-start.16 = (bf16[50,512]{1,0:T(8,128)(2,1)}, bf16[50,512]{1,0:T(8,128)(2,1)S(1)}, u32[]{:S(2)}, u32[]{:S(2)}) collective-permute-start(bf16[50,512]{1,0:T(8,128)(2,1)} %get-tuple-element.69), channel_id=1, source_target_pairs={{0,4},{2,6},{4,0},{6,2},{1,5},{3,7},{5,1},{7,3},{8,12},{10,14},{12... | collective-permute-start | bytes 153608 | tf_op jit(solution)/shard_map/ppermute | solution.py:501
  87.2 19.2 %collective-permute-start.17 = (bf16[50,512]{1,0:T(8,128)(2,1)}, bf16[50,512]{1,0:T(8,128)(2,1)S(1)}, u32[]{:S(2)}, u32[]{:S(2)}) collective-permute-start(bf16[50,512]{1,0:T(8,128)(2,1)} %get-tuple-element.70), channel_id=1, source_target_pairs={{0,2},{2,0},{4,6},{6,4},{1,3},{3,1},{5,7},{7,5},{8,10},{10,8},{12,... | collective-permute-start | bytes 153608 | tf_op jit(solution)/shard_map/ppermute | solution.py:501
  103.0 5.3 %collective-permute-start.18 = (bf16[50,512]{1,0:T(8,128)(2,1)}, bf16[50,512]{1,0:T(8,128)(2,1)S(1)}, u32[]{:S(2)}, u32[]{:S(2)}) collective-permute-start(bf16[50,512]{1,0:T(8,128)(2,1)} %get-tuple-element.71), channel_id=1, source_target_pairs={{0,6},{2,4},{4,2},{6,0},{1,7},{3,5},{5,3},{7,1},{8,14},{10,12},{12... | collective-permute-start | bytes 153608 | tf_op jit(solution)/shard_map/ppermute | solution.py:501
  105.8 4.0 %collective-permute-start.23 = (bf16[1536,128]{1,0:T(8,128)(2,1)S(1)}, bf16[1536,128]{1,0:T(8,128)(2,1)S(1)}, u32[]{:S(2)}, u32[]{:S(2)}) collective-permute-start(bf16[1536,128]{1,0:T(8,128)(2,1)S(1)} %collective-permute-done.19.refs_4_.refs_20_), channel_id=1, source_target_pairs={{0,1},{1,0},{2,3},{3,2},{4,5},{5,4},{6,7},{7,6},{8,9},{9,8},{10,11... | collective-permute-start | bytes 1179656 | tf_op jit(solution)/shard_map/ppermute | solution.py:495
  105.8 5.4 %collective-permute-start.24 = (bf16[1536,128]{1,0:T(8,128)(2,1)S(1)}, bf16[1536,128]{1,0:T(8,128)(2,1)}, u32[]{:S(2)}, u32[]{:S(2)}) collective-permute-start(bf16[1536,128]{1,0:T(8,128)(2,1)S(1)} %collective-permute-done.20.refs_5_.refs_21_), channel_id=1, source_target_pairs={{0,1},{1,0},{2,3},{3,2},{4,5},{5,4},{6,7},{7,6},{8,9},{9,8},{10,11... | collective-permute-start | bytes 1179656 | tf_op jit(solution)/shard_map/ppermute | solution.py:495
  106.4 4.9 %collective-permute-start.25 = (bf16[1536,128]{1,0:T(8,128)(2,1)S(1)}, bf16[1536,128]{1,0:T(8,128)(2,1)}, u32[]{:S(2)}, u32[]{:S(2)}) collective-permute-start(bf16[1536,128]{1,0:T(8,128)(2,1)S(1)} %collective-permute-done.21.refs_6_.refs_22_), channel_id=1, source_target_pairs={{0,1},{1,0},{2,3},{3,2},{4,5},{5,4},{6,7},{7,6},{8,9},{9,8},{10,11... | collective-permute-start | bytes 1179656 | tf_op jit(solution)/shard_map/ppermute | solution.py:495
  108.3 3.0 %collective-permute-start.26 = (bf16[1536,128]{1,0:T(8,128)(2,1)S(1)}, bf16[1536,128]{1,0:T(8,128)(2,1)}, u32[]{:S(2)}, u32[]{:S(2)}) collective-permute-start(bf16[1536,128]{1,0:T(8,128)(2,1)S(1)} %collective-permute-done.22.refs_7_.refs_23_), channel_id=1, source_target_pairs={{0,1},{1,0},{2,3},{3,2},{4,5},{5,4},{6,7},{7,6},{8,9},{9,8},{10,11... | collective-permute-start | bytes 1179656 | tf_op jit(solution)/shard_map/ppermute | solution.py:495
  108.3 10.5 %collective-permute-start.36 = (bf16[128,2048]{1,0:T(8,128)(2,1)S(1)}, bf16[128,2048]{1,0:T(8,128)(2,1)}, u32[]{:S(2)}, u32[]{:S(2)}) collective-permute-start(bf16[128,2048]{1,0:T(8,128)(2,1)S(1)} %collective-permute-done.33.refs_4_.refs_12_), channel_id=1, source_target_pairs={{8,16},{16,8},{9,17},{17,9},{10,18},{18,10},{11,19},{19,11},{12,20... | collective-permute-start | bytes 1572872 | tf_op jit(solution)/shard_map/ppermute | solution.py:522
  109.8 15.1 %collective-permute-start.35 = (bf16[128,2048]{1,0:T(8,128)(2,1)S(1)}, bf16[128,2048]{1,0:T(8,128)(2,1)}, u32[]{:S(2)}, u32[]{:S(2)}) collective-permute-start(bf16[128,2048]{1,0:T(8,128)(2,1)S(1)} %collective-permute-done.34.refs_5_.refs_13_), channel_id=1, source_target_pairs={{8,16},{16,8},{9,17},{17,9},{10,18},{18,10},{11,19},{19,11},{12,20... | collective-permute-start | bytes 1572872 | tf_op jit(solution)/shard_map/ppermute | solution.py:522
  114.0 6.2 %collective-permute-start.27 = (bf16[50,1024]{1,0:T(8,128)(2,1)}, bf16[50,1024]{1,0:T(8,128)(2,1)S(1)}, u32[]{:S(2)}, u32[]{:S(2)}) collective-permute-start(bf16[50,1024]{1,0:T(8,128)(2,1)} %get-tuple-element.79), channel_id=1, source_target_pairs={{0,4},{2,6},{4,0},{6,2},{1,5},{3,7},{5,1},{7,3},{8,12},{10,14},{12... | collective-permute-start | bytes 307208 | tf_op jit(solution)/shard_map/ppermute | solution.py:501
  115.9 6.2 %collective-permute-start.28 = (bf16[50,1024]{1,0:T(8,128)(2,1)}, bf16[50,1024]{1,0:T(8,128)(2,1)S(1)}, u32[]{:S(2)}, u32[]{:S(2)}) collective-permute-start(bf16[50,1024]{1,0:T(8,128)(2,1)} %get-tuple-element.80), channel_id=1, source_target_pairs={{0,2},{2,0},{4,6},{6,4},{1,3},{3,1},{5,7},{7,5},{8,10},{10,8},{12,... | collective-permute-start | bytes 307208 | tf_op jit(solution)/shard_map/ppermute | solution.py:501
  116.5 7.2 %collective-permute-start.29 = (bf16[50,1024]{1,0:T(8,128)(2,1)}, bf16[50,1024]{1,0:T(8,128)(2,1)S(1)}, u32[]{:S(2)}, u32[]{:S(2)}) collective-permute-start(bf16[50,1024]{1,0:T(8,128)(2,1)} %get-tuple-element.81), channel_id=1, source_target_pairs={{0,6},{2,4},{4,2},{6,0},{1,7},{3,5},{5,3},{7,1},{8,14},{10,12},{12... | collective-permute-start | bytes 307208 | tf_op jit(solution)/shard_map/ppermute | solution.py:501
  118.9 18.5 %collective-permute-start.37 = (bf16[128,2048]{1,0:T(8,128)(2,1)}, bf16[128,2048]{1,0:T(8,128)(2,1)S(1)}, u32[]{:S(2)}, u32[]{:S(2)}) collective-permute-start(bf16[128,2048]{1,0:T(8,128)(2,1)} %collective-permute-done.36), channel_id=1, source_target_pairs={{8,0},{16,24},{9,1},{17,25},{10,2},{18,26},{11,3},{19,27},{12,4},{... | collective-permute-start | bytes 1572872 | tf_op jit(solution)/shard_map/ppermute | solution.py:522
  124.9 23.7 %collective-permute-start.38 = (bf16[128,2048]{1,0:T(8,128)(2,1)}, bf16[128,2048]{1,0:T(8,128)(2,1)S(1)}, u32[]{:S(2)}, u32[]{:S(2)}) collective-permute-start(bf16[128,2048]{1,0:T(8,128)(2,1)} %collective-permute-done.35), channel_id=1, source_target_pairs={{8,0},{16,24},{9,1},{17,25},{10,2},{18,26},{11,3},{19,27},{12,4},{... | collective-permute-start | bytes 1572872 | tf_op jit(solution)/shard_map/ppermute | solution.py:522
  126.3 11.2 %collective-permute-start.32 = (bf16[50,1024]{1,0:T(8,128)(2,1)S(1)}, bf16[50,1024]{1,0:T(8,128)(2,1)S(1)}, u32[]{:S(2)}, u32[]{:S(2)}) collective-permute-start(bf16[50,1024]{1,0:T(8,128)(2,1)S(1)} %multiply_convert_fusion.1.refs_0_), channel_id=1, source_target_pairs={{0,6},{2,4},{4,2},{6,0},{1,7},{3,5},{5,3},{7,1},{8,14},{10,12},{12... | collective-permute-start | bytes 307208 | tf_op jit(solution)/shard_map/ppermute | solution.py:501
  128.0 10.0 %collective-permute-start.31 = (bf16[50,1024]{1,0:T(8,128)(2,1)S(1)}, bf16[50,1024]{1,0:T(8,128)(2,1)S(1)}, u32[]{:S(2)}, u32[]{:S(2)}) collective-permute-start(bf16[50,1024]{1,0:T(8,128)(2,1)S(1)} %multiply_convert_fusion.1.refs_0_), channel_id=1, source_target_pairs={{0,2},{2,0},{4,6},{6,4},{1,3},{3,1},{5,7},{7,5},{8,10},{10,8},{12,... | collective-permute-start | bytes 307208 | tf_op jit(solution)/shard_map/ppermute | solution.py:501
  129.5 8.6 %collective-permute-start.30 = (bf16[50,1024]{1,0:T(8,128)(2,1)S(1)}, bf16[50,1024]{1,0:T(8,128)(2,1)S(1)}, u32[]{:S(2)}, u32[]{:S(2)}) collective-permute-start(bf16[50,1024]{1,0:T(8,128)(2,1)S(1)} %multiply_convert_fusion.1.refs_0_), channel_id=1, source_target_pairs={{0,4},{2,6},{4,0},{6,2},{1,5},{3,7},{5,1},{7,3},{8,12},{10,14},{12... | collective-permute-start | bytes 307208 | tf_op jit(solution)/shard_map/ppermute | solution.py:501
  137.4 11.4 %collective-permute-start.39 = (bf16[128,2048]{1,0:T(8,128)(2,1)S(1)}, bf16[128,2048]{1,0:T(8,128)(2,1)S(1)}, u32[]{:S(2)}, u32[]{:S(2)}) collective-permute-start(bf16[128,2048]{1,0:T(8,128)(2,1)S(1)} %collective-permute-done.33.refs_4_.refs_12_), channel_id=1, source_target_pairs={{0,1},{1,0},{2,3},{3,2},{4,5},{5,4},{6,7},{7,6},{8,9},{9,8},{10,11... | collective-permute-start | bytes 1572872 | tf_op jit(solution)/shard_map/ppermute | solution.py:495
  137.5 11.3 %collective-permute-start.40 = (bf16[128,2048]{1,0:T(8,128)(2,1)S(1)}, bf16[128,2048]{1,0:T(8,128)(2,1)S(1)}, u32[]{:S(2)}, u32[]{:S(2)}) collective-permute-start(bf16[128,2048]{1,0:T(8,128)(2,1)S(1)} %collective-permute-done.34.refs_5_.refs_13_), channel_id=1, source_target_pairs={{0,1},{1,0},{2,3},{3,2},{4,5},{5,4},{6,7},{7,6},{8,9},{9,8},{10,11... | collective-permute-start | bytes 1572872 | tf_op jit(solution)/shard_map/ppermute | solution.py:495
  138.0 10.8 %collective-permute-start.41 = (bf16[128,2048]{1,0:T(8,128)(2,1)S(1)}, bf16[128,2048]{1,0:T(8,128)(2,1)S(1)}, u32[]{:S(2)}, u32[]{:S(2)}) collective-permute-start(bf16[128,2048]{1,0:T(8,128)(2,1)S(1)} %broadcast_select_fusion.1.refs_6_.refs_14_), channel_id=1, source_target_pairs={{0,1},{1,0},{2,3},{3,2},{4,5},{5,4},{6,7},{7,6},{8,9},{9,8},{10,11... | collective-permute-start | bytes 1572872 | tf_op jit(solution)/shard_map/ppermute | solution.py:495
  148.7 2.1 %collective-permute-start.42 = (bf16[128,2048]{1,0:T(8,128)(2,1)S(1)}, bf16[128,2048]{1,0:T(8,128)(2,1)}, u32[]{:S(2)}, u32[]{:S(2)}) collective-permute-start(bf16[128,2048]{1,0:T(8,128)(2,1)S(1)} %broadcast_select_fusion.refs_7_.refs_15_), channel_id=1, source_target_pairs={{0,1},{1,0},{2,3},{3,2},{4,5},{5,4},{6,7},{7,6},{8,9},{9,8},{10,11... | collective-permute-start | bytes 1572872 | tf_op jit(solution)/shard_map/ppermute | solution.py:495
  157.2 5.5 %collective-permute-start.43 = (bf16[50,1024]{1,0:T(8,128)(2,1)}, bf16[50,1024]{1,0:T(8,128)(2,1)S(1)}, u32[]{:S(2)}, u32[]{:S(2)}) collective-permute-start(bf16[50,1024]{1,0:T(8,128)(2,1)} %get-tuple-element.96), channel_id=1, source_target_pairs={{0,4},{2,6},{4,0},{6,2},{1,5},{3,7},{5,1},{7,3},{8,12},{10,14},{12... | collective-permute-start | bytes 307208 | tf_op jit(solution)/shard_map/ppermute | solution.py:501
  158.5 6.2 %collective-permute-start.44 = (bf16[50,1024]{1,0:T(8,128)(2,1)}, bf16[50,1024]{1,0:T(8,128)(2,1)S(1)}, u32[]{:S(2)}, u32[]{:S(2)}) collective-permute-start(bf16[50,1024]{1,0:T(8,128)(2,1)} %get-tuple-element.97), channel_id=1, source_target_pairs={{0,2},{2,0},{4,6},{6,4},{1,3},{3,1},{5,7},{7,5},{8,10},{10,8},{12,... | collective-permute-start | bytes 307208 | tf_op jit(solution)/shard_map/ppermute | solution.py:501
  159.1 7.2 %collective-permute-start.45 = (bf16[50,1024]{1,0:T(8,128)(2,1)}, bf16[50,1024]{1,0:T(8,128)(2,1)S(1)}, u32[]{:S(2)}, u32[]{:S(2)}) collective-permute-start(bf16[50,1024]{1,0:T(8,128)(2,1)} %get-tuple-element.98), channel_id=1, source_target_pairs={{0,6},{2,4},{4,2},{6,0},{1,7},{3,5},{5,3},{7,1},{8,14},{10,12},{12... | collective-permute-start | bytes 307208 | tf_op jit(solution)/shard_map/ppermute | solution.py:501
  (32 other events, 282.0 us)

commit v2 on v1

--- a/solution.py
+++ b/solution.py
@@ -185,6 +185,10 @@
     return pl.BlockSpec(block, lambda *s: (0,) * len(block))
 
 
+def grant(mib):
+    return pltpu.CompilerParams(vmem_limit_bytes=mib * 2**20)
+
+
 def like(*shape, dtype=BF):
     return jax.ShapeDtypeStruct(shape, dtype)
 
@@ -195,13 +199,13 @@
         outs[k][...] = total[PAD * k : PAD * k + rows].astype(outs[k].dtype)
 
 
-def pack_weights(query_w, akey_w, avalue_w, key_w, value_w, down_w, out_w, gate_w, up_w):
+def pack_weights(query_w, akey_w, avalue_w, key_w, value_w, gate_w, up_w):
     rows, hq = query_w.shape
     ha, hk = akey_w.shape[1], key_w.shape[1]
     quarter, half = ha // 2, key_w.shape[0] // 2
-    nd, units = down_w.shape[0], gate_w.shape[1]
-
-    def kernel(q, ak, av, kw, vw, dw, ow, gw, uw, first, od, gu):
+    units = gate_w.shape[1]
+
+    def kernel(q, ak, av, kw, vw, gw, uw, first, gu):
         xx, cc = lax.axis_index("x"), lax.axis_index("c")
         cols = pl.ds(pl.multiple_of(cc * quarter, quarter), quarter)
         part = pl.ds(pl.multiple_of(cc * half, half), half)
@@ -217,8 +221,6 @@
             first[:, hq : hq + quarter] = av[:, cols]
             first[:, hq + quarter :] = vw[part, :]
 
-        od[:nd] = dw[...]
-        od[nd:] = ow[...]
         gu[:, :units] = gw[...]
         gu[:, units:] = uw[...]
 
@@ -226,11 +228,10 @@
         kernel,
         out_shape=(
             like(rows, hq + quarter + hk),
-            like(nd + out_w.shape[0], down_w.shape[1]),
             like(rows, 2 * units),
         ),
         name="pack_weights",
-    )(query_w, akey_w, avalue_w, key_w, value_w, down_w, out_w, gate_w, up_w)
+    )(query_w, akey_w, avalue_w, key_w, value_w, gate_w, up_w)
 
 
 def expert_in(x_g, temb, action_in, attn_gain, mlp_gain, final_gain, head_w, span, per):
@@ -294,6 +295,7 @@
         kernel,
         out_shape=(like(count * rows, cols), like(count * rows, total - cols)),
         name="unpack_first",
+        compiler_params=grant(8),
     )(*got)
 
 
@@ -312,10 +314,37 @@
         out_shape=[like(span, cols) for _ in RELS],
         scratch_shapes=[pltpu.VMEM((an.shape[0], cols), F32)],
         name="queries",
+        compiler_params=grant(8),
     )(an, own, other)
 
 
-def attention(prefix, gain, kv_own, kv_oth, qa, length, heads_cols):
+def normed_blocks(prefix, gain):
+    positions, width = prefix.shape
+    step, count = 256, 16
+    per, no = width // 16, 4
+
+    def kernel(x, g, out):
+        oo, ii, cc = (lax.axis_index(n) for n in ("o", "i", "c"))
+        v = x[...].astype(F32)
+        scale = lax.rsqrt(jnp.mean(v * v, axis=-1, keepdims=True) + 1e-06)
+        for b in range(count):
+            r, i, c = b % no, (b // no) % 2, b // (2 * no)
+            block = ((oo ^ r) * 2 + (cc ^ c)) * 2 + (ii ^ i)
+            src = pl.ds(pl.multiple_of(block * per, per), per)
+            out[:, b * per : (b + 1) * per] = (x[:, src].astype(F32) * scale * g[:, src]).astype(BF)
+
+    return pl.pallas_call(
+        kernel,
+        grid=(positions // step,),
+        out_shape=like(positions, width),
+        in_specs=[pl.BlockSpec((step, width), lambda s: (s, 0)), at(1, width)],
+        out_specs=pl.BlockSpec((step, width), lambda s: (s, 0)),
+        name="normed_blocks",
+        compiler_params=grant(16),
+    )(prefix, gain.reshape(1, width))
+
+
+def attention(prefix, kv_own, kv_oth, qa, length, heads_cols):
     positions, width = prefix.shape
     tall, hd = kv_own[0].shape
     span, qa_cols = qa[0].shape
@@ -323,16 +352,13 @@
     heads = len(RELS) * per_part
     step = 512
     steps = positions // step
-    count = 16
-    per = width // count
-    no = count // 4
-
-    def kernel(len_ref, x, g, *refs):
+
+    def kernel(len_ref, pn, *refs):
         own, oth, qs = refs[0:4], refs[4:8], refs[8:12]
         outs = refs[12:16]
-        q_all, pn, acc, den = refs[16:20]
+        q_all, acc, den = refs[16:19]
         s = pl.program_id(0)
-        oo, ii, xx, cc = (lax.axis_index(n) for n in ("o", "i", "x", "c"))
+        ii, xx = lax.axis_index("i"), lax.axis_index("x")
 
         @pl.when(s == 0)
         def _():
@@ -345,13 +371,6 @@
             acc[...] = jnp.zeros_like(acc)
             den[...] = jnp.zeros_like(den)
 
-        v = x[...].astype(F32)
-        scale = lax.rsqrt(jnp.mean(v * v, axis=-1, keepdims=True) + 1e-06)
-        for b in range(count):
-            r, i, c = b % no, (b // no) % 2, b // (2 * no)
-            block = ((oo ^ r) * 2 + (cc ^ c)) * 2 + (ii ^ i)
-            src = pl.ds(pl.multiple_of(block * per, per), per)
-            pn[:, b * per : (b + 1) * per] = (x[:, src].astype(F32) * scale * g[:, src]).astype(BF)
         same = diff = 0.0
         for c, refs_c in enumerate((own, oth)):
             for i in range(2):
@@ -365,7 +384,7 @@
         nt = (((1,), (1,)), ((), ()))
         sc = lax.dot_general(q_all[...], keys, nt, preferred_element_type=F32)
         spot = s * step + lax.broadcasted_iota(jnp.int32, sc.shape, 1)
-        p = jnp.where(spot < len_ref[0], jnp.exp(sc), 0.0)
+        p = jnp.where(spot < len_ref[lax.axis_index("x") * 2 + lax.axis_index("c")], jnp.exp(sc), 0.0)
         den[...] += jnp.sum(p, axis=-1, keepdims=True)
         acc[...] += dot(p.astype(BF), vals)
 
@@ -393,19 +412,18 @@
         in_specs=[
             pl.BlockSpec(memory_space=pltpu.SMEM),
             pl.BlockSpec((step, width), lambda s: (s, 0)),
-            at(1, width),
         ]
         + [at(tall, hd)] * 8
         + [at(span, qa_cols)] * 4,
         out_specs=[at(span, heads_cols)] * 4,
         scratch_shapes=[
             pltpu.VMEM((PAD * heads, hd), BF),
-            pltpu.VMEM((step, width), BF),
             pltpu.VMEM((PAD * heads, hd), F32),
             pltpu.VMEM((PAD * heads, 1), F32),
         ],
         name="prefix_attention",
-    )(length, prefix, gain.reshape(1, width), *kv_own, *kv_oth, *qa)
+        compiler_params=grant(24),
+    )(length, prefix, *kv_own, *kv_oth, *qa)
 
 
 def row_outs(rows, width, parts):
@@ -440,6 +458,7 @@
             pltpu.VMEM((PAD * parts, count * cols), F32),
         ],
         name="out_project",
+        compiler_params=grant(12),
     )(*attn, *pieces)
 
 
@@ -487,7 +506,34 @@
             pltpu.VMEM((PAD * parts, count * cols), F32),
         ],
         name="feed_forward",
+        compiler_params=grant(20),
     )(*mn, *gu, *gu, *od)
+
+
+def velocity_and_loss(h1, parts, gains, head_p, noise, actions):
+    rows, _ = h1.shape
+    adim = head_p.shape[0]
+    nt = (((1,), (1,)), ((), ()))
+
+    def kernel(h, *refs):
+        p_refs, (g, w, nz, ac, vel, loss) = refs[: len(parts)], refs[len(parts) :]
+        at_own = lax.axis_index("x") * 2 + lax.axis_index("c")
+        v = h[...]
+        for p in p_refs:
+            v = v + p[...].astype(F32)
+        v = v * lax.rsqrt(jnp.mean(v * v, axis=-1, keepdims=True) + 1e-06) * g[1:2, :]
+        out = lax.dot_general(w[...], v.astype(BF), nt, preferred_element_type=F32)
+        vel[...] = out
+        diff = out - (nz[at_own] - ac[at_own])
+        square = jnp.sum(diff * diff, axis=1, keepdims=True)
+        loss[...] = jnp.sum(square, axis=0, keepdims=True) / (rows * adim)
+
+    return pl.pallas_call(
+        kernel,
+        out_shape=(like(adim, rows, dtype=F32), like(1, 1, dtype=F32)),
+        name="velocity_and_loss",
+        compiler_params=grant(8),
+    )(h1, *parts, gains, head_p, noise, actions)
 
 
 def make(no, ni, nx, nc):
@@ -555,16 +601,17 @@
         heads_cols = query_w.shape[1]
         units = gate_w.shape[1]
         oo, xx, cc = (lax.axis_index(a) for a in ("o", "x", "c"))
-        member = xx * nc + cc
 
         def order(first, second, at_one):
             return jnp.where(at_one == 0, first, second), jnp.where(at_one == 0, second, first)
 
-        first, od, gu = pack_weights(
-            query_w, akey_w, avalue_w, key_weight, value_weight, down_w, out_w, gate_w, up_w
+        first, gu = pack_weights(
+            query_w, akey_w, avalue_w, key_weight, value_weight, gate_w, up_w
         )
         got = [turned(first, r) for r in range(no)]
-        od_0, gu_0 = turned(od, 0), turned(gu, 0)
+        gu_0 = turned(gu, 0)
+        out_0 = turned(out_w, 0)
+        down_0 = turned(down_w, 0)
 
         times = (time_index.astype(F32) + 0.5) / TSTEPS
         x_t = times[:, None, None] * noise + (1.0 - times)[:, None, None] * actions
@@ -600,54 +647,49 @@
         )
 
         got = [after(t, an) for t in got]
+        gu_t = after(gu_0, *got)
+        gu_a, gu_b = hop(gu_t, partner(1)), hop(gu_t, MIDDLE)
         qa_own, kv = unpack_first(got, first.shape[1] - hd)
         kv_all = spread(kv)
-        od_got = [od_0] + [hop(after(od_0, qa_own), partner(r)) for r in range(1, no)]
+        out_t = after(out_0, qa_own)
+        out_got = [out_t] + [hop(out_t, partner(r)) for r in range(1, no)]
         qa_oth = flip(qa_own, "c")
         q_parts = queries(an, qa_own, qa_oth, heads_cols, hd ** (-0.5), span)
         qa = exchange(q_parts)
-        gu_t = after(gu_0, q_parts[0])
-        gu_a, gu_b = hop(gu_t, partner(1)), hop(gu_t, MIDDLE)
-        kv_all = [after(t, q_parts[0]) for t in kv_all]
+        pn = normed_blocks(
+            after(prefix_hidden, q_parts[0]).reshape(positions, width), prefix_gain
+        )
+        gu_c, gu_d = hop(after(gu_b, q_parts[0]), OUTWARD), hop(after(gu_a, q_parts[0]), MIDDLE)
+        down_t = after(down_0, q_parts[0])
+        down_got = [down_t] + [hop(down_t, partner(r)) for r in range(1, no)]
+        kv_all = [after(t, pn) for t in kv_all]
         kv_oth = [flip(t, "c") for t in kv_all]
-        length = lax.dynamic_slice_in_dim(prefix_len, member, 1, 0)
-        attn = attention(
-            prefix_hidden.reshape(positions, width),
-            prefix_gain,
-            kv_all,
-            kv_oth,
-            qa,
-            length,
-            heads_cols,
-        )
+        attn = attention(pn, kv_all, kv_oth, qa, prefix_len, heads_cols)
 
         attn_in = exchange(attn)
-        gu_c, gu_d = hop(after(gu_b, attn[0]), OUTWARD), hop(after(gu_a, attn[0]), MIDDLE)
-        od_all = od_got + [flip(after(t, attn[0]), "c") for t in od_got]
-        out_parts = out_project(attn_in, od_all, heads_cols)
+        gu_e = hop(after(gu_d, attn[0]), OUTWARD)
+        out_all = out_got + [flip(after(t, pn), "c") for t in out_got]
+        out_parts = out_project(attn_in, out_all, heads_cols)
         out_in = exchange(out_parts)
-        gu_e = hop(after(gu_d, out_parts[0]), OUTWARD)
         h1 = h0 + sum(t.astype(F32) for t in out_in)
 
         mn = spread(rms(h1, gains[0]).astype(BF))
         inner = (oo == 1) | (oo == 2)
-        gu_t, gu_a, gu_b, gu_c, gu_d, gu_e = (
-            after(t, h1) for t in (gu_t, gu_a, gu_b, gu_c, gu_d, after(gu_e, *mn))
-        )
+        gu_t, gu_a, gu_b, gu_c, gu_d = (
+            after(t, out_parts[0]) for t in (gu_t, gu_a, gu_b, gu_c, gu_d)
+        )
+        gu_e = after(gu_e, *mn)
         gu_got = [gu_t, gu_a, jnp.where(inner, gu_d, gu_c), jnp.where(inner, gu_b, gu_e)]
         gu_all = gu_got + [flip(t, "c") for t in gu_got]
-        ff_parts = feed_forward(mn, gu_all, od_all, units)
-        h2 = h1 + sum(t.astype(F32) for t in exchange(ff_parts))
-
-        final = rms(h2, gains[1]).astype(BF)
-        velocity = lax.dot_general(
-            final, head_p, (((1,), (1,)), ((), ())), preferred_element_type=F32
-        )
-        target = noise - actions
-        own_target = lax.dynamic_slice_in_dim(target, member, own_eps, 0)
-        velocity = velocity.reshape(own_eps, span, adim)
-        diff = velocity - own_target
-        return velocity, jnp.mean(diff * diff, axis=(1, 2))
+        down_got = [after(t, *mn) for t in down_got]
+        down_all = down_got + [flip(t, "c") for t in down_got]
+        ff_parts = feed_forward(mn, gu_all, down_all, units)
+        ff_in = exchange(ff_parts)
+        velocity, loss = velocity_and_loss(
+            h1, ff_in, gains, head_p, noise.transpose(0, 2, 1), actions.transpose(0, 2, 1)
+        )
+        velocity = velocity.reshape(own_eps, adim, span).transpose(0, 2, 1)
+        return velocity, loss.reshape(own_eps)
 
     def on_device(*values):
         eps, positions, _ = values[0].shape

time: 172 us -> 153 us (0.89)
  the two profiles are of different devices: /device:TPU:0 before, /device:TPU:6 now
where the time goes in v2:
time: 153 us; the launch traced here: 151 us
  waiting for transfers between devices  63.8 us (42%)
  starting transfers between devices  58 us (38%)
  Pallas kernels  18.2 us (12%)
  other arithmetic  5.24 us (3%)
  local copies, waits for them, and re-layouts  4.38 us (3%)
    ppermute x11, waiting for transfers between devices, hop(): return lax.ppermute(value, 'o', pairs)  28.9 us
    ppermute x18, starting transfers between devices, cross(): return lax.ppermute(value, ('i', 'x'), pairs)  21.4 us
    ppermute x18, waiting for transfers between devices, cross(): return lax.ppermute(value, ('i', 'x'), pairs)  21 us
    ppermute x11, starting transfers between devices, hop(): return lax.ppermute(value, 'o', pairs)  17.6 us
    ppermute x7, starting transfers between devices, turned(): lax.ppermute(value, ('o', 'i', 'c'), [((o * ni + i) * nc + c, ((o ^ r) *...  16.1 us
    ppermute x7, waiting for transfers between devices, turned(): lax.ppermute(value, ('o', 'i', 'c'), [((o * ni + i) * nc + c, ((o ^ r) *...  7.1 us
    ppermute x18, waiting for transfers between devices, flip(): return lax.ppermute(value, axis, [(0, 1), (1, 0)])  6.83 us
    pallas_call x1, Pallas kernels, attention(): pl.pallas_call(kernel, grid=(steps,), out_shape=[like(span, heads_cols) f...  5.06 us
  transfers between devices with their start and end apart: 54, of which 19 were waited for; matrix products, arithmetic and copies ran while one was open for 4% of the time, Pallas kernels for 7%

profile of v2, /device:TPU:6, one launch (start us, length us, event | category | flops | bytes accessed | tf_op | source)
XLA Modules:
  0.0 150.7 jit_solution(12536619810833503849)
XLA Ops:
  0.6 2.2 %pack_weights.1 = (bf16[128,896]{1,0:T(8,128)(2,1)}, bf16[128,2048]{1,0:T(8,128)(2,1)}) custom-call(bf16[128,512]{1,0:T(8,128)(2,1)} %q.1, bf16[128,256]{1,0:T(8,128)(2,1)} %ak.1, bf16[128,256]{1,0:T(8,128)(2,1)} %av.1, bf16[256,256]{1,0:T(8,128)(2,1)} %kw.1, bf16[256,256]{1,0:T(8,128)(2,1)} %vw.1, bf16[128,1024]{1,0:T(8,128)(2,1)} %gw.1, bf16[128,1024]{1,0:T(8,128)(2,1)} %uw.1), custom_call_target="tpu_custom_call" | custom-call | tf_op jit(solution)/shard_map/pack_weights/pallas_call | solution.py:227
  2.8 1.9 %collective-permute-start.1 = (bf16[128,896]{1,0:T(8,128)(2,1)}, bf16[128,896]{1,0:T(8,128)(2,1)S(1)}, u32[]{:S(2)}, u32[]{:S(2)}) collective-permute-start(bf16[128,896]{1,0:T(8,128)(2,1)} %get-tuple-element.59), channel_id=1, source_target_pairs={{0,0},{1,4},{4,1},{5,5},{8,8},{9,12},{12,9},{13,13},{16,16},{17,20... | collective-permute-start | bytes 688136 | tf_op jit(solution)/shard_map/ppermute | solution.py:556
  4.7 2.8 %collective-permute-start.2 = (bf16[128,896]{1,0:T(8,128)(2,1)}, bf16[128,896]{1,0:T(8,128)(2,1)S(1)}, u32[]{:S(2)}, u32[]{:S(2)}) collective-permute-start(bf16[128,896]{1,0:T(8,128)(2,1)} %get-tuple-element.59), channel_id=1, source_target_pairs={{0,8},{1,12},{4,9},{5,13},{8,0},{9,4},{12,1},{13,5},{16,24},{17,28... | collective-permute-start | bytes 688136 | tf_op jit(solution)/shard_map/ppermute | solution.py:556
  7.6 2.0 %collective-permute-start.3 = (bf16[128,896]{1,0:T(8,128)(2,1)}, bf16[128,896]{1,0:T(8,128)(2,1)S(1)}, u32[]{:S(2)}, u32[]{:S(2)}) collective-permute-start(bf16[128,896]{1,0:T(8,128)(2,1)} %get-tuple-element.59), channel_id=1, source_target_pairs={{0,16},{1,20},{4,17},{5,21},{8,24},{9,28},{12,25},{13,29},{16,0},{... | collective-permute-start | bytes 688136 | tf_op jit(solution)/shard_map/ppermute | solution.py:556
  9.6 1.4 collective-permute-start.4
  13.2 4.0 %collective-permute-done = f32[2,51,32]{1,2,0:T(8,128)S(1)} collective-permute-done((f32[2,51,32]{1,2,0:T(8,128)S(1)}, f32[2,51,32]{1,2,0:T(8,128)S(1)}, u32[]{:S(2)}, u32[]{:S(2)}) %collective-permute-start) | collective-permute-done | bytes 13088 | tf_op jit(solution)/shard_map/ppermute | solution.py:541
  18.9 2.2 %expert_in.1 = (bf16[256,1024]{1,0:T(8,128)(2,1)}, f32[50,1024]{1,0:T(8,128)}, f32[8,1024]{1,0:T(8,128)}, bf16[32,1024]{1,0:T(8,128)(2,1)}) custom-call(bf16[256,32]{1,0:T(8,128)(2,1)} %bitcast.23, f32[4,1024]{1,0:T(4,128)} %pad_maximum_fusion.2.te, bf16[32,1024]{1,0:T(8,128)(2,1)} %act.1, f32[1,1024]{1,0:T(1,128)} %bitcast.28, f32[1,1024]{1,0:T(1,128)} %bitcast.29, ...), custom_call_target="tpu_custom_call" | custom-call | tf_op jit(solution)/shard_map/expert_in/pallas_call | solution.py:263
  21.1 6.2 %collective-permute-done.3.refs_2_ = bf16[128,896]{1,0:T(8,128)(2,1)S(1)} collective-permute-done((bf16[128,896]{1,0:T(8,128)(2,1)}, bf16[128,896]{1,0:T(8,128)(2,1)S(1)}, u32[]{:S(2)}, u32[]{:S(2)}) %collective-permute-start.3) | collective-permute-done | bytes 229408 | tf_op jit(solution)/shard_map/ppermute | solution.py:556
  27.5 1.9 %collective-permute-start.19 = (bf16[512,128]{1,0:T(8,128)(2,1)}, bf16[512,128]{1,0:T(8,128)(2,1)S(1)}, u32[]{:S(2)}, u32[]{:S(2)}) collective-permute-start(bf16[512,128]{1,0:T(8,128)(2,1)} %param.33), channel_id=1, source_target_pairs={{0,0},{1,4},{4,1},{5,5},{8,8},{9,12},{12,9},{13,13},{16,16},{17,20... | collective-permute-start | bytes 393224 | tf_op jit(solution)/shard_map/ppermute | solution.py:556
  29.4 3.6 %collective-permute-start.33 = (bf16[128,2048]{1,0:T(8,128)(2,1)}, bf16[128,2048]{1,0:T(8,128)(2,1)S(1)}, u32[]{:S(2)}, u32[]{:S(2)}) collective-permute-start(bf16[128,2048]{1,0:T(8,128)(2,1)} %get-tuple-element.89), channel_id=1, source_target_pairs={{0,0},{1,4},{4,1},{5,5},{8,8},{9,12},{12,9},{13,13},{16,16},{17,20... | collective-permute-start | bytes 1572872 | tf_op jit(solution)/shard_map/ppermute | solution.py:556
  34.0 3.6 %collective-permute-start.20 = (bf16[512,128]{1,0:T(8,128)(2,1)S(1)}, bf16[512,128]{1,0:T(8,128)(2,1)S(1)}, u32[]{:S(2)}, u32[]{:S(2)}) collective-permute-start(bf16[512,128]{1,0:T(8,128)(2,1)S(1)} %collective-permute-done.19.refs_4_), channel_id=1, source_target_pairs={{0,8},{8,0},{16,24},{24,16},{1,9},{9,1},{17,25},{25,17},{2,10},{10... | collective-permute-start | bytes 393224 | tf_op jit(solution)/shard_map/ppermute | solution.py:568
  38.5 2.2 %collective-permute-done.20.refs_5_ = bf16[512,128]{1,0:T(8,128)(2,1)S(1)} collective-permute-done((bf16[512,128]{1,0:T(8,128)(2,1)S(1)}, bf16[512,128]{1,0:T(8,128)(2,1)S(1)}, u32[]{:S(2)}, u32[]{:S(2)}) %collective-permute-start.20) | collective-permute-done | bytes 131104 | tf_op jit(solution)/shard_map/ppermute | solution.py:568
  41.3 3.5 %collective-permute-done.21.refs_6_ = bf16[512,128]{1,0:T(8,128)(2,1)S(1)} collective-permute-done((bf16[512,128]{1,0:T(8,128)(2,1)S(1)}, bf16[512,128]{1,0:T(8,128)(2,1)S(1)}, u32[]{:S(2)}, u32[]{:S(2)}) %collective-permute-start.21) | collective-permute-done | bytes 131104 | tf_op jit(solution)/shard_map/ppermute | solution.py:568
  44.8 2.3 %collective-permute-start.22 = (bf16[512,128]{1,0:T(8,128)(2,1)S(1)}, bf16[512,128]{1,0:T(8,128)(2,1)S(1)}, u32[]{:S(2)}, u32[]{:S(2)}) collective-permute-start(bf16[512,128]{1,0:T(8,128)(2,1)S(1)} %collective-permute-done.19.refs_4_), channel_id=1, source_target_pairs={{0,24},{8,16},{16,8},{24,0},{1,25},{9,17},{17,9},{25,1},{2,26},{10... | collective-permute-start | bytes 393224 | tf_op jit(solution)/shard_map/ppermute | solution.py:568
  48.8 2.2 %copy-done = bf16[1,1024,2048]{2,1,0:T(8,128)(2,1)S(1)} copy-done((bf16[1,1024,2048]{2,1,0:T(8,128)(2,1)S(1)}, bf16[1,1024,2048]{2,1,0:T(8,128)(2,1)}, u32[]{:S(2)}) %copy-start) | copy-done | bytes 4194328
  50.9 2.8 %normed_blocks.1.pn = bf16[1024,2048]{1,0:T(8,128)(2,1)S(1)} custom-call(bf16[1024,2048]{1,0:T(8,128)(2,1)S(1)} %bitcast.19, f32[1,2048]{1,0:T(1,128)S(1)} %bitcast.22), custom_call_target="tpu_custom_call" | custom-call | tf_op jit(solution)/shard_map/normed_blocks/pallas_call | solution.py:336
  53.9 2.0 %collective-permute-start.13 = (bf16[50,640]{1,0:T(8,128)(2,1)S(1)}, bf16[50,640]{1,0:T(8,128)(2,1)S(1)}, u32[]{:S(2)}, u32[]{:S(2)}) collective-permute-start(bf16[50,640]{1,0:T(8,128)(2,1)S(1)} %get-tuple-element.72), channel_id=1, source_target_pairs={{0,4},{2,6},{4,0},{6,2},{1,5},{3,7},{5,1},{7,3},{8,12},{10,14},{12... | collective-permute-start | bytes 192008 | tf_op jit(solution)/shard_map/ppermute | solution.py:547
  55.9 1.5 collective-permute-start.14
  57.6 1.1 collective-permute-done.13.refs_9_
  58.7 1.7 %collective-permute-done.14.refs_10_ = bf16[50,640]{1,0:T(8,128)(2,1)S(1)} collective-permute-done((bf16[50,640]{1,0:T(8,128)(2,1)S(1)}, bf16[50,640]{1,0:T(8,128)(2,1)S(1)}, u32[]{:S(2)}, u32[]{:S(2)}) %collective-permute-start.14) | collective-permute-done | bytes 64032 | tf_op jit(solution)/shard_map/ppermute | solution.py:547
  60.5 2.5 %collective-permute-done.15.refs_11_ = bf16[50,640]{1,0:T(8,128)(2,1)S(1)} collective-permute-done((bf16[50,640]{1,0:T(8,128)(2,1)S(1)}, bf16[50,640]{1,0:T(8,128)(2,1)S(1)}, u32[]{:S(2)}, u32[]{:S(2)}) %collective-permute-start.15) | collective-permute-done | bytes 64032 | tf_op jit(solution)/shard_map/ppermute | solution.py:547
  64.5 2.4 %collective-permute-start.43 = (bf16[1024,128]{1,0:T(8,128)(2,1)S(1)}, bf16[1024,128]{1,0:T(8,128)(2,1)S(1)}, u32[]{:S(2)}, u32[]{:S(2)}) collective-permute-start(bf16[1024,128]{1,0:T(8,128)(2,1)S(1)} %copy-done.9), channel_id=1, source_target_pairs={{0,0},{1,4},{4,1},{5,5},{8,8},{9,12},{12,9},{13,13},{16,16},{17,20... | collective-permute-start | bytes 786440 | tf_op jit(solution)/shard_map/ppermute | solution.py:556
  67.5 5.1 %prefix_attention.1 = (bf16[50,512]{1,0:T(8,128)(2,1)S(1)}, bf16[50,512]{1,0:T(8,128)(2,1)S(1)}, bf16[50,512]{1,0:T(8,128)(2,1)S(1)}, bf16[50,512]{1,0:T(8,128)(2,1)S(1)}) custom-call(s32[4]{0:T(128)S(1)} %copy-done.7, bf16[1024,2048]{1,0:T(8,128)(2,1)S(1)} %normed_blocks.1.pn, bf16[512,256]{1,0:T(8,128)(2,1)S(1)} %get-tuple-element.68.refs_0_, ...), custom_call_target="tpu_custom_call" | custom-call | tf_op jit(solution)/shard_map/prefix_attention/pallas_call | solution.py:408
  72.6 1.3 collective-permute-start.16
  73.9 1.5 collective-permute-start.17
  75.4 1.4 collective-permute-done.16.refs_1_
  76.8 2.2 %collective-permute-start.18 = (bf16[50,512]{1,0:T(8,128)(2,1)S(1)}, bf16[50,512]{1,0:T(8,128)(2,1)S(1)}, u32[]{:S(2)}, u32[]{:S(2)}) collective-permute-start(bf16[50,512]{1,0:T(8,128)(2,1)S(1)} %get-tuple-element.78), channel_id=1, source_target_pairs={{0,6},{2,4},{4,2},{6,0},{1,7},{3,5},{5,3},{7,1},{8,14},{10,12},{12... | collective-permute-start | bytes 153608 | tf_op jit(solution)/shard_map/ppermute | solution.py:547
  79.1 2.8 %collective-permute-done.18.refs_3_ = bf16[50,512]{1,0:T(8,128)(2,1)S(1)} collective-permute-done((bf16[50,512]{1,0:T(8,128)(2,1)S(1)}, bf16[50,512]{1,0:T(8,128)(2,1)S(1)}, u32[]{:S(2)}, u32[]{:S(2)}) %collective-permute-start.18) | collective-permute-done | bytes 51232 | tf_op jit(solution)/shard_map/ppermute | solution.py:547
  82.4 2.3 %collective-permute-start.29 = (bf16[50,1024]{1,0:T(8,128)(2,1)S(1)}, bf16[50,1024]{1,0:T(8,128)(2,1)S(1)}, u32[]{:S(2)}, u32[]{:S(2)}) collective-permute-start(bf16[50,1024]{1,0:T(8,128)(2,1)S(1)} %get-tuple-element.87), channel_id=1, source_target_pairs={{0,6},{2,4},{4,2},{6,0},{1,7},{3,5},{5,3},{7,1},{8,14},{10,12},{12... | collective-permute-start | bytes 307208 | tf_op jit(solution)/shard_map/ppermute | solution.py:547
  86.0 3.2 %collective-permute-start.44 = (bf16[1024,128]{1,0:T(8,128)(2,1)S(1)}, bf16[1024,128]{1,0:T(8,128)(2,1)S(1)}, u32[]{:S(2)}, u32[]{:S(2)}) collective-permute-start(bf16[1024,128]{1,0:T(8,128)(2,1)S(1)} %collective-permute-done.43.refs_20_), channel_id=1, source_target_pairs={{0,8},{8,0},{16,24},{24,16},{1,9},{9,1},{17,25},{25,17},{2,10},{10... | collective-permute-start | bytes 786440 | tf_op jit(solution)/shard_map/ppermute | solution.py:568
  90.0 1.5 collective-permute-start.35
  91.5 1.3 collective-permute-start.37
  93.1 1.8 %collective-permute-start.30 = (bf16[50,1024]{1,0:T(8,128)(2,1)S(1)}, bf16[50,1024]{1,0:T(8,128)(2,1)S(1)}, u32[]{:S(2)}, u32[]{:S(2)}) collective-permute-start(bf16[50,1024]{1,0:T(8,128)(2,1)S(1)} %multiply_convert_fusion.refs_0_), channel_id=1, source_target_pairs={{0,4},{2,6},{4,0},{6,2},{1,5},{3,7},{5,1},{7,3},{8,12},{10,14},{12... | collective-permute-start | bytes 307208 | tf_op jit(solution)/shard_map/ppermute | solution.py:547
  94.9 3.0 %collective-permute-done.30.refs_1_ = bf16[50,1024]{1,0:T(8,128)(2,1)S(1)} collective-permute-done((bf16[50,1024]{1,0:T(8,128)(2,1)S(1)}, bf16[50,1024]{1,0:T(8,128)(2,1)S(1)}, u32[]{:S(2)}, u32[]{:S(2)}) %collective-permute-start.30) | collective-permute-done | bytes 102432 | tf_op jit(solution)/shard_map/ppermute | solution.py:547
  98.8 2.4 %collective-permute-start.32 = (bf16[50,1024]{1,0:T(8,128)(2,1)S(1)}, bf16[50,1024]{1,0:T(8,128)(2,1)S(1)}, u32[]{:S(2)}, u32[]{:S(2)}) collective-permute-start(bf16[50,1024]{1,0:T(8,128)(2,1)S(1)} %multiply_convert_fusion.refs_0_), channel_id=1, source_target_pairs={{0,6},{2,4},{4,2},{6,0},{1,7},{3,5},{5,3},{7,1},{8,14},{10,12},{12... | collective-permute-start | bytes 307208 | tf_op jit(solution)/shard_map/ppermute | solution.py:547
  101.2 1.6 %collective-permute-done.31.refs_2_ = bf16[50,1024]{1,0:T(8,128)(2,1)S(1)} collective-permute-done((bf16[50,1024]{1,0:T(8,128)(2,1)S(1)}, bf16[50,1024]{1,0:T(8,128)(2,1)S(1)}, u32[]{:S(2)}, u32[]{:S(2)}) %collective-permute-start.31) | collective-permute-done | bytes 102432 | tf_op jit(solution)/shard_map/ppermute | solution.py:547
  102.8 1.3 collective-permute-start.38
  104.0 1.1 collective-permute-done.32.refs_3_
  105.2 1.6 %collective-permute-start.46 = (bf16[1024,128]{1,0:T(8,128)(2,1)S(1)}, bf16[1024,128]{1,0:T(8,128)(2,1)S(1)}, u32[]{:S(2)}, u32[]{:S(2)}) collective-permute-start(bf16[1024,128]{1,0:T(8,128)(2,1)S(1)} %collective-permute-done.43.refs_20_), channel_id=1, source_target_pairs={{0,24},{8,16},{16,8},{24,0},{1,25},{9,17},{17,9},{25,1},{2,26},{10... | collective-permute-start | bytes 786440 | tf_op jit(solution)/shard_map/ppermute | solution.py:568
  107.2 8.5 %collective-permute-done.37 = bf16[128,2048]{1,0:T(8,128)(2,1)} collective-permute-done((bf16[128,2048]{1,0:T(8,128)(2,1)S(1)}, bf16[128,2048]{1,0:T(8,128)(2,1)}, u32[]{:S(2)}, u32[]{:S(2)}) %collective-permute-start.37) | collective-permute-done | bytes 524320 | tf_op jit(solution)/shard_map/ppermute | solution.py:568
  115.8 1.1 broadcast_select_fusion.1.refs_6_.refs_14_
  116.9 14.7 %collective-permute-done.38 = bf16[128,2048]{1,0:T(8,128)(2,1)} collective-permute-done((bf16[128,2048]{1,0:T(8,128)(2,1)}, bf16[128,2048]{1,0:T(8,128)(2,1)}, u32[]{:S(2)}, u32[]{:S(2)}) %collective-permute-start.38) | collective-permute-done | bytes 524320 | tf_op jit(solution)/shard_map/ppermute | solution.py:568
  133.9 2.8 %collective-permute-done.50.refs_27_ = bf16[1024,128]{1,0:T(8,128)(2,1)S(1)} collective-permute-done((bf16[1024,128]{1,0:T(8,128)(2,1)S(1)}, bf16[1024,128]{1,0:T(8,128)(2,1)S(1)}, u32[]{:S(2)}, u32[]{:S(2)}) %collective-permute-start.50) | collective-permute-done | bytes 262176 | tf_op jit(solution)/shard_map/ppermute | solution.py:541
  136.7 3.9 %feed_forward.1 = (f32[50,1024]{1,0:T(8,128)S(1)}, bf16[50,1024]{1,0:T(8,128)(2,1)S(1)}, bf16[50,1024]{1,0:T(8,128)(2,1)S(1)}, bf16[50,1024]{1,0:T(8,128)(2,1)S(1)}) custom-call(bf16[50,1024]{1,0:T(8,128)(2,1)S(1)} %multiply_convert_fusion.refs_0_, bf16[50,1024]{1,0:T(8,128)(2,1)S(1)} %collective-permute-done.30.refs_1_, ...), custom_call_target="tpu_custom_call" | custom-call | tf_op jit(solution)/shard_map/feed_forward/pallas_call | solution.py:495
  141.0 1.2 collective-permute-start.52
  142.1 2.0 %collective-permute-start.53 = (bf16[50,1024]{1,0:T(8,128)(2,1)S(1)}, bf16[50,1024]{1,0:T(8,128)(2,1)S(1)}, u32[]{:S(2)}, u32[]{:S(2)}) collective-permute-start(bf16[50,1024]{1,0:T(8,128)(2,1)S(1)} %get-tuple-element.108), channel_id=1, source_target_pairs={{0,6},{2,4},{4,2},{6,0},{1,7},{3,5},{5,3},{7,1},{8,14},{10,12},{12... | collective-permute-start | bytes 307208 | tf_op jit(solution)/shard_map/ppermute | solution.py:547
  144.2 1.9 %collective-permute-done.51.refs_1_ = bf16[50,1024]{1,0:T(8,128)(2,1)S(1)} collective-permute-done((bf16[50,1024]{1,0:T(8,128)(2,1)S(1)}, bf16[50,1024]{1,0:T(8,128)(2,1)S(1)}, u32[]{:S(2)}, u32[]{:S(2)}) %collective-permute-start.51) | collective-permute-done | bytes 102432 | tf_op jit(solution)/shard_map/ppermute | solution.py:547
  146.6 3.1 %collective-permute-done.53.refs_3_ = bf16[50,1024]{1,0:T(8,128)(2,1)S(1)} collective-permute-done((bf16[50,1024]{1,0:T(8,128)(2,1)S(1)}, bf16[50,1024]{1,0:T(8,128)(2,1)S(1)}, u32[]{:S(2)}, u32[]{:S(2)}) %collective-permute-start.53) | collective-permute-done | bytes 102432 | tf_op jit(solution)/shard_map/ppermute | solution.py:547
  (111 shorter events, 18.9 us)
Async XLA Ops:
  2.8 18.3 %collective-permute-start.1 = (bf16[128,896]{1,0:T(8,128)(2,1)}, bf16[128,896]{1,0:T(8,128)(2,1)S(1)}, u32[]{:S(2)}, u32[]{:S(2)}) collective-permute-start(bf16[128,896]{1,0:T(8,128)(2,1)} %get-tuple-element.59), channel_id=1, source_target_pairs={{0,0},{1,4},{4,1},{5,5},{8,8},{9,12},{12,9},{13,13},{16,16},{17,20... | collective-permute-start | bytes 688136 | tf_op jit(solution)/shard_map/ppermute | solution.py:556
  4.7 16.4 %collective-permute-start.2 = (bf16[128,896]{1,0:T(8,128)(2,1)}, bf16[128,896]{1,0:T(8,128)(2,1)S(1)}, u32[]{:S(2)}, u32[]{:S(2)}) collective-permute-start(bf16[128,896]{1,0:T(8,128)(2,1)} %get-tuple-element.59), channel_id=1, source_target_pairs={{0,8},{1,12},{4,9},{5,13},{8,0},{9,4},{12,1},{13,5},{16,24},{17,28... | collective-permute-start | bytes 688136 | tf_op jit(solution)/shard_map/ppermute | solution.py:556
  7.6 19.7 %collective-permute-start.3 = (bf16[128,896]{1,0:T(8,128)(2,1)}, bf16[128,896]{1,0:T(8,128)(2,1)S(1)}, u32[]{:S(2)}, u32[]{:S(2)}) collective-permute-start(bf16[128,896]{1,0:T(8,128)(2,1)} %get-tuple-element.59), channel_id=1, source_target_pairs={{0,16},{1,20},{4,17},{5,21},{8,24},{9,28},{12,25},{13,29},{16,0},{... | collective-permute-start | bytes 688136 | tf_op jit(solution)/shard_map/ppermute | solution.py:556
  9.6 17.7 %collective-permute-start.4 = (bf16[128,896]{1,0:T(8,128)(2,1)}, bf16[128,896]{1,0:T(8,128)(2,1)S(1)}, u32[]{:S(2)}, u32[]{:S(2)}) collective-permute-start(bf16[128,896]{1,0:T(8,128)(2,1)} %get-tuple-element.59), channel_id=1, source_target_pairs={{0,24},{1,28},{4,25},{5,29},{8,16},{9,20},{12,17},{13,21},{16,8},{... | collective-permute-start | bytes 688136 | tf_op jit(solution)/shard_map/ppermute | solution.py:556
  13.1 4.1 %collective-permute-start = (f32[2,51,32]{1,2,0:T(8,128)S(1)}, f32[2,51,32]{1,2,0:T(8,128)S(1)}, u32[]{:S(2)}, u32[]{:S(2)}) collective-permute-start(f32[2,51,32]{1,2,0:T(8,128)S(1)} %pad_maximum_fusion.1), channel_id=1, source_target_pairs={{0,4},{4,0},{1,5},{5,1},{2,6},{6,2},{3,7},{7,3},{8,12},{12,8},{9,1... | collective-permute-start | bytes 39176 | tf_op jit(solution)/shard_map/ppermute | solution.py:541
  27.4 17.4 %collective-permute-start.5 = (bf16[512,640]{1,0:T(8,128)(2,1)S(1)}, bf16[512,640]{1,0:T(8,128)(2,1)S(1)}, u32[]{:S(2)}, u32[]{:S(2)}) collective-permute-start(bf16[512,640]{1,0:T(8,128)(2,1)S(1)} %get-tuple-element.64.w0), channel_id=1, source_target_pairs={{0,1},{1,0},{2,3},{3,2},{4,5},{5,4},{6,7},{7,6},{8,9},{9,8},{10,11... | collective-permute-start | bytes 1966088 | tf_op jit(solution)/shard_map/ppermute | solution.py:541
  27.5 6.5 %collective-permute-start.19 = (bf16[512,128]{1,0:T(8,128)(2,1)}, bf16[512,128]{1,0:T(8,128)(2,1)S(1)}, u32[]{:S(2)}, u32[]{:S(2)}) collective-permute-start(bf16[512,128]{1,0:T(8,128)(2,1)} %param.33), channel_id=1, source_target_pairs={{0,0},{1,4},{4,1},{5,5},{8,8},{9,12},{12,9},{13,13},{16,16},{17,20... | collective-permute-start | bytes 393224 | tf_op jit(solution)/shard_map/ppermute | solution.py:556
  29.4 28.0 %collective-permute-start.33 = (bf16[128,2048]{1,0:T(8,128)(2,1)}, bf16[128,2048]{1,0:T(8,128)(2,1)S(1)}, u32[]{:S(2)}, u32[]{:S(2)}) collective-permute-start(bf16[128,2048]{1,0:T(8,128)(2,1)} %get-tuple-element.89), channel_id=1, source_target_pairs={{0,0},{1,4},{4,1},{5,5},{8,8},{9,12},{12,9},{13,13},{16,16},{17,20... | collective-permute-start | bytes 1572872 | tf_op jit(solution)/shard_map/ppermute | solution.py:556
  34.0 6.8 %collective-permute-start.20 = (bf16[512,128]{1,0:T(8,128)(2,1)S(1)}, bf16[512,128]{1,0:T(8,128)(2,1)S(1)}, u32[]{:S(2)}, u32[]{:S(2)}) collective-permute-start(bf16[512,128]{1,0:T(8,128)(2,1)S(1)} %collective-permute-done.19.refs_4_), channel_id=1, source_target_pairs={{0,8},{8,0},{16,24},{24,16},{1,9},{9,1},{17,25},{25,17},{2,10},{10... | collective-permute-start | bytes 393224 | tf_op jit(solution)/shard_map/ppermute | solution.py:568
  37.5 7.3 %collective-permute-start.21 = (bf16[512,128]{1,0:T(8,128)(2,1)S(1)}, bf16[512,128]{1,0:T(8,128)(2,1)S(1)}, u32[]{:S(2)}, u32[]{:S(2)}) collective-permute-start(bf16[512,128]{1,0:T(8,128)(2,1)S(1)} %collective-permute-done.19.refs_4_), channel_id=1, source_target_pairs={{0,16},{8,24},{16,0},{24,8},{1,17},{9,25},{17,1},{25,9},{2,18},{10... | collective-permute-start | bytes 393224 | tf_op jit(solution)/shard_map/ppermute | solution.py:568
  38.5 15.4 %collective-permute-start.6 = (bf16[512,256]{1,0:T(8,128)(2,1)S(1)}, bf16[512,256]{1,0:T(8,128)(2,1)S(1)}, u32[]{:S(2)}, u32[]{:S(2)}) collective-permute-start(bf16[512,256]{1,0:T(8,128)(2,1)S(1)} %get-tuple-element.68.refs_0_), channel_id=1, source_target_pairs={{0,4},{2,6},{4,0},{6,2},{1,5},{3,7},{5,1},{7,3},{8,12},{10,14},{12... | collective-permute-start | bytes 786440 | tf_op jit(solution)/shard_map/ppermute | solution.py:547
  40.7 15.2 %collective-permute-start.7 = (bf16[512,256]{1,0:T(8,128)(2,1)S(1)}, bf16[512,256]{1,0:T(8,128)(2,1)S(1)}, u32[]{:S(2)}, u32[]{:S(2)}) collective-permute-start(bf16[512,256]{1,0:T(8,128)(2,1)S(1)} %get-tuple-element.68.refs_0_), channel_id=1, source_target_pairs={{0,2},{2,0},{4,6},{6,4},{1,3},{3,1},{5,7},{7,5},{8,10},{10,8},{12,... | collective-permute-start | bytes 786440 | tf_op jit(solution)/shard_map/ppermute | solution.py:547
  44.8 12.6 %collective-permute-start.8 = (bf16[512,256]{1,0:T(8,128)(2,1)S(1)}, bf16[512,256]{1,0:T(8,128)(2,1)S(1)}, u32[]{:S(2)}, u32[]{:S(2)}) collective-permute-start(bf16[512,256]{1,0:T(8,128)(2,1)S(1)} %get-tuple-element.68.refs_0_), channel_id=1, source_target_pairs={{0,6},{2,4},{4,2},{6,0},{1,7},{3,5},{5,3},{7,1},{8,14},{10,12},{12... | collective-permute-start | bytes 786440 | tf_op jit(solution)/shard_map/ppermute | solution.py:547
  44.8 9.0 %collective-permute-start.22 = (bf16[512,128]{1,0:T(8,128)(2,1)S(1)}, bf16[512,128]{1,0:T(8,128)(2,1)S(1)}, u32[]{:S(2)}, u32[]{:S(2)}) collective-permute-start(bf16[512,128]{1,0:T(8,128)(2,1)S(1)} %collective-permute-done.19.refs_4_), channel_id=1, source_target_pairs={{0,24},{8,16},{16,8},{24,0},{1,25},{9,17},{17,9},{25,1},{2,26},{10... | collective-permute-start | bytes 393224 | tf_op jit(solution)/shard_map/ppermute | solution.py:568
  53.8 10.0 %collective-permute-start.9 = (bf16[512,256]{1,0:T(8,128)(2,1)S(1)}, bf16[512,256]{1,0:T(8,128)(2,1)S(1)}, u32[]{:S(2)}, u32[]{:S(2)}) collective-permute-start(bf16[512,256]{1,0:T(8,128)(2,1)S(1)} %get-tuple-element.68.refs_0_), channel_id=1, source_target_pairs={{0,1},{1,0},{2,3},{3,2},{4,5},{5,4},{6,7},{7,6},{8,9},{9,8},{10,11... | collective-permute-start | bytes 786440 | tf_op jit(solution)/shard_map/ppermute | solution.py:541
  53.9 4.8 %collective-permute-start.13 = (bf16[50,640]{1,0:T(8,128)(2,1)S(1)}, bf16[50,640]{1,0:T(8,128)(2,1)S(1)}, u32[]{:S(2)}, u32[]{:S(2)}) collective-permute-start(bf16[50,640]{1,0:T(8,128)(2,1)S(1)} %get-tuple-element.72), channel_id=1, source_target_pairs={{0,4},{2,6},{4,0},{6,2},{1,5},{3,7},{5,1},{7,3},{8,12},{10,14},{12... | collective-permute-start | bytes 192008 | tf_op jit(solution)/shard_map/ppermute | solution.py:547
  55.9 4.5 %collective-permute-start.14 = (bf16[50,640]{1,0:T(8,128)(2,1)S(1)}, bf16[50,640]{1,0:T(8,128)(2,1)S(1)}, u32[]{:S(2)}, u32[]{:S(2)}) collective-permute-start(bf16[50,640]{1,0:T(8,128)(2,1)S(1)} %get-tuple-element.73), channel_id=1, source_target_pairs={{0,2},{2,0},{4,6},{6,4},{1,3},{3,1},{5,7},{7,5},{8,10},{10,8},{12,... | collective-permute-start | bytes 192008 | tf_op jit(solution)/shard_map/ppermute | solution.py:547
  57.4 5.5 %collective-permute-start.23 = (bf16[512,128]{1,0:T(8,128)(2,1)S(1)}, bf16[512,128]{1,0:T(8,128)(2,1)S(1)}, u32[]{:S(2)}, u32[]{:S(2)}) collective-permute-start(bf16[512,128]{1,0:T(8,128)(2,1)S(1)} %collective-permute-done.19.refs_4_), channel_id=1, source_target_pairs={{0,1},{1,0},{2,3},{3,2},{4,5},{5,4},{6,7},{7,6},{8,9},{9,8},{10,11... | collective-permute-start | bytes 393224 | tf_op jit(solution)/shard_map/ppermute | solution.py:541
  57.4 5.5 %collective-permute-start.15 = (bf16[50,640]{1,0:T(8,128)(2,1)S(1)}, bf16[50,640]{1,0:T(8,128)(2,1)S(1)}, u32[]{:S(2)}, u32[]{:S(2)}) collective-permute-start(bf16[50,640]{1,0:T(8,128)(2,1)S(1)} %get-tuple-element.74), channel_id=1, source_target_pairs={{0,6},{2,4},{4,2},{6,0},{1,7},{3,5},{5,3},{7,1},{8,14},{10,12},{12... | collective-permute-start | bytes 192008 | tf_op jit(solution)/shard_map/ppermute | solution.py:547
  58.7 4.7 %collective-permute-start.24 = (bf16[512,128]{1,0:T(8,128)(2,1)S(1)}, bf16[512,128]{1,0:T(8,128)(2,1)S(1)}, u32[]{:S(2)}, u32[]{:S(2)}) collective-permute-start(bf16[512,128]{1,0:T(8,128)(2,1)S(1)} %collective-permute-done.20.refs_5_), channel_id=1, source_target_pairs={{0,1},{1,0},{2,3},{3,2},{4,5},{5,4},{6,7},{7,6},{8,9},{9,8},{10,11... | collective-permute-start | bytes 393224 | tf_op jit(solution)/shard_map/ppermute | solution.py:541
  60.5 4.1 %collective-permute-start.10 = (bf16[512,256]{1,0:T(8,128)(2,1)S(1)}, bf16[512,256]{1,0:T(8,128)(2,1)S(1)}, u32[]{:S(2)}, u32[]{:S(2)}) collective-permute-start(bf16[512,256]{1,0:T(8,128)(2,1)S(1)} %collective-permute-done.6.refs_1_), channel_id=1, source_target_pairs={{0,1},{1,0},{2,3},{3,2},{4,5},{5,4},{6,7},{7,6},{8,9},{9,8},{10,11... | collective-permute-start | bytes 786440 | tf_op jit(solution)/shard_map/ppermute | solution.py:541
  63.0 4.1 %collective-permute-start.12 = (bf16[512,256]{1,0:T(8,128)(2,1)S(1)}, bf16[512,256]{1,0:T(8,128)(2,1)S(1)}, u32[]{:S(2)}, u32[]{:S(2)}) collective-permute-start(bf16[512,256]{1,0:T(8,128)(2,1)S(1)} %collective-permute-done.8.refs_3_), channel_id=1, source_target_pairs={{0,1},{1,0},{2,3},{3,2},{4,5},{5,4},{6,7},{7,6},{8,9},{9,8},{10,11... | collective-permute-start | bytes 786440 | tf_op jit(solution)/shard_map/ppermute | solution.py:541
  63.5 22.5 %collective-permute-start.34 = (bf16[128,2048]{1,0:T(8,128)(2,1)S(1)}, bf16[128,2048]{1,0:T(8,128)(2,1)S(1)}, u32[]{:S(2)}, u32[]{:S(2)}) collective-permute-start(bf16[128,2048]{1,0:T(8,128)(2,1)S(1)} %collective-permute-done.33.refs_4_.refs_12_), channel_id=1, source_target_pairs={{0,8},{8,0},{16,24},{24,16},{1,9},{9,1},{17,25},{25,17},{2,10},{10... | collective-permute-start | bytes 1572872 | tf_op jit(solution)/shard_map/ppermute | solution.py:568
  63.8 25.3 %collective-permute-start.36 = (bf16[128,2048]{1,0:T(8,128)(2,1)S(1)}, bf16[128,2048]{1,0:T(8,128)(2,1)S(1)}, u32[]{:S(2)}, u32[]{:S(2)}) collective-permute-start(bf16[128,2048]{1,0:T(8,128)(2,1)S(1)} %collective-permute-done.33.refs_4_.refs_12_), channel_id=1, source_target_pairs={{8,16},{16,8},{9,17},{17,9},{10,18},{18,10},{11,19},{19,11},{12,20... | collective-permute-start | bytes 1572872 | tf_op jit(solution)/shard_map/ppermute | solution.py:568
  64.5 20.7 %collective-permute-start.43 = (bf16[1024,128]{1,0:T(8,128)(2,1)S(1)}, bf16[1024,128]{1,0:T(8,128)(2,1)S(1)}, u32[]{:S(2)}, u32[]{:S(2)}) collective-permute-start(bf16[1024,128]{1,0:T(8,128)(2,1)S(1)} %copy-done.9), channel_id=1, source_target_pairs={{0,0},{1,4},{4,1},{5,5},{8,8},{9,12},{12,9},{13,13},{16,16},{17,20... | collective-permute-start | bytes 786440 | tf_op jit(solution)/shard_map/ppermute | solution.py:556
  66.9 5.7 %collective-permute-start.25 = (bf16[512,128]{1,0:T(8,128)(2,1)S(1)}, bf16[512,128]{1,0:T(8,128)(2,1)S(1)}, u32[]{:S(2)}, u32[]{:S(2)}) collective-permute-start(bf16[512,128]{1,0:T(8,128)(2,1)S(1)} %collective-permute-done.21.refs_6_), channel_id=1, source_target_pairs={{0,1},{1,0},{2,3},{3,2},{4,5},{5,4},{6,7},{7,6},{8,9},{9,8},{10,11... | collective-permute-start | bytes 393224 | tf_op jit(solution)/shard_map/ppermute | solution.py:541
  67.0 6.9 %collective-permute-start.26 = (bf16[512,128]{1,0:T(8,128)(2,1)S(1)}, bf16[512,128]{1,0:T(8,128)(2,1)S(1)}, u32[]{:S(2)}, u32[]{:S(2)}) collective-permute-start(bf16[512,128]{1,0:T(8,128)(2,1)S(1)} %collective-permute-done.22.refs_7_), channel_id=1, source_target_pairs={{0,1},{1,0},{2,3},{3,2},{4,5},{5,4},{6,7},{7,6},{8,9},{9,8},{10,11... | collective-permute-start | bytes 393224 | tf_op jit(solution)/shard_map/ppermute | solution.py:541
  72.6 4.2 %collective-permute-start.16 = (bf16[50,512]{1,0:T(8,128)(2,1)S(1)}, bf16[50,512]{1,0:T(8,128)(2,1)S(1)}, u32[]{:S(2)}, u32[]{:S(2)}) collective-permute-start(bf16[50,512]{1,0:T(8,128)(2,1)S(1)} %get-tuple-element.76), channel_id=1, source_target_pairs={{0,4},{2,6},{4,0},{6,2},{1,5},{3,7},{5,1},{7,3},{8,12},{10,14},{12... | collective-permute-start | bytes 153608 | tf_op jit(solution)/shard_map/ppermute | solution.py:547
  73.9 5.2 %collective-permute-start.17 = (bf16[50,512]{1,0:T(8,128)(2,1)S(1)}, bf16[50,512]{1,0:T(8,128)(2,1)S(1)}, u32[]{:S(2)}, u32[]{:S(2)}) collective-permute-start(bf16[50,512]{1,0:T(8,128)(2,1)S(1)} %get-tuple-element.77), channel_id=1, source_target_pairs={{0,2},{2,0},{4,6},{6,4},{1,3},{3,1},{5,7},{7,5},{8,10},{10,8},{12,... | collective-permute-start | bytes 153608 | tf_op jit(solution)/shard_map/ppermute | solution.py:547
  76.8 5.1 %collective-permute-start.18 = (bf16[50,512]{1,0:T(8,128)(2,1)S(1)}, bf16[50,512]{1,0:T(8,128)(2,1)S(1)}, u32[]{:S(2)}, u32[]{:S(2)}) collective-permute-start(bf16[50,512]{1,0:T(8,128)(2,1)S(1)} %get-tuple-element.78), channel_id=1, source_target_pairs={{0,6},{2,4},{4,2},{6,0},{1,7},{3,5},{5,3},{7,1},{8,14},{10,12},{12... | collective-permute-start | bytes 153608 | tf_op jit(solution)/shard_map/ppermute | solution.py:547
  82.4 7.6 %collective-permute-start.29 = (bf16[50,1024]{1,0:T(8,128)(2,1)S(1)}, bf16[50,1024]{1,0:T(8,128)(2,1)S(1)}, u32[]{:S(2)}, u32[]{:S(2)}) collective-permute-start(bf16[50,1024]{1,0:T(8,128)(2,1)S(1)} %get-tuple-element.87), channel_id=1, source_target_pairs={{0,6},{2,4},{4,2},{6,0},{1,7},{3,5},{5,3},{7,1},{8,14},{10,12},{12... | collective-permute-start | bytes 307208 | tf_op jit(solution)/shard_map/ppermute | solution.py:547
  84.7 6.8 %collective-permute-start.28 = (bf16[50,1024]{1,0:T(8,128)(2,1)S(1)}, bf16[50,1024]{1,0:T(8,128)(2,1)S(1)}, u32[]{:S(2)}, u32[]{:S(2)}) collective-permute-start(bf16[50,1024]{1,0:T(8,128)(2,1)S(1)} %get-tuple-element.86), channel_id=1, source_target_pairs={{0,2},{2,0},{4,6},{6,4},{1,3},{3,1},{5,7},{7,5},{8,10},{10,8},{12,... | collective-permute-start | bytes 307208 | tf_op jit(solution)/shard_map/ppermute | solution.py:547
  85.2 7.6 %collective-permute-start.27 = (bf16[50,1024]{1,0:T(8,128)(2,1)S(1)}, bf16[50,1024]{1,0:T(8,128)(2,1)S(1)}, u32[]{:S(2)}, u32[]{:S(2)}) collective-permute-start(bf16[50,1024]{1,0:T(8,128)(2,1)S(1)} %get-tuple-element.85), channel_id=1, source_target_pairs={{0,4},{2,6},{4,0},{6,2},{1,5},{3,7},{5,1},{7,3},{8,12},{10,14},{12... | collective-permute-start | bytes 307208 | tf_op jit(solution)/shard_map/ppermute | solution.py:547
  86.0 20.8 %collective-permute-start.44 = (bf16[1024,128]{1,0:T(8,128)(2,1)S(1)}, bf16[1024,128]{1,0:T(8,128)(2,1)S(1)}, u32[]{:S(2)}, u32[]{:S(2)}) collective-permute-start(bf16[1024,128]{1,0:T(8,128)(2,1)S(1)} %collective-permute-done.43.refs_20_), channel_id=1, source_target_pairs={{0,8},{8,0},{16,24},{24,16},{1,9},{9,1},{17,25},{25,17},{2,10},{10... | collective-permute-start | bytes 786440 | tf_op jit(solution)/shard_map/ppermute | solution.py:568
  89.1 17.6 %collective-permute-start.45 = (bf16[1024,128]{1,0:T(8,128)(2,1)S(1)}, bf16[1024,128]{1,0:T(8,128)(2,1)S(1)}, u32[]{:S(2)}, u32[]{:S(2)}) collective-permute-start(bf16[1024,128]{1,0:T(8,128)(2,1)S(1)} %collective-permute-done.43.refs_20_), channel_id=1, source_target_pairs={{0,16},{8,24},{16,0},{24,8},{1,17},{9,25},{17,1},{25,9},{2,18},{10... | collective-permute-start | bytes 786440 | tf_op jit(solution)/shard_map/ppermute | solution.py:568
  90.0 8.7 %collective-permute-start.35 = (bf16[128,2048]{1,0:T(8,128)(2,1)S(1)}, bf16[128,2048]{1,0:T(8,128)(2,1)}, u32[]{:S(2)}, u32[]{:S(2)}) collective-permute-start(bf16[128,2048]{1,0:T(8,128)(2,1)S(1)} %collective-permute-done.34.refs_5_.refs_13_), channel_id=1, source_target_pairs={{8,16},{16,8},{9,17},{17,9},{10,18},{18,10},{11,19},{19,11},{12,20... | collective-permute-start | bytes 1572872 | tf_op jit(solution)/shard_map/ppermute | solution.py:568
  91.5 24.3 %collective-permute-start.37 = (bf16[128,2048]{1,0:T(8,128)(2,1)S(1)}, bf16[128,2048]{1,0:T(8,128)(2,1)}, u32[]{:S(2)}, u32[]{:S(2)}) collective-permute-start(bf16[128,2048]{1,0:T(8,128)(2,1)S(1)} %collective-permute-done.36), channel_id=1, source_target_pairs={{8,0},{16,24},{9,1},{17,25},{10,2},{18,26},{11,3},{19,27},{12,4},{... | collective-permute-start | bytes 1572872 | tf_op jit(solution)/shard_map/ppermute | solution.py:568
  93.1 4.9 %collective-permute-start.30 = (bf16[50,1024]{1,0:T(8,128)(2,1)S(1)}, bf16[50,1024]{1,0:T(8,128)(2,1)S(1)}, u32[]{:S(2)}, u32[]{:S(2)}) collective-permute-start(bf16[50,1024]{1,0:T(8,128)(2,1)S(1)} %multiply_convert_fusion.refs_0_), channel_id=1, source_target_pairs={{0,4},{2,6},{4,0},{6,2},{1,5},{3,7},{5,1},{7,3},{8,12},{10,14},{12... | collective-permute-start | bytes 307208 | tf_op jit(solution)/shard_map/ppermute | solution.py:547
  98.0 4.8 %collective-permute-start.31 = (bf16[50,1024]{1,0:T(8,128)(2,1)S(1)}, bf16[50,1024]{1,0:T(8,128)(2,1)S(1)}, u32[]{:S(2)}, u32[]{:S(2)}) collective-permute-start(bf16[50,1024]{1,0:T(8,128)(2,1)S(1)} %multiply_convert_fusion.refs_0_), channel_id=1, source_target_pairs={{0,2},{2,0},{4,6},{6,4},{1,3},{3,1},{5,7},{7,5},{8,10},{10,8},{12,... | collective-permute-start | bytes 307208 | tf_op jit(solution)/shard_map/ppermute | solution.py:547
  98.8 6.4 %collective-permute-start.32 = (bf16[50,1024]{1,0:T(8,128)(2,1)S(1)}, bf16[50,1024]{1,0:T(8,128)(2,1)S(1)}, u32[]{:S(2)}, u32[]{:S(2)}) collective-permute-start(bf16[50,1024]{1,0:T(8,128)(2,1)S(1)} %multiply_convert_fusion.refs_0_), channel_id=1, source_target_pairs={{0,6},{2,4},{4,2},{6,0},{1,7},{3,5},{5,3},{7,1},{8,14},{10,12},{12... | collective-permute-start | bytes 307208 | tf_op jit(solution)/shard_map/ppermute | solution.py:547
  102.8 28.8 %collective-permute-start.38 = (bf16[128,2048]{1,0:T(8,128)(2,1)}, bf16[128,2048]{1,0:T(8,128)(2,1)}, u32[]{:S(2)}, u32[]{:S(2)}) collective-permute-start(bf16[128,2048]{1,0:T(8,128)(2,1)} %collective-permute-done.35), channel_id=1, source_target_pairs={{8,0},{16,24},{9,1},{17,25},{10,2},{18,26},{11,3},{19,27},{12,4},{... | collective-permute-start | bytes 1572872 | tf_op jit(solution)/shard_map/ppermute | solution.py:568
  105.2 27.5 %collective-permute-start.46 = (bf16[1024,128]{1,0:T(8,128)(2,1)S(1)}, bf16[1024,128]{1,0:T(8,128)(2,1)S(1)}, u32[]{:S(2)}, u32[]{:S(2)}) collective-permute-start(bf16[1024,128]{1,0:T(8,128)(2,1)S(1)} %collective-permute-done.43.refs_20_), channel_id=1, source_target_pairs={{0,24},{8,16},{16,8},{24,0},{1,25},{9,17},{17,9},{25,1},{2,26},{10... | collective-permute-start | bytes 786440 | tf_op jit(solution)/shard_map/ppermute | solution.py:568
  106.7 30.0 %collective-permute-start.39 = (bf16[128,2048]{1,0:T(8,128)(2,1)S(1)}, bf16[128,2048]{1,0:T(8,128)(2,1)S(1)}, u32[]{:S(2)}, u32[]{:S(2)}) collective-permute-start(bf16[128,2048]{1,0:T(8,128)(2,1)S(1)} %collective-permute-done.33.refs_4_.refs_12_), channel_id=1, source_target_pairs={{0,1},{1,0},{2,3},{3,2},{4,5},{5,4},{6,7},{7,6},{8,9},{9,8},{10,11... | collective-permute-start | bytes 1572872 | tf_op jit(solution)/shard_map/ppermute | solution.py:541
  106.7 26.5 %collective-permute-start.47 = (bf16[1024,128]{1,0:T(8,128)(2,1)S(1)}, bf16[1024,128]{1,0:T(8,128)(2,1)S(1)}, u32[]{:S(2)}, u32[]{:S(2)}) collective-permute-start(bf16[1024,128]{1,0:T(8,128)(2,1)S(1)} %collective-permute-done.43.refs_20_), channel_id=1, source_target_pairs={{0,1},{1,0},{2,3},{3,2},{4,5},{5,4},{6,7},{7,6},{8,9},{9,8},{10,11... | collective-permute-start | bytes 786440 | tf_op jit(solution)/shard_map/ppermute | solution.py:541
  115.8 17.6 %collective-permute-start.48 = (bf16[1024,128]{1,0:T(8,128)(2,1)S(1)}, bf16[1024,128]{1,0:T(8,128)(2,1)S(1)}, u32[]{:S(2)}, u32[]{:S(2)}) collective-permute-start(bf16[1024,128]{1,0:T(8,128)(2,1)S(1)} %collective-permute-done.44.refs_21_), channel_id=1, source_target_pairs={{0,1},{1,0},{2,3},{3,2},{4,5},{5,4},{6,7},{7,6},{8,9},{9,8},{10,11... | collective-permute-start | bytes 786440 | tf_op jit(solution)/shard_map/ppermute | solution.py:541
  140.6 5.5 %collective-permute-start.51 = (bf16[50,1024]{1,0:T(8,128)(2,1)S(1)}, bf16[50,1024]{1,0:T(8,128)(2,1)S(1)}, u32[]{:S(2)}, u32[]{:S(2)}) collective-permute-start(bf16[50,1024]{1,0:T(8,128)(2,1)S(1)} %get-tuple-element.106), channel_id=1, source_target_pairs={{0,4},{2,6},{4,0},{6,2},{1,5},{3,7},{5,1},{7,3},{8,12},{10,14},{12... | collective-permute-start | bytes 307208 | tf_op jit(solution)/shard_map/ppermute | solution.py:547
  141.0 5.6 %collective-permute-start.52 = (bf16[50,1024]{1,0:T(8,128)(2,1)S(1)}, bf16[50,1024]{1,0:T(8,128)(2,1)S(1)}, u32[]{:S(2)}, u32[]{:S(2)}) collective-permute-start(bf16[50,1024]{1,0:T(8,128)(2,1)S(1)} %get-tuple-element.107), channel_id=1, source_target_pairs={{0,2},{2,0},{4,6},{6,4},{1,3},{3,1},{5,7},{7,5},{8,10},{10,8},{12,... | collective-permute-start | bytes 307208 | tf_op jit(solution)/shard_map/ppermute | solution.py:547
  142.1 7.6 %collective-permute-start.53 = (bf16[50,1024]{1,0:T(8,128)(2,1)S(1)}, bf16[50,1024]{1,0:T(8,128)(2,1)S(1)}, u32[]{:S(2)}, u32[]{:S(2)}) collective-permute-start(bf16[50,1024]{1,0:T(8,128)(2,1)S(1)} %get-tuple-element.108), channel_id=1, source_target_pairs={{0,6},{2,4},{4,2},{6,0},{1,7},{3,5},{5,3},{7,1},{8,14},{10,12},{12... | collective-permute-start | bytes 307208 | tf_op jit(solution)/shard_map/ppermute | solution.py:547
  (16 other events, 223.7 us)

commit v3 on v2

--- a/solution.py
+++ b/solution.py
@@ -318,112 +318,94 @@
     )(an, own, other)
 
 
-def normed_blocks(prefix, gain):
+def attention(prefix, gain, kv_own, kv_oth, qa, length, heads_cols):
     positions, width = prefix.shape
-    step, count = 256, 16
-    per, no = width // 16, 4
-
-    def kernel(x, g, out):
-        oo, ii, cc = (lax.axis_index(n) for n in ("o", "i", "c"))
-        v = x[...].astype(F32)
-        scale = lax.rsqrt(jnp.mean(v * v, axis=-1, keepdims=True) + 1e-06)
-        for b in range(count):
-            r, i, c = b % no, (b // no) % 2, b // (2 * no)
-            block = ((oo ^ r) * 2 + (cc ^ c)) * 2 + (ii ^ i)
-            src = pl.ds(pl.multiple_of(block * per, per), per)
-            out[:, b * per : (b + 1) * per] = (x[:, src].astype(F32) * scale * g[:, src]).astype(BF)
-
+    tall, hd = kv_own[0].shape
+    span, _ = qa[0].shape
+    per_part = heads_cols // hd
+    heads = len(RELS) * per_part
+    step = 512 if positions % 512 == 0 else 256
+    steps = positions // step
+    count = 16
+    per, no = width // count, count // 4
+
+    def kernel(len_ref, x_hbm, g, *refs):
+        own, oth, qs = refs[0:4], refs[4:8], refs[8:12]
+        outs = refs[12:16]
+        x_all, q_all, pn, sems = refs[16:20]
+        oo, ii, xx, cc = (lax.axis_index(n) for n in ("o", "i", "x", "c"))
+        copies = [
+            pltpu.make_async_copy(
+                x_hbm.at[s * step : (s + 1) * step], x_all.at[s * step : (s + 1) * step], sems.at[s]
+            )
+            for s in range(steps)
+        ]
+        for copy in copies:
+            copy.start()
+        q_all[...] = jnp.zeros_like(q_all)
+        for k in range(len(RELS)):
+            for h in range(per_part):
+                n = PAD * (k * per_part + h)
+                q_all[n : n + span] = qs[k][:, h * hd : (h + 1) * hd]
+        first = xx == 0
+        nt = (((1,), (1,)), ((), ()))
+        parts = [q[:, heads_cols:] for q in qs]
+        flat = ii == 0
+        lo = [jnp.where(flat, parts[2 * k], parts[2 * k + 1]) for k in range(2)]
+        hi = [jnp.where(flat, parts[2 * k + 1], parts[2 * k]) for k in range(2)]
+        sa = jnp.concatenate([lo[0], hi[0]], axis=1)
+        da = jnp.concatenate([lo[1], hi[1]], axis=1)
+        ak, av = jnp.where(first, sa, da), jnp.where(first, da, sa)
+        pa = jnp.exp(lax.dot_general(q_all[...], ak, nt, preferred_element_type=F32))
+        den = jnp.sum(pa, axis=-1, keepdims=True)
+        acc = dot(pa.astype(BF), av)
+        limit = len_ref[xx * 2 + cc]
+        for s in range(steps):
+            copies[s].wait()
+            x = x_all.at[s * step : (s + 1) * step]
+            v = x[...].astype(F32)
+            scale = lax.rsqrt(jnp.mean(v * v, axis=-1, keepdims=True) + 1e-06)
+            for b in range(count):
+                r, i, c = b % no, (b // no) % 2, b // (2 * no)
+                block = ((oo ^ r) * 2 + (cc ^ c)) * 2 + (ii ^ i)
+                src = pl.ds(pl.multiple_of(block * per, per), per)
+                pn[:, b * per : (b + 1) * per] = (x[:, src].astype(F32) * scale * g[:, src]).astype(BF)
+            same = diff = 0.0
+            for c, refs_c in enumerate((own, oth)):
+                for i in range(2):
+                    m = pn[:, (c * 2 + i) * tall : (c * 2 + i + 1) * tall]
+                    same = same + dot(m, refs_c[i][...])
+                    diff = diff + dot(m, refs_c[2 + i][...])
+            same, diff = same.astype(BF), diff.astype(BF)
+            keys = jnp.where(first, same, diff)
+            vals = jnp.where(first, diff, same)
+            sc = lax.dot_general(q_all[...], keys, nt, preferred_element_type=F32)
+            spot = s * step + lax.broadcasted_iota(jnp.int32, sc.shape, 1)
+            p = jnp.where(spot < limit, jnp.exp(sc), 0.0)
+            den = den + jnp.sum(p, axis=-1, keepdims=True)
+            acc = acc + dot(p.astype(BF), vals)
+        res = (acc / den).astype(BF)
+        for k in range(len(RELS)):
+            for h in range(per_part):
+                n = PAD * (k * per_part + h)
+                outs[k][:, h * hd : (h + 1) * hd] = res[n : n + span]
+
+    vmem = pl.BlockSpec(memory_space=pltpu.VMEM)
     return pl.pallas_call(
         kernel,
-        grid=(positions // step,),
-        out_shape=like(positions, width),
-        in_specs=[pl.BlockSpec((step, width), lambda s: (s, 0)), at(1, width)],
-        out_specs=pl.BlockSpec((step, width), lambda s: (s, 0)),
-        name="normed_blocks",
-        compiler_params=grant(16),
-    )(prefix, gain.reshape(1, width))
-
-
-def attention(prefix, kv_own, kv_oth, qa, length, heads_cols):
-    positions, width = prefix.shape
-    tall, hd = kv_own[0].shape
-    span, qa_cols = qa[0].shape
-    per_part = heads_cols // hd
-    heads = len(RELS) * per_part
-    step = 512
-    steps = positions // step
-
-    def kernel(len_ref, pn, *refs):
-        own, oth, qs = refs[0:4], refs[4:8], refs[8:12]
-        outs = refs[12:16]
-        q_all, acc, den = refs[16:19]
-        s = pl.program_id(0)
-        ii, xx = lax.axis_index("i"), lax.axis_index("x")
-
-        @pl.when(s == 0)
-        def _():
-            q_all[...] = jnp.zeros_like(q_all)
-            for k in range(len(RELS)):
-                for h in range(per_part):
-                    q_all[PAD * (k * per_part + h) : PAD * (k * per_part + h) + span] = qs[k][
-                        :, h * hd : (h + 1) * hd
-                    ]
-            acc[...] = jnp.zeros_like(acc)
-            den[...] = jnp.zeros_like(den)
-
-        same = diff = 0.0
-        for c, refs_c in enumerate((own, oth)):
-            for i in range(2):
-                m = pn[:, (c * 2 + i) * tall : (c * 2 + i + 1) * tall]
-                same = same + dot(m, refs_c[i][...])
-                diff = diff + dot(m, refs_c[2 + i][...])
-        first = xx == 0
-        same, diff = same.astype(BF), diff.astype(BF)
-        keys = jnp.where(first, same, diff)
-        vals = jnp.where(first, diff, same)
-        nt = (((1,), (1,)), ((), ()))
-        sc = lax.dot_general(q_all[...], keys, nt, preferred_element_type=F32)
-        spot = s * step + lax.broadcasted_iota(jnp.int32, sc.shape, 1)
-        p = jnp.where(spot < len_ref[lax.axis_index("x") * 2 + lax.axis_index("c")], jnp.exp(sc), 0.0)
-        den[...] += jnp.sum(p, axis=-1, keepdims=True)
-        acc[...] += dot(p.astype(BF), vals)
-
-        @pl.when(s == steps - 1)
-        def _():
-            parts = [q[:, heads_cols:] for q in qs]
-            flat = ii == 0
-            lo = [jnp.where(flat, parts[2 * k], parts[2 * k + 1]) for k in range(2)]
-            hi = [jnp.where(flat, parts[2 * k + 1], parts[2 * k]) for k in range(2)]
-            sa = jnp.concatenate([lo[0], hi[0]], axis=1)
-            da = jnp.concatenate([lo[1], hi[1]], axis=1)
-            ak, av = jnp.where(first, sa, da), jnp.where(first, da, sa)
-            pa = jnp.exp(lax.dot_general(q_all[...], ak, nt, preferred_element_type=F32))
-            total = den[...] + jnp.sum(pa, axis=-1, keepdims=True)
-            res = ((acc[...] + dot(pa.astype(BF), av)) / total).astype(BF)
-            for k in range(len(RELS)):
-                for h in range(per_part):
-                    n = PAD * (k * per_part + h)
-                    outs[k][:, h * hd : (h + 1) * hd] = res[n : n + span]
-
-    return pl.pallas_call(
-        kernel,
-        grid=(steps,),
         out_shape=[like(span, heads_cols) for _ in RELS],
-        in_specs=[
-            pl.BlockSpec(memory_space=pltpu.SMEM),
-            pl.BlockSpec((step, width), lambda s: (s, 0)),
-        ]
-        + [at(tall, hd)] * 8
-        + [at(span, qa_cols)] * 4,
-        out_specs=[at(span, heads_cols)] * 4,
+        in_specs=[pl.BlockSpec(memory_space=pltpu.SMEM), pl.BlockSpec(memory_space=pltpu.HBM)]
+        + [vmem] * 13,
+        out_specs=[vmem] * 4,
         scratch_shapes=[
+            pltpu.VMEM((positions, width), BF),
             pltpu.VMEM((PAD * heads, hd), BF),
-            pltpu.VMEM((PAD * heads, hd), F32),
-            pltpu.VMEM((PAD * heads, 1), F32),
+            pltpu.VMEM((step, width), BF),
+            pltpu.SemaphoreType.DMA((steps,)),
         ],
         name="prefix_attention",
-        compiler_params=grant(24),
-    )(length, prefix, *kv_own, *kv_oth, *qa)
+        compiler_params=grant(28),
+    )(length, prefix, gain.reshape(1, width), *kv_own, *kv_oth, *qa)
 
 
 def row_outs(rows, width, parts):
@@ -462,52 +444,46 @@
     )(*attn, *pieces)
 
 
-def feed_forward(mn, gu, od, units):
-    rows = mn[0].shape[0]
-    parts, count = len(mn), len(gu)
-    per, cols = gu[0].shape[0], od[0].shape[1]
+def feed_forward(mn, gu_own, gu_oth, down, units):
+    rows, parts = mn[0].shape[0], len(mn)
+    count, per, cols = len(down), gu_own[0].shape[0], down[0].shape[1]
     step = 256
-    steps = units // step
 
     def kernel(*refs):
         m_refs, refs = refs[:parts], refs[parts:]
-        g_refs, u_refs, d_refs = refs[:count], refs[count : 2 * count], refs[2 * count : 3 * count]
-        outs, m_all, total = refs[3 * count : -2], refs[-2], refs[-1]
-        s = pl.program_id(0)
-
-        @pl.when(s == 0)
-        def _():
+        own, oth, d_refs = refs[:6], refs[6:12], refs[12 : 12 + count]
+        outs, m_all = refs[12 + count : -1], refs[-1]
+        oo = lax.axis_index("o")
+        inner = (oo == 1) | (oo == 2)
+        for k in range(parts):
+            m_all[PAD * k : PAD * k + rows] = m_refs[k][...]
+        m = m_all[...]
+
+        def stacked(u):
+            blocks = []
+            for t, a, b, c, d, e in (own, oth):
+                t, a, b, c, d, e = (w[:, u : u + step] for w in (t, a, b, c, d, e))
+                blocks += [t, a, jnp.where(inner, d, c), jnp.where(inner, b, e)]
+            return jnp.concatenate(blocks, axis=0)
+
+        hid = []
+        for u in range(0, units, step):
+            gate, up = dot(m, stacked(u)), dot(m, stacked(units + u))
+            hid.append((jax.nn.gelu(gate, approximate=True) * up).astype(BF))
+        hid = jnp.concatenate(hid, axis=1)
+        for b in range(0, count, 2):
+            total = dot(hid, jnp.concatenate([d_refs[b][...], d_refs[b + 1][...]], axis=1))
             for k in range(parts):
-                m_all[PAD * k : PAD * k + rows] = m_refs[k][...]
-            total[...] = jnp.zeros_like(total)
-
-        gate = dot(m_all[...], jnp.concatenate([g[...] for g in g_refs], axis=0))
-        up = dot(m_all[...], jnp.concatenate([u[...] for u in u_refs], axis=0))
-        hid = (jax.nn.gelu(gate, approximate=True) * up).astype(BF)
-        for b in range(0, count, 2):
-            pair = jnp.concatenate([d_refs[b][...], d_refs[b + 1][...]], axis=1)
-            total[:, b * cols : (b + 2) * cols] += dot(hid, pair)
-
-        @pl.when(s == steps - 1)
-        def _():
-            split_rows(total, rows, outs)
+                part = total[PAD * k : PAD * k + rows]
+                outs[k][:, b * cols : (b + 2) * cols] = part.astype(outs[k].dtype)
 
     return pl.pallas_call(
         kernel,
-        grid=(steps,),
         out_shape=row_outs(rows, count * cols, parts),
-        in_specs=[at(rows, count * per)] * parts
-        + [pl.BlockSpec((per, step), lambda s: (0, s))] * count
-        + [pl.BlockSpec((per, step), lambda s: (0, s + steps))] * count
-        + [pl.BlockSpec((step, cols), lambda s: (s, 0))] * count,
-        out_specs=[at(rows, count * cols)] * parts,
-        scratch_shapes=[
-            pltpu.VMEM((PAD * parts, count * per), BF),
-            pltpu.VMEM((PAD * parts, count * cols), F32),
-        ],
+        scratch_shapes=[pltpu.VMEM((PAD * parts, count * per), BF)],
         name="feed_forward",
-        compiler_params=grant(20),
-    )(*mn, *gu, *gu, *od)
+        compiler_params=grant(24),
+    )(*mn, *gu_own, *gu_oth, *down)
 
 
 def velocity_and_loss(h1, parts, gains, head_p, noise, actions):
@@ -600,7 +576,7 @@
         hd = key_weight.shape[1]
         heads_cols = query_w.shape[1]
         units = gate_w.shape[1]
-        oo, xx, cc = (lax.axis_index(a) for a in ("o", "x", "c"))
+        xx, cc = (lax.axis_index(a) for a in ("x", "c"))
 
         def order(first, second, at_one):
             return jnp.where(at_one == 0, first, second), jnp.where(at_one == 0, second, first)
@@ -656,34 +632,40 @@
         qa_oth = flip(qa_own, "c")
         q_parts = queries(an, qa_own, qa_oth, heads_cols, hd ** (-0.5), span)
         qa = exchange(q_parts)
-        pn = normed_blocks(
-            after(prefix_hidden, q_parts[0]).reshape(positions, width), prefix_gain
-        )
         gu_c, gu_d = hop(after(gu_b, q_parts[0]), OUTWARD), hop(after(gu_a, q_parts[0]), MIDDLE)
         down_t = after(down_0, q_parts[0])
         down_got = [down_t] + [hop(down_t, partner(r)) for r in range(1, no)]
-        kv_all = [after(t, pn) for t in kv_all]
+        kv_all = [after(t, *qa) for t in kv_all]
         kv_oth = [flip(t, "c") for t in kv_all]
-        attn = attention(pn, kv_all, kv_oth, qa, prefix_len, heads_cols)
+        attn = attention(
+            prefix_hidden.reshape(positions, width),
+            prefix_gain,
+            kv_all,
+            kv_oth,
+            qa,
+            prefix_len,
+            heads_cols,
+        )
 
         attn_in = exchange(attn)
         gu_e = hop(after(gu_d, attn[0]), OUTWARD)
-        out_all = out_got + [flip(after(t, pn), "c") for t in out_got]
+        out_all = out_got + [flip(after(t, attn[0]), "c") for t in out_got]
+        gu_early = [after(t, attn[0]) for t in (gu_t, gu_a, gu_b)]
+        early_oth = [flip(t, "c") for t in gu_early]
         out_parts = out_project(attn_in, out_all, heads_cols)
         out_in = exchange(out_parts)
+        gu_mid = [after(t, out_parts[0]) for t in (gu_c, gu_d)]
+        mid_oth = [flip(t, "c") for t in gu_mid]
         h1 = h0 + sum(t.astype(F32) for t in out_in)
 
         mn = spread(rms(h1, gains[0]).astype(BF))
-        inner = (oo == 1) | (oo == 2)
-        gu_t, gu_a, gu_b, gu_c, gu_d = (
-            after(t, out_parts[0]) for t in (gu_t, gu_a, gu_b, gu_c, gu_d)
-        )
-        gu_e = after(gu_e, *mn)
-        gu_got = [gu_t, gu_a, jnp.where(inner, gu_d, gu_c), jnp.where(inner, gu_b, gu_e)]
-        gu_all = gu_got + [flip(t, "c") for t in gu_got]
-        down_got = [after(t, *mn) for t in down_got]
-        down_all = down_got + [flip(t, "c") for t in down_got]
-        ff_parts = feed_forward(mn, gu_all, down_all, units)
+        down_got = [after(t, h1) for t in down_got]
+        down_oth = [flip(t, "c") for t in down_got]
+        gu_e = after(gu_e, *mn, *down_oth)
+        gu_e_oth = flip(gu_e, "c")
+        gu_own = [*gu_early, *gu_mid, gu_e]
+        gu_oth = [*early_oth, *mid_oth, gu_e_oth]
+        ff_parts = feed_forward(mn, gu_own, gu_oth, down_got + down_oth, units)
         ff_in = exchange(ff_parts)
         velocity, loss = velocity_and_loss(
             h1, ff_in, gains, head_p, noise.transpose(0, 2, 1), actions.transpose(0, 2, 1)

time: 153 us -> 162 us (1.059)
  waiting for transfers between devices: 63.8 us -> 86.1 us
  starting transfers between devices: 58 us -> 50.3 us
  Pallas kernels: 18.2 us -> 14.6 us
  other arithmetic: 5.24 us -> 3.05 us
    ppermute x18, waiting for transfers between devices: 21 us -> 35.5 us  [cross(): return lax.ppermute(value, ('i', 'x'), pairs)]
    ppermute x18 -> x20, waiting for transfers between devices: 6.83 us -> 11.5 us  [flip(): return lax.ppermute(value, axis, [(0, 1), (1, 0)])]
    ppermute x18, starting transfers between devices: 21.4 us -> 17.6 us  [cross(): return lax.ppermute(value, ('i', 'x'), pairs)]
    pallas_call x3 -> x2, Pallas kernels: 11.8 us -> 8.14 us  [the longest x1 6.05 us: attention(): pl.pallas_call(kernel, out_shape=[like(span, heads_cols) for _ in RELS],...]
    ppermute x11, starting transfers between devices: 17.6 us -> 14.6 us  [hop(): return lax.ppermute(value, 'o', pairs)]
    select_n x2 -> x0, other arithmetic: 2.2 us -> none  [the longest x1 1.1 us: fast(): jnp.where(inner, gu_d, gu_c)]
    ppermute x7, waiting for transfers between devices: 7.1 us -> 9.25 us  [turned(): lax.ppermute(value, ('o', 'i', 'c'), [((o * ni + i) * nc + c, ((o ^ r) *...]
    unnamed x21 -> x23, local copies, waits for them, and re-layouts: 3.39 us -> 3.39 us
  transfers between devices with their start and end apart: 54 -> 56, of which waited for: 19 -> 26; matrix products, arithmetic and copies ran while one was open for 4% -> 3% of each run, Pallas kernels for 7% -> 5%
where the time goes in v3:
time: 162 us; the launch traced here: 159 us
  waiting for transfers between devices  86.1 us (53%)
  starting transfers between devices  50.3 us (31%)
  Pallas kernels  14.6 us (9%)
  local copies, waits for them, and re-layouts  4.37 us (3%)
  other arithmetic  3.05 us (2%)
    ppermute x18, waiting for transfers between devices, cross(): return lax.ppermute(value, ('i', 'x'), pairs)  35.5 us
    ppermute x11, waiting for transfers between devices, hop(): return lax.ppermute(value, 'o', pairs)  29.8 us
    ppermute x18, starting transfers between devices, cross(): return lax.ppermute(value, ('i', 'x'), pairs)  17.6 us
    ppermute x7, starting transfers between devices, turned(): lax.ppermute(value, ('o', 'i', 'c'), [((o * ni + i) * nc + c, ((o ^ r) *...  15.1 us
    ppermute x11, starting transfers between devices, hop(): return lax.ppermute(value, 'o', pairs)  14.6 us
    ppermute x20, waiting for transfers between devices, flip(): return lax.ppermute(value, axis, [(0, 1), (1, 0)])  11.5 us
    ppermute x7, waiting for transfers between devices, turned(): lax.ppermute(value, ('o', 'i', 'c'), [((o * ni + i) * nc + c, ((o ^ r) *...  9.25 us
    pallas_call x1, Pallas kernels, attention(): pl.pallas_call(kernel, out_shape=[like(span, heads_cols) for _ in RELS],...  6.05 us
  transfers between devices with their start and end apart: 56, of which 26 were waited for; matrix products, arithmetic and copies ran while one was open for 3% of the time, Pallas kernels for 5%

profile of v3, /device:TPU:6, one launch (start us, length us, event | category | flops | bytes accessed | tf_op | source)
XLA Modules:
  0.0 159.4 jit_solution(8173384459305064941)
XLA Ops:
  0.7 2.2 %pack_weights.1 = (bf16[128,896]{1,0:T(8,128)(2,1)}, bf16[128,2048]{1,0:T(8,128)(2,1)}) custom-call(bf16[128,512]{1,0:T(8,128)(2,1)} %q.1, bf16[128,256]{1,0:T(8,128)(2,1)} %ak.1, bf16[128,256]{1,0:T(8,128)(2,1)} %av.1, bf16[256,256]{1,0:T(8,128)(2,1)} %kw.1, bf16[256,256]{1,0:T(8,128)(2,1)} %vw.1, bf16[128,1024]{1,0:T(8,128)(2,1)} %gw.1, bf16[128,1024]{1,0:T(8,128)(2,1)} %uw.1), custom_call_target="tpu_custom_call" | custom-call | tf_op jit(solution)/shard_map/pack_weights/pallas_call | solution.py:227
  2.9 3.0 %collective-permute-start.4 = (bf16[128,896]{1,0:T(8,128)(2,1)}, bf16[128,896]{1,0:T(8,128)(2,1)S(1)}, u32[]{:S(2)}, u32[]{:S(2)}) collective-permute-start(bf16[128,896]{1,0:T(8,128)(2,1)} %get-tuple-element.57), channel_id=1, source_target_pairs={{0,24},{1,28},{4,25},{5,29},{8,16},{9,20},{12,17},{13,21},{16,8},{... | collective-permute-start | bytes 688136 | tf_op jit(solution)/shard_map/ppermute | solution.py:532
  6.5 1.1 collective-permute-start.2
  7.7 3.3 %collective-permute-start.1 = (bf16[128,896]{1,0:T(8,128)(2,1)}, bf16[128,896]{1,0:T(8,128)(2,1)S(1)}, u32[]{:S(2)}, u32[]{:S(2)}) collective-permute-start(bf16[128,896]{1,0:T(8,128)(2,1)} %get-tuple-element.57), channel_id=1, source_target_pairs={{0,0},{1,4},{4,1},{5,5},{8,8},{9,12},{12,9},{13,13},{16,16},{17,20... | collective-permute-start | bytes 688136 | tf_op jit(solution)/shard_map/ppermute | solution.py:532
  11.9 1.0 add_convert_fusion
  13.2 4.8 %collective-permute-done = f32[2,51,32]{1,2,0:T(8,128)S(1)} collective-permute-done((f32[2,51,32]{1,2,0:T(8,128)S(1)}, f32[2,51,32]{1,2,0:T(8,128)S(1)}, u32[]{:S(2)}, u32[]{:S(2)}) %collective-permute-start) | collective-permute-done | bytes 13088 | tf_op jit(solution)/shard_map/ppermute | solution.py:517
  19.7 2.2 %expert_in.1 = (bf16[256,1024]{1,0:T(8,128)(2,1)}, f32[50,1024]{1,0:T(8,128)}, f32[8,1024]{1,0:T(8,128)}, bf16[32,1024]{1,0:T(8,128)(2,1)}) custom-call(bf16[256,32]{1,0:T(8,128)(2,1)} %bitcast.23, f32[4,1024]{1,0:T(4,128)} %pad_maximum_fusion.2.te, bf16[32,1024]{1,0:T(8,128)(2,1)} %act.1, f32[1,1024]{1,0:T(1,128)} %bitcast.28, f32[1,1024]{1,0:T(1,128)} %bitcast.29, ...), custom_call_target="tpu_custom_call" | custom-call | tf_op jit(solution)/shard_map/expert_in/pallas_call | solution.py:263
  22.0 5.3 %collective-permute-done.3.refs_2_ = bf16[128,896]{1,0:T(8,128)(2,1)S(1)} collective-permute-done((bf16[128,896]{1,0:T(8,128)(2,1)}, bf16[128,896]{1,0:T(8,128)(2,1)S(1)}, u32[]{:S(2)}, u32[]{:S(2)}) %collective-permute-start.3) | collective-permute-done | bytes 229408 | tf_op jit(solution)/shard_map/ppermute | solution.py:532
  27.4 2.1 %collective-permute-done.5.w1 = bf16[512,640]{1,0:T(8,128)(2,1)S(1)} collective-permute-done((bf16[512,640]{1,0:T(8,128)(2,1)S(1)}, bf16[512,640]{1,0:T(8,128)(2,1)S(1)}, u32[]{:S(2)}, u32[]{:S(2)}) %collective-permute-start.5) | collective-permute-done | bytes 655392 | tf_op jit(solution)/shard_map/ppermute | solution.py:517
  29.5 1.0 copy-done.1
  31.4 3.2 %collective-permute-start.33 = (bf16[128,2048]{1,0:T(8,128)(2,1)}, bf16[128,2048]{1,0:T(8,128)(2,1)S(1)}, u32[]{:S(2)}, u32[]{:S(2)}) collective-permute-start(bf16[128,2048]{1,0:T(8,128)(2,1)} %get-tuple-element.87), channel_id=1, source_target_pairs={{0,0},{1,4},{4,1},{5,5},{8,8},{9,12},{12,9},{13,13},{16,16},{17,20... | collective-permute-start | bytes 1572872 | tf_op jit(solution)/shard_map/ppermute | solution.py:532
  35.5 2.7 %collective-permute-start.11 = (bf16[512,256]{1,0:T(8,128)(2,1)S(1)}, bf16[512,256]{1,0:T(8,128)(2,1)S(1)}, u32[]{:S(2)}, u32[]{:S(2)}) collective-permute-start(bf16[512,256]{1,0:T(8,128)(2,1)S(1)} %get-tuple-element.69.refs_0_), channel_id=1, source_target_pairs={{0,6},{2,4},{4,2},{6,0},{1,7},{3,5},{5,3},{7,1},{8,14},{10,12},{12... | collective-permute-start | bytes 786440 | tf_op jit(solution)/shard_map/ppermute | solution.py:523
  38.7 11.9 %collective-permute-done.7.refs_10_ = bf16[50,640]{1,0:T(8,128)(2,1)S(1)} collective-permute-done((bf16[50,640]{1,0:T(8,128)(2,1)S(1)}, bf16[50,640]{1,0:T(8,128)(2,1)S(1)}, u32[]{:S(2)}, u32[]{:S(2)}) %collective-permute-start.7) | collective-permute-done | bytes 64032 | tf_op jit(solution)/shard_map/ppermute | solution.py:523
  51.0 4.9 %collective-permute-done.8.refs_11_ = bf16[50,640]{1,0:T(8,128)(2,1)S(1)} collective-permute-done((bf16[50,640]{1,0:T(8,128)(2,1)S(1)}, bf16[50,640]{1,0:T(8,128)(2,1)S(1)}, u32[]{:S(2)}, u32[]{:S(2)}) %collective-permute-start.8) | collective-permute-done | bytes 64032 | tf_op jit(solution)/shard_map/ppermute | solution.py:523
  55.9 1.9 %collective-permute-start.19 = (bf16[512,128]{1,0:T(8,128)(2,1)S(1)}, bf16[512,128]{1,0:T(8,128)(2,1)S(1)}, u32[]{:S(2)}, u32[]{:S(2)}) collective-permute-start(bf16[512,128]{1,0:T(8,128)(2,1)S(1)} %copy-done.10), channel_id=1, source_target_pairs={{0,0},{1,4},{4,1},{5,5},{8,8},{9,12},{12,9},{13,13},{16,16},{17,20... | collective-permute-start | bytes 393224 | tf_op jit(solution)/shard_map/ppermute | solution.py:532
  58.5 3.7 %collective-permute-done.19.refs_4_ = bf16[512,128]{1,0:T(8,128)(2,1)S(1)} collective-permute-done((bf16[512,128]{1,0:T(8,128)(2,1)S(1)}, bf16[512,128]{1,0:T(8,128)(2,1)S(1)}, u32[]{:S(2)}, u32[]{:S(2)}) %collective-permute-start.19) | collective-permute-done | bytes 131104 | tf_op jit(solution)/shard_map/ppermute | solution.py:532
  62.1 2.5 %collective-permute-start.22 = (bf16[512,128]{1,0:T(8,128)(2,1)S(1)}, bf16[512,128]{1,0:T(8,128)(2,1)S(1)}, u32[]{:S(2)}, u32[]{:S(2)}) collective-permute-start(bf16[512,128]{1,0:T(8,128)(2,1)S(1)} %collective-permute-done.19.refs_4_), channel_id=1, source_target_pairs={{0,24},{8,16},{16,8},{24,0},{1,25},{9,17},{17,9},{25,1},{2,26},{10... | collective-permute-start | bytes 393224 | tf_op jit(solution)/shard_map/ppermute | solution.py:544
  65.0 1.5 collective-permute-start.20
  67.8 2.2 %copy-done = bf16[1,1024,2048]{2,1,0:T(8,128)(2,1)S(1)} copy-done((bf16[1,1024,2048]{2,1,0:T(8,128)(2,1)S(1)}, bf16[1,1024,2048]{2,1,0:T(8,128)(2,1)}, u32[]{:S(2)}) %copy-start) | copy-done | bytes 4194328
  69.9 6.0 %prefix_attention.1 = (bf16[50,512]{1,0:T(8,128)(2,1)S(1)}, bf16[50,512]{1,0:T(8,128)(2,1)S(1)}, bf16[50,512]{1,0:T(8,128)(2,1)S(1)}, bf16[50,512]{1,0:T(8,128)(2,1)S(1)}) custom-call(s32[4]{0:T(128)S(1)} %copy-done.7, bf16[1024,2048]{1,0:T(8,128)(2,1)S(1)} %bitcast.19, f32[1,2048]{1,0:T(1,128)S(1)} %bitcast.22, ...), custom_call_target="tpu_custom_call" | custom-call | tf_op jit(solution)/shard_map/prefix_attention/pallas_call | solution.py:394
  76.5 1.4 collective-permute-done.21.refs_6_
  78.3 1.3 collective-permute-start.18
  80.2 1.7 %collective-permute-done.17.refs_2_ = bf16[50,512]{1,0:T(8,128)(2,1)S(1)} collective-permute-done((bf16[50,512]{1,0:T(8,128)(2,1)S(1)}, bf16[50,512]{1,0:T(8,128)(2,1)S(1)}, u32[]{:S(2)}, u32[]{:S(2)}) %collective-permute-start.17) | collective-permute-done | bytes 51232 | tf_op jit(solution)/shard_map/ppermute | solution.py:523
  82.0 1.4 collective-permute-done.18.refs_3_
  83.4 1.9 %collective-permute-start.39 = (bf16[1024,128]{1,0:T(8,128)(2,1)S(1)}, bf16[1024,128]{1,0:T(8,128)(2,1)S(1)}, u32[]{:S(2)}, u32[]{:S(2)}) collective-permute-start(bf16[1024,128]{1,0:T(8,128)(2,1)S(1)} %copy-done.9), channel_id=1, source_target_pairs={{0,0},{1,4},{4,1},{5,5},{8,8},{9,12},{12,9},{13,13},{16,16},{17,20... | collective-permute-start | bytes 786440 | tf_op jit(solution)/shard_map/ppermute | solution.py:532
  85.9 0.8 collective-permute-done.25.refs_10_
  87.4 2.0 %collective-permute-start.27 = (bf16[50,1024]{1,0:T(8,128)(2,1)S(1)}, bf16[50,1024]{1,0:T(8,128)(2,1)S(1)}, u32[]{:S(2)}, u32[]{:S(2)}) collective-permute-start(bf16[50,1024]{1,0:T(8,128)(2,1)S(1)} %get-tuple-element.83), channel_id=1, source_target_pairs={{0,4},{2,6},{4,0},{6,2},{1,5},{3,7},{5,1},{7,3},{8,12},{10,14},{12... | collective-permute-start | bytes 307208 | tf_op jit(solution)/shard_map/ppermute | solution.py:523
  89.4 1.5 collective-permute-start.28
  91.2 2.1 %collective-permute-start.45 = (bf16[1024,128]{1,0:T(8,128)(2,1)S(1)}, bf16[1024,128]{1,0:T(8,128)(2,1)S(1)}, u32[]{:S(2)}, u32[]{:S(2)}) collective-permute-start(bf16[1024,128]{1,0:T(8,128)(2,1)S(1)} %collective-permute-done.39.refs_16_), channel_id=1, source_target_pairs={{0,24},{8,16},{16,8},{24,0},{1,25},{9,17},{17,9},{25,1},{2,26},{10... | collective-permute-start | bytes 786440 | tf_op jit(solution)/shard_map/ppermute | solution.py:544
  93.3 2.6 %collective-permute-start.43 = (bf16[1024,128]{1,0:T(8,128)(2,1)S(1)}, bf16[1024,128]{1,0:T(8,128)(2,1)S(1)}, u32[]{:S(2)}, u32[]{:S(2)}) collective-permute-start(bf16[1024,128]{1,0:T(8,128)(2,1)S(1)} %collective-permute-done.39.refs_16_), channel_id=1, source_target_pairs={{0,16},{8,24},{16,0},{24,8},{1,17},{9,25},{17,1},{25,9},{2,18},{10... | collective-permute-start | bytes 786440 | tf_op jit(solution)/shard_map/ppermute | solution.py:544
  95.9 0.9 collective-permute-start.41
  96.8 1.3 collective-permute-start.36
  99.2 3.3 %collective-permute-done.45.refs_19_ = bf16[1024,128]{1,0:T(8,128)(2,1)S(1)} collective-permute-done((bf16[1024,128]{1,0:T(8,128)(2,1)S(1)}, bf16[1024,128]{1,0:T(8,128)(2,1)S(1)}, u32[]{:S(2)}, u32[]{:S(2)}) %collective-permute-start.45) | collective-permute-done | bytes 262176 | tf_op jit(solution)/shard_map/ppermute | solution.py:544
  102.4 2.9 %collective-permute-start.32 = (bf16[50,1024]{1,0:T(8,128)(2,1)S(1)}, bf16[50,1024]{1,0:T(8,128)(2,1)S(1)}, u32[]{:S(2)}, u32[]{:S(2)}) collective-permute-start(bf16[50,1024]{1,0:T(8,128)(2,1)S(1)} %multiply_convert_fusion.refs_0_), channel_id=1, source_target_pairs={{0,6},{2,4},{4,2},{6,0},{1,7},{3,5},{5,3},{7,1},{8,14},{10,12},{12... | collective-permute-start | bytes 307208 | tf_op jit(solution)/shard_map/ppermute | solution.py:523
  105.3 13.9 %collective-permute-done.43.refs_18_ = bf16[1024,128]{1,0:T(8,128)(2,1)S(1)} collective-permute-done((bf16[1024,128]{1,0:T(8,128)(2,1)S(1)}, bf16[1024,128]{1,0:T(8,128)(2,1)S(1)}, u32[]{:S(2)}, u32[]{:S(2)}) %collective-permute-start.43) | collective-permute-done | bytes 262176 | tf_op jit(solution)/shard_map/ppermute | solution.py:544
  119.2 1.5 collective-permute-start.38
  121.4 4.9 %collective-permute-done.31.refs_2_ = bf16[50,1024]{1,0:T(8,128)(2,1)S(1)} collective-permute-done((bf16[50,1024]{1,0:T(8,128)(2,1)S(1)}, bf16[50,1024]{1,0:T(8,128)(2,1)S(1)}, u32[]{:S(2)}, u32[]{:S(2)}) %collective-permute-start.31) | collective-permute-done | bytes 102432 | tf_op jit(solution)/shard_map/ppermute | solution.py:523
  126.5 4.6 %collective-permute-done.30.refs_1_ = bf16[50,1024]{1,0:T(8,128)(2,1)S(1)} collective-permute-done((bf16[50,1024]{1,0:T(8,128)(2,1)S(1)}, bf16[50,1024]{1,0:T(8,128)(2,1)S(1)}, u32[]{:S(2)}, u32[]{:S(2)}) %collective-permute-start.30) | collective-permute-done | bytes 102432 | tf_op jit(solution)/shard_map/ppermute | solution.py:523
  131.7 0.9 collective-permute-done.46.refs_23_
  133.5 11.3 %collective-permute-done.38.refs_9_ = bf16[128,2048]{1,0:T(8,128)(2,1)S(1)} collective-permute-done((bf16[128,2048]{1,0:T(8,128)(2,1)S(1)}, bf16[128,2048]{1,0:T(8,128)(2,1)S(1)}, u32[]{:S(2)}, u32[]{:S(2)}) %collective-permute-start.38) | collective-permute-done | bytes 524320 | tf_op jit(solution)/shard_map/ppermute | solution.py:544
  145.3 1.4 collective-permute-done.51.refs_14_
  147.5 2.1 %feed_forward.1 = (f32[50,1024]{1,0:T(8,128)S(1)}, bf16[50,1024]{1,0:T(8,128)(2,1)S(1)}, bf16[50,1024]{1,0:T(8,128)(2,1)S(1)}, bf16[50,1024]{1,0:T(8,128)(2,1)S(1)}) custom-call(bf16[50,1024]{1,0:T(8,128)(2,1)S(1)} %multiply_convert_fusion.refs_0_, bf16[50,1024]{1,0:T(8,128)(2,1)S(1)} %collective-permute-done.30.refs_1_, ...), custom_call_target="tpu_custom_call" | custom-call | tf_op jit(solution)/shard_map/feed_forward/pallas_call | solution.py:480
  149.7 1.5 collective-permute-start.54
  151.2 1.9 %collective-permute-start.55 = (bf16[50,1024]{1,0:T(8,128)(2,1)S(1)}, bf16[50,1024]{1,0:T(8,128)(2,1)S(1)}, u32[]{:S(2)}, u32[]{:S(2)}) collective-permute-start(bf16[50,1024]{1,0:T(8,128)(2,1)S(1)} %get-tuple-element.106), channel_id=1, source_target_pairs={{0,6},{2,4},{4,2},{6,0},{1,7},{3,5},{5,3},{7,1},{8,14},{10,12},{12... | collective-permute-start | bytes 307208 | tf_op jit(solution)/shard_map/ppermute | solution.py:523
  153.1 1.7 %collective-permute-done.53.refs_1_ = bf16[50,1024]{1,0:T(8,128)(2,1)S(1)} collective-permute-done((bf16[50,1024]{1,0:T(8,128)(2,1)S(1)}, bf16[50,1024]{1,0:T(8,128)(2,1)S(1)}, u32[]{:S(2)}, u32[]{:S(2)}) %collective-permute-start.53) | collective-permute-done | bytes 102432 | tf_op jit(solution)/shard_map/ppermute | solution.py:523
  154.8 1.0 collective-permute-done.54.refs_2_
  155.7 2.7 %collective-permute-done.55.refs_3_ = bf16[50,1024]{1,0:T(8,128)(2,1)S(1)} collective-permute-done((bf16[50,1024]{1,0:T(8,128)(2,1)S(1)}, bf16[50,1024]{1,0:T(8,128)(2,1)S(1)}, u32[]{:S(2)}, u32[]{:S(2)}) %collective-permute-start.55) | collective-permute-done | bytes 102432 | tf_op jit(solution)/shard_map/ppermute | solution.py:523
  158.4 0.9 velocity_and_loss.1
  (114 shorter events, 16.4 us)
Async XLA Ops:
  2.9 19.1 %collective-permute-start.4 = (bf16[128,896]{1,0:T(8,128)(2,1)}, bf16[128,896]{1,0:T(8,128)(2,1)S(1)}, u32[]{:S(2)}, u32[]{:S(2)}) collective-permute-start(bf16[128,896]{1,0:T(8,128)(2,1)} %get-tuple-element.57), channel_id=1, source_target_pairs={{0,24},{1,28},{4,25},{5,29},{8,16},{9,20},{12,17},{13,21},{16,8},{... | collective-permute-start | bytes 688136 | tf_op jit(solution)/shard_map/ppermute | solution.py:532
  5.9 21.4 %collective-permute-start.3 = (bf16[128,896]{1,0:T(8,128)(2,1)}, bf16[128,896]{1,0:T(8,128)(2,1)S(1)}, u32[]{:S(2)}, u32[]{:S(2)}) collective-permute-start(bf16[128,896]{1,0:T(8,128)(2,1)} %get-tuple-element.57), channel_id=1, source_target_pairs={{0,16},{1,20},{4,17},{5,21},{8,24},{9,28},{12,25},{13,29},{16,0},{... | collective-permute-start | bytes 688136 | tf_op jit(solution)/shard_map/ppermute | solution.py:532
  6.5 20.7 %collective-permute-start.2 = (bf16[128,896]{1,0:T(8,128)(2,1)}, bf16[128,896]{1,0:T(8,128)(2,1)S(1)}, u32[]{:S(2)}, u32[]{:S(2)}) collective-permute-start(bf16[128,896]{1,0:T(8,128)(2,1)} %get-tuple-element.57), channel_id=1, source_target_pairs={{0,8},{1,12},{4,9},{5,13},{8,0},{9,4},{12,1},{13,5},{16,24},{17,28... | collective-permute-start | bytes 688136 | tf_op jit(solution)/shard_map/ppermute | solution.py:532
  7.7 19.6 %collective-permute-start.1 = (bf16[128,896]{1,0:T(8,128)(2,1)}, bf16[128,896]{1,0:T(8,128)(2,1)S(1)}, u32[]{:S(2)}, u32[]{:S(2)}) collective-permute-start(bf16[128,896]{1,0:T(8,128)(2,1)} %get-tuple-element.57), channel_id=1, source_target_pairs={{0,0},{1,4},{4,1},{5,5},{8,8},{9,12},{12,9},{13,13},{16,16},{17,20... | collective-permute-start | bytes 688136 | tf_op jit(solution)/shard_map/ppermute | solution.py:532
  13.0 5.0 %collective-permute-start = (f32[2,51,32]{1,2,0:T(8,128)S(1)}, f32[2,51,32]{1,2,0:T(8,128)S(1)}, u32[]{:S(2)}, u32[]{:S(2)}) collective-permute-start(f32[2,51,32]{1,2,0:T(8,128)S(1)} %pad_maximum_fusion.1), channel_id=1, source_target_pairs={{0,4},{4,0},{1,5},{5,1},{2,6},{6,2},{3,7},{7,3},{8,12},{12,8},{9,1... | collective-permute-start | bytes 39176 | tf_op jit(solution)/shard_map/ppermute | solution.py:517
  31.1 7.0 %collective-permute-start.6 = (bf16[50,640]{1,0:T(8,128)(2,1)S(1)}, bf16[50,640]{1,0:T(8,128)(2,1)S(1)}, u32[]{:S(2)}, u32[]{:S(2)}) collective-permute-start(bf16[50,640]{1,0:T(8,128)(2,1)S(1)} %get-tuple-element.66), channel_id=1, source_target_pairs={{0,4},{2,6},{4,0},{6,2},{1,5},{3,7},{5,1},{7,3},{8,12},{10,14},{12... | collective-permute-start | bytes 192008 | tf_op jit(solution)/shard_map/ppermute | solution.py:523
  31.4 30.8 %collective-permute-start.33 = (bf16[128,2048]{1,0:T(8,128)(2,1)}, bf16[128,2048]{1,0:T(8,128)(2,1)S(1)}, u32[]{:S(2)}, u32[]{:S(2)}) collective-permute-start(bf16[128,2048]{1,0:T(8,128)(2,1)} %get-tuple-element.87), channel_id=1, source_target_pairs={{0,0},{1,4},{4,1},{5,5},{8,8},{9,12},{12,9},{13,13},{16,16},{17,20... | collective-permute-start | bytes 1572872 | tf_op jit(solution)/shard_map/ppermute | solution.py:532
  34.6 23.2 %collective-permute-start.9 = (bf16[512,256]{1,0:T(8,128)(2,1)S(1)}, bf16[512,256]{1,0:T(8,128)(2,1)S(1)}, u32[]{:S(2)}, u32[]{:S(2)}) collective-permute-start(bf16[512,256]{1,0:T(8,128)(2,1)S(1)} %get-tuple-element.69.refs_0_), channel_id=1, source_target_pairs={{0,4},{2,6},{4,0},{6,2},{1,5},{3,7},{5,1},{7,3},{8,12},{10,14},{12... | collective-permute-start | bytes 786440 | tf_op jit(solution)/shard_map/ppermute | solution.py:523
  34.9 22.9 %collective-permute-start.10 = (bf16[512,256]{1,0:T(8,128)(2,1)S(1)}, bf16[512,256]{1,0:T(8,128)(2,1)S(1)}, u32[]{:S(2)}, u32[]{:S(2)}) collective-permute-start(bf16[512,256]{1,0:T(8,128)(2,1)S(1)} %get-tuple-element.69.refs_0_), channel_id=1, source_target_pairs={{0,2},{2,0},{4,6},{6,4},{1,3},{3,1},{5,7},{7,5},{8,10},{10,8},{12,... | collective-permute-start | bytes 786440 | tf_op jit(solution)/shard_map/ppermute | solution.py:523
  35.5 22.9 %collective-permute-start.11 = (bf16[512,256]{1,0:T(8,128)(2,1)S(1)}, bf16[512,256]{1,0:T(8,128)(2,1)S(1)}, u32[]{:S(2)}, u32[]{:S(2)}) collective-permute-start(bf16[512,256]{1,0:T(8,128)(2,1)S(1)} %get-tuple-element.69.refs_0_), channel_id=1, source_target_pairs={{0,6},{2,4},{4,2},{6,0},{1,7},{3,5},{5,3},{7,1},{8,14},{10,12},{12... | collective-permute-start | bytes 786440 | tf_op jit(solution)/shard_map/ppermute | solution.py:523
  38.2 12.5 %collective-permute-start.7 = (bf16[50,640]{1,0:T(8,128)(2,1)S(1)}, bf16[50,640]{1,0:T(8,128)(2,1)S(1)}, u32[]{:S(2)}, u32[]{:S(2)}) collective-permute-start(bf16[50,640]{1,0:T(8,128)(2,1)S(1)} %get-tuple-element.67), channel_id=1, source_target_pairs={{0,2},{2,0},{4,6},{6,4},{1,3},{3,1},{5,7},{7,5},{8,10},{10,8},{12,... | collective-permute-start | bytes 192008 | tf_op jit(solution)/shard_map/ppermute | solution.py:523
  50.6 5.2 %collective-permute-start.8 = (bf16[50,640]{1,0:T(8,128)(2,1)S(1)}, bf16[50,640]{1,0:T(8,128)(2,1)S(1)}, u32[]{:S(2)}, u32[]{:S(2)}) collective-permute-start(bf16[50,640]{1,0:T(8,128)(2,1)S(1)} %get-tuple-element.68), channel_id=1, source_target_pairs={{0,6},{2,4},{4,2},{6,0},{1,7},{3,5},{5,3},{7,1},{8,14},{10,12},{12... | collective-permute-start | bytes 192008 | tf_op jit(solution)/shard_map/ppermute | solution.py:523
  55.9 6.3 %collective-permute-start.19 = (bf16[512,128]{1,0:T(8,128)(2,1)S(1)}, bf16[512,128]{1,0:T(8,128)(2,1)S(1)}, u32[]{:S(2)}, u32[]{:S(2)}) collective-permute-start(bf16[512,128]{1,0:T(8,128)(2,1)S(1)} %copy-done.10), channel_id=1, source_target_pairs={{0,0},{1,4},{4,1},{5,5},{8,8},{9,12},{12,9},{13,13},{16,16},{17,20... | collective-permute-start | bytes 393224 | tf_op jit(solution)/shard_map/ppermute | solution.py:532
  57.8 6.8 %collective-permute-start.12 = (bf16[512,256]{1,0:T(8,128)(2,1)S(1)}, bf16[512,256]{1,0:T(8,128)(2,1)S(1)}, u32[]{:S(2)}, u32[]{:S(2)}) collective-permute-start(bf16[512,256]{1,0:T(8,128)(2,1)S(1)} %get-tuple-element.69.refs_0_), channel_id=1, source_target_pairs={{0,1},{1,0},{2,3},{3,2},{4,5},{5,4},{6,7},{7,6},{8,9},{9,8},{10,11... | collective-permute-start | bytes 786440 | tf_op jit(solution)/shard_map/ppermute | solution.py:517
  57.9 7.1 %collective-permute-start.13 = (bf16[512,256]{1,0:T(8,128)(2,1)S(1)}, bf16[512,256]{1,0:T(8,128)(2,1)S(1)}, u32[]{:S(2)}, u32[]{:S(2)}) collective-permute-start(bf16[512,256]{1,0:T(8,128)(2,1)S(1)} %collective-permute-done.9.refs_1_), channel_id=1, source_target_pairs={{0,1},{1,0},{2,3},{3,2},{4,5},{5,4},{6,7},{7,6},{8,9},{9,8},{10,11... | collective-permute-start | bytes 786440 | tf_op jit(solution)/shard_map/ppermute | solution.py:517
  58.4 8.2 %collective-permute-start.14 = (bf16[512,256]{1,0:T(8,128)(2,1)S(1)}, bf16[512,256]{1,0:T(8,128)(2,1)S(1)}, u32[]{:S(2)}, u32[]{:S(2)}) collective-permute-start(bf16[512,256]{1,0:T(8,128)(2,1)S(1)} %collective-permute-done.10.refs_2_), channel_id=1, source_target_pairs={{0,1},{1,0},{2,3},{3,2},{4,5},{5,4},{6,7},{7,6},{8,9},{9,8},{10,11... | collective-permute-start | bytes 786440 | tf_op jit(solution)/shard_map/ppermute | solution.py:517
  62.1 4.9 %collective-permute-start.15 = (bf16[512,256]{1,0:T(8,128)(2,1)S(1)}, bf16[512,256]{1,0:T(8,128)(2,1)S(1)}, u32[]{:S(2)}, u32[]{:S(2)}) collective-permute-start(bf16[512,256]{1,0:T(8,128)(2,1)S(1)} %collective-permute-done.11.refs_3_), channel_id=1, source_target_pairs={{0,1},{1,0},{2,3},{3,2},{4,5},{5,4},{6,7},{7,6},{8,9},{9,8},{10,11... | collective-permute-start | bytes 786440 | tf_op jit(solution)/shard_map/ppermute | solution.py:517
  62.1 13.8 %collective-permute-start.22 = (bf16[512,128]{1,0:T(8,128)(2,1)S(1)}, bf16[512,128]{1,0:T(8,128)(2,1)S(1)}, u32[]{:S(2)}, u32[]{:S(2)}) collective-permute-start(bf16[512,128]{1,0:T(8,128)(2,1)S(1)} %collective-permute-done.19.refs_4_), channel_id=1, source_target_pairs={{0,24},{8,16},{16,8},{24,0},{1,25},{9,17},{17,9},{25,1},{2,26},{10... | collective-permute-start | bytes 393224 | tf_op jit(solution)/shard_map/ppermute | solution.py:544
  64.6 13.2 %collective-permute-start.21 = (bf16[512,128]{1,0:T(8,128)(2,1)S(1)}, bf16[512,128]{1,0:T(8,128)(2,1)S(1)}, u32[]{:S(2)}, u32[]{:S(2)}) collective-permute-start(bf16[512,128]{1,0:T(8,128)(2,1)S(1)} %collective-permute-done.19.refs_4_), channel_id=1, source_target_pairs={{0,16},{8,24},{16,0},{24,8},{1,17},{9,25},{17,1},{25,9},{2,18},{10... | collective-permute-start | bytes 393224 | tf_op jit(solution)/shard_map/ppermute | solution.py:544
  65.0 13.3 %collective-permute-start.20 = (bf16[512,128]{1,0:T(8,128)(2,1)S(1)}, bf16[512,128]{1,0:T(8,128)(2,1)S(1)}, u32[]{:S(2)}, u32[]{:S(2)}) collective-permute-start(bf16[512,128]{1,0:T(8,128)(2,1)S(1)} %collective-permute-done.19.refs_4_), channel_id=1, source_target_pairs={{0,8},{8,0},{16,24},{24,16},{1,9},{9,1},{17,25},{25,17},{2,10},{10... | collective-permute-start | bytes 393224 | tf_op jit(solution)/shard_map/ppermute | solution.py:544
  66.5 24.6 %collective-permute-start.34 = (bf16[128,2048]{1,0:T(8,128)(2,1)S(1)}, bf16[128,2048]{1,0:T(8,128)(2,1)S(1)}, u32[]{:S(2)}, u32[]{:S(2)}) collective-permute-start(bf16[128,2048]{1,0:T(8,128)(2,1)S(1)} %collective-permute-done.33.refs_4_), channel_id=1, source_target_pairs={{0,8},{8,0},{16,24},{24,16},{1,9},{9,1},{17,25},{25,17},{2,10},{10... | collective-permute-start | bytes 1572872 | tf_op jit(solution)/shard_map/ppermute | solution.py:544
  67.0 26.3 %collective-permute-start.35 = (bf16[128,2048]{1,0:T(8,128)(2,1)S(1)}, bf16[128,2048]{1,0:T(8,128)(2,1)S(1)}, u32[]{:S(2)}, u32[]{:S(2)}) collective-permute-start(bf16[128,2048]{1,0:T(8,128)(2,1)S(1)} %collective-permute-done.33.refs_4_), channel_id=1, source_target_pairs={{8,16},{16,8},{9,17},{17,9},{10,18},{18,10},{11,19},{19,11},{12,20... | collective-permute-start | bytes 1572872 | tf_op jit(solution)/shard_map/ppermute | solution.py:544
  76.0 4.2 %collective-permute-start.16 = (bf16[50,512]{1,0:T(8,128)(2,1)S(1)}, bf16[50,512]{1,0:T(8,128)(2,1)S(1)}, u32[]{:S(2)}, u32[]{:S(2)}) collective-permute-start(bf16[50,512]{1,0:T(8,128)(2,1)S(1)} %get-tuple-element.74), channel_id=1, source_target_pairs={{0,4},{2,6},{4,0},{6,2},{1,5},{3,7},{5,1},{7,3},{8,12},{10,14},{12... | collective-permute-start | bytes 153608 | tf_op jit(solution)/shard_map/ppermute | solution.py:523
  77.8 4.2 %collective-permute-start.17 = (bf16[50,512]{1,0:T(8,128)(2,1)S(1)}, bf16[50,512]{1,0:T(8,128)(2,1)S(1)}, u32[]{:S(2)}, u32[]{:S(2)}) collective-permute-start(bf16[50,512]{1,0:T(8,128)(2,1)S(1)} %get-tuple-element.75), channel_id=1, source_target_pairs={{0,2},{2,0},{4,6},{6,4},{1,3},{3,1},{5,7},{7,5},{8,10},{10,8},{12,... | collective-permute-start | bytes 153608 | tf_op jit(solution)/shard_map/ppermute | solution.py:523
  78.3 5.1 %collective-permute-start.18 = (bf16[50,512]{1,0:T(8,128)(2,1)S(1)}, bf16[50,512]{1,0:T(8,128)(2,1)S(1)}, u32[]{:S(2)}, u32[]{:S(2)}) collective-permute-start(bf16[50,512]{1,0:T(8,128)(2,1)S(1)} %get-tuple-element.76), channel_id=1, source_target_pairs={{0,6},{2,4},{4,2},{6,0},{1,7},{3,5},{5,3},{7,1},{8,14},{10,12},{12... | collective-permute-start | bytes 153608 | tf_op jit(solution)/shard_map/ppermute | solution.py:523
  80.2 5.1 %collective-permute-start.23 = (bf16[512,128]{1,0:T(8,128)(2,1)S(1)}, bf16[512,128]{1,0:T(8,128)(2,1)S(1)}, u32[]{:S(2)}, u32[]{:S(2)}) collective-permute-start(bf16[512,128]{1,0:T(8,128)(2,1)S(1)} %collective-permute-done.19.refs_4_), channel_id=1, source_target_pairs={{0,1},{1,0},{2,3},{3,2},{4,5},{5,4},{6,7},{7,6},{8,9},{9,8},{10,11... | collective-permute-start | bytes 393224 | tf_op jit(solution)/shard_map/ppermute | solution.py:517
  82.0 3.5 %collective-permute-start.24 = (bf16[512,128]{1,0:T(8,128)(2,1)S(1)}, bf16[512,128]{1,0:T(8,128)(2,1)S(1)}, u32[]{:S(2)}, u32[]{:S(2)}) collective-permute-start(bf16[512,128]{1,0:T(8,128)(2,1)S(1)} %collective-permute-done.20.refs_5_), channel_id=1, source_target_pairs={{0,1},{1,0},{2,3},{3,2},{4,5},{5,4},{6,7},{7,6},{8,9},{9,8},{10,11... | collective-permute-start | bytes 393224 | tf_op jit(solution)/shard_map/ppermute | solution.py:517
  83.4 7.7 %collective-permute-start.39 = (bf16[1024,128]{1,0:T(8,128)(2,1)S(1)}, bf16[1024,128]{1,0:T(8,128)(2,1)S(1)}, u32[]{:S(2)}, u32[]{:S(2)}) collective-permute-start(bf16[1024,128]{1,0:T(8,128)(2,1)S(1)} %copy-done.9), channel_id=1, source_target_pairs={{0,0},{1,4},{4,1},{5,5},{8,8},{9,12},{12,9},{13,13},{16,16},{17,20... | collective-permute-start | bytes 786440 | tf_op jit(solution)/shard_map/ppermute | solution.py:532
  87.4 8.5 %collective-permute-start.27 = (bf16[50,1024]{1,0:T(8,128)(2,1)S(1)}, bf16[50,1024]{1,0:T(8,128)(2,1)S(1)}, u32[]{:S(2)}, u32[]{:S(2)}) collective-permute-start(bf16[50,1024]{1,0:T(8,128)(2,1)S(1)} %get-tuple-element.83), channel_id=1, source_target_pairs={{0,4},{2,6},{4,0},{6,2},{1,5},{3,7},{5,1},{7,3},{8,12},{10,14},{12... | collective-permute-start | bytes 307208 | tf_op jit(solution)/shard_map/ppermute | solution.py:523
  89.4 7.4 %collective-permute-start.28 = (bf16[50,1024]{1,0:T(8,128)(2,1)S(1)}, bf16[50,1024]{1,0:T(8,128)(2,1)S(1)}, u32[]{:S(2)}, u32[]{:S(2)}) collective-permute-start(bf16[50,1024]{1,0:T(8,128)(2,1)S(1)} %get-tuple-element.84), channel_id=1, source_target_pairs={{0,2},{2,0},{4,6},{6,4},{1,3},{3,1},{5,7},{7,5},{8,10},{10,8},{12,... | collective-permute-start | bytes 307208 | tf_op jit(solution)/shard_map/ppermute | solution.py:523
  91.2 6.9 %collective-permute-start.29 = (bf16[50,1024]{1,0:T(8,128)(2,1)S(1)}, bf16[50,1024]{1,0:T(8,128)(2,1)S(1)}, u32[]{:S(2)}, u32[]{:S(2)}) collective-permute-start(bf16[50,1024]{1,0:T(8,128)(2,1)S(1)} %get-tuple-element.85), channel_id=1, source_target_pairs={{0,6},{2,4},{4,2},{6,0},{1,7},{3,5},{5,3},{7,1},{8,14},{10,12},{12... | collective-permute-start | bytes 307208 | tf_op jit(solution)/shard_map/ppermute | solution.py:523
  91.2 11.2 %collective-permute-start.45 = (bf16[1024,128]{1,0:T(8,128)(2,1)S(1)}, bf16[1024,128]{1,0:T(8,128)(2,1)S(1)}, u32[]{:S(2)}, u32[]{:S(2)}) collective-permute-start(bf16[1024,128]{1,0:T(8,128)(2,1)S(1)} %collective-permute-done.39.refs_16_), channel_id=1, source_target_pairs={{0,24},{8,16},{16,8},{24,0},{1,25},{9,17},{17,9},{25,1},{2,26},{10... | collective-permute-start | bytes 786440 | tf_op jit(solution)/shard_map/ppermute | solution.py:544
  93.3 25.9 %collective-permute-start.43 = (bf16[1024,128]{1,0:T(8,128)(2,1)S(1)}, bf16[1024,128]{1,0:T(8,128)(2,1)S(1)}, u32[]{:S(2)}, u32[]{:S(2)}) collective-permute-start(bf16[1024,128]{1,0:T(8,128)(2,1)S(1)} %collective-permute-done.39.refs_16_), channel_id=1, source_target_pairs={{0,16},{8,24},{16,0},{24,8},{1,17},{9,25},{17,1},{25,9},{2,18},{10... | collective-permute-start | bytes 786440 | tf_op jit(solution)/shard_map/ppermute | solution.py:544
  95.9 24.7 %collective-permute-start.41 = (bf16[1024,128]{1,0:T(8,128)(2,1)S(1)}, bf16[1024,128]{1,0:T(8,128)(2,1)S(1)}, u32[]{:S(2)}, u32[]{:S(2)}) collective-permute-start(bf16[1024,128]{1,0:T(8,128)(2,1)S(1)} %collective-permute-done.39.refs_16_), channel_id=1, source_target_pairs={{0,8},{8,0},{16,24},{24,16},{1,9},{9,1},{17,25},{25,17},{2,10},{10... | collective-permute-start | bytes 786440 | tf_op jit(solution)/shard_map/ppermute | solution.py:544
  96.8 34.3 %collective-permute-start.36 = (bf16[128,2048]{1,0:T(8,128)(2,1)S(1)}, bf16[128,2048]{1,0:T(8,128)(2,1)S(1)}, u32[]{:S(2)}, u32[]{:S(2)}) collective-permute-start(bf16[128,2048]{1,0:T(8,128)(2,1)S(1)} %collective-permute-done.35.refs_6_), channel_id=1, source_target_pairs={{8,0},{16,24},{9,1},{17,25},{10,2},{18,26},{11,3},{19,27},{12,4},{... | collective-permute-start | bytes 1572872 | tf_op jit(solution)/shard_map/ppermute | solution.py:544
  98.1 7.2 %collective-permute-start.37 = (bf16[128,2048]{1,0:T(8,128)(2,1)S(1)}, bf16[128,2048]{1,0:T(8,128)(2,1)S(1)}, u32[]{:S(2)}, u32[]{:S(2)}) collective-permute-start(bf16[128,2048]{1,0:T(8,128)(2,1)S(1)} %collective-permute-done.34.refs_5_), channel_id=1, source_target_pairs={{8,16},{16,8},{9,17},{17,9},{10,18},{18,10},{11,19},{19,11},{12,20... | collective-permute-start | bytes 1572872 | tf_op jit(solution)/shard_map/ppermute | solution.py:544
  102.4 18.4 %collective-permute-start.32 = (bf16[50,1024]{1,0:T(8,128)(2,1)S(1)}, bf16[50,1024]{1,0:T(8,128)(2,1)S(1)}, u32[]{:S(2)}, u32[]{:S(2)}) collective-permute-start(bf16[50,1024]{1,0:T(8,128)(2,1)S(1)} %multiply_convert_fusion.refs_0_), channel_id=1, source_target_pairs={{0,6},{2,4},{4,2},{6,0},{1,7},{3,5},{5,3},{7,1},{8,14},{10,12},{12... | collective-permute-start | bytes 307208 | tf_op jit(solution)/shard_map/ppermute | solution.py:523
  105.3 26.3 %collective-permute-start.40 = (bf16[1024,128]{1,0:T(8,128)(2,1)S(1)}, bf16[1024,128]{1,0:T(8,128)(2,1)S(1)}, u32[]{:S(2)}, u32[]{:S(2)}) collective-permute-start(bf16[1024,128]{1,0:T(8,128)(2,1)S(1)} %collective-permute-done.39.refs_16_), channel_id=1, source_target_pairs={{0,1},{1,0},{2,3},{3,2},{4,5},{5,4},{6,7},{7,6},{8,9},{9,8},{10,11... | collective-permute-start | bytes 786440 | tf_op jit(solution)/shard_map/ppermute | solution.py:517
  119.2 25.6 %collective-permute-start.38 = (bf16[128,2048]{1,0:T(8,128)(2,1)S(1)}, bf16[128,2048]{1,0:T(8,128)(2,1)S(1)}, u32[]{:S(2)}, u32[]{:S(2)}) collective-permute-start(bf16[128,2048]{1,0:T(8,128)(2,1)S(1)} %collective-permute-done.37.refs_8_), channel_id=1, source_target_pairs={{8,0},{16,24},{9,1},{17,25},{10,2},{18,26},{11,3},{19,27},{12,4},{... | collective-permute-start | bytes 1572872 | tf_op jit(solution)/shard_map/ppermute | solution.py:544
  120.7 24.1 %collective-permute-start.47 = (bf16[128,2048]{1,0:T(8,128)(2,1)S(1)}, bf16[128,2048]{1,0:T(8,128)(2,1)S(1)}, u32[]{:S(2)}, u32[]{:S(2)}) collective-permute-start(bf16[128,2048]{1,0:T(8,128)(2,1)S(1)} %collective-permute-done.33.refs_4_), channel_id=1, source_target_pairs={{0,1},{1,0},{2,3},{3,2},{4,5},{5,4},{6,7},{7,6},{8,9},{9,8},{10,11... | collective-permute-start | bytes 1572872 | tf_op jit(solution)/shard_map/ppermute | solution.py:517
  120.8 5.5 %collective-permute-start.31 = (bf16[50,1024]{1,0:T(8,128)(2,1)S(1)}, bf16[50,1024]{1,0:T(8,128)(2,1)S(1)}, u32[]{:S(2)}, u32[]{:S(2)}) collective-permute-start(bf16[50,1024]{1,0:T(8,128)(2,1)S(1)} %multiply_convert_fusion.refs_0_), channel_id=1, source_target_pairs={{0,2},{2,0},{4,6},{6,4},{1,3},{3,1},{5,7},{7,5},{8,10},{10,8},{12,... | collective-permute-start | bytes 307208 | tf_op jit(solution)/shard_map/ppermute | solution.py:523
  126.3 4.8 %collective-permute-start.30 = (bf16[50,1024]{1,0:T(8,128)(2,1)S(1)}, bf16[50,1024]{1,0:T(8,128)(2,1)S(1)}, u32[]{:S(2)}, u32[]{:S(2)}) collective-permute-start(bf16[50,1024]{1,0:T(8,128)(2,1)S(1)} %multiply_convert_fusion.refs_0_), channel_id=1, source_target_pairs={{0,4},{2,6},{4,0},{6,2},{1,5},{3,7},{5,1},{7,3},{8,12},{10,14},{12... | collective-permute-start | bytes 307208 | tf_op jit(solution)/shard_map/ppermute | solution.py:523
  132.6 12.7 %collective-permute-start.48 = (bf16[128,2048]{1,0:T(8,128)(2,1)S(1)}, bf16[128,2048]{1,0:T(8,128)(2,1)S(1)}, u32[]{:S(2)}, u32[]{:S(2)}) collective-permute-start(bf16[128,2048]{1,0:T(8,128)(2,1)S(1)} %collective-permute-done.34.refs_5_), channel_id=1, source_target_pairs={{0,1},{1,0},{2,3},{3,2},{4,5},{5,4},{6,7},{7,6},{8,9},{9,8},{10,11... | collective-permute-start | bytes 1572872 | tf_op jit(solution)/shard_map/ppermute | solution.py:517
  133.0 12.3 %collective-permute-start.49 = (bf16[128,2048]{1,0:T(8,128)(2,1)S(1)}, bf16[128,2048]{1,0:T(8,128)(2,1)S(1)}, u32[]{:S(2)}, u32[]{:S(2)}) collective-permute-start(bf16[128,2048]{1,0:T(8,128)(2,1)S(1)} %collective-permute-done.35.refs_6_), channel_id=1, source_target_pairs={{0,1},{1,0},{2,3},{3,2},{4,5},{5,4},{6,7},{7,6},{8,9},{9,8},{10,11... | collective-permute-start | bytes 1572872 | tf_op jit(solution)/shard_map/ppermute | solution.py:517
  133.4 11.9 %collective-permute-start.50 = (bf16[128,2048]{1,0:T(8,128)(2,1)S(1)}, bf16[128,2048]{1,0:T(8,128)(2,1)S(1)}, u32[]{:S(2)}, u32[]{:S(2)}) collective-permute-start(bf16[128,2048]{1,0:T(8,128)(2,1)S(1)} %collective-permute-done.36.refs_7_), channel_id=1, source_target_pairs={{0,1},{1,0},{2,3},{3,2},{4,5},{5,4},{6,7},{7,6},{8,9},{9,8},{10,11... | collective-permute-start | bytes 1572872 | tf_op jit(solution)/shard_map/ppermute | solution.py:517
  149.6 5.2 %collective-permute-start.53 = (bf16[50,1024]{1,0:T(8,128)(2,1)S(1)}, bf16[50,1024]{1,0:T(8,128)(2,1)S(1)}, u32[]{:S(2)}, u32[]{:S(2)}) collective-permute-start(bf16[50,1024]{1,0:T(8,128)(2,1)S(1)} %get-tuple-element.104), channel_id=1, source_target_pairs={{0,4},{2,6},{4,0},{6,2},{1,5},{3,7},{5,1},{7,3},{8,12},{10,14},{12... | collective-permute-start | bytes 307208 | tf_op jit(solution)/shard_map/ppermute | solution.py:523
  149.7 6.0 %collective-permute-start.54 = (bf16[50,1024]{1,0:T(8,128)(2,1)S(1)}, bf16[50,1024]{1,0:T(8,128)(2,1)S(1)}, u32[]{:S(2)}, u32[]{:S(2)}) collective-permute-start(bf16[50,1024]{1,0:T(8,128)(2,1)S(1)} %get-tuple-element.105), channel_id=1, source_target_pairs={{0,2},{2,0},{4,6},{6,4},{1,3},{3,1},{5,7},{7,5},{8,10},{10,8},{12,... | collective-permute-start | bytes 307208 | tf_op jit(solution)/shard_map/ppermute | solution.py:523
  151.2 7.2 %collective-permute-start.55 = (bf16[50,1024]{1,0:T(8,128)(2,1)S(1)}, bf16[50,1024]{1,0:T(8,128)(2,1)S(1)}, u32[]{:S(2)}, u32[]{:S(2)}) collective-permute-start(bf16[50,1024]{1,0:T(8,128)(2,1)S(1)} %get-tuple-element.106), channel_id=1, source_target_pairs={{0,6},{2,4},{4,2},{6,0},{1,7},{3,5},{5,3},{7,1},{8,14},{10,12},{12... | collective-permute-start | bytes 307208 | tf_op jit(solution)/shard_map/ppermute | solution.py:523
  (19 other events, 567.1 us)
